TPU v7x, 32 devices: a whole 2x2x4 slice. The times are simulated.
32 devices in a mesh: expert: 16 (over z, y, x), tensor: 2 (over core).
Axes of the slice: x: 2, y: 2, z: 4, core: 2. Of those that a mesh axis runs over, the one named last changes fastest.
Arguments:
- layer_in: float32 [2048, 2048], P('expert'), may hold values from -20 to 20
- norm1_gain: bfloat16 [2048], P('expert'), may hold values from 0.5 to 1.5
- q_weight: bfloat16 [2048, 3072], P('expert', 'tensor'), may hold values from -0.125 to 0.125
- kva_weight: bfloat16 [2048, 576], P('expert'), may hold values from -0.125 to 0.125
- kv_gain: bfloat16 [512], P('expert'), may hold values from 0.5 to 1.5
- kvb_weight: bfloat16 [512, 4096], P('expert', 'tensor'), may hold values from -0.25 to 0.25
- o_weight: bfloat16 [2048, 2048], P('tensor', 'expert'), may hold values from -0.5 to 0.5
- norm2_gain: bfloat16 [2048], P('expert'), may hold values from 0.5 to 1.5
- router_weight: bfloat16 [2048, 16], P('expert'), may hold values from -0.25 to 0.25
- shared_gate: bfloat16 [2048, 2816], P('expert', 'tensor'), may hold values from -0.125 to 0.125
- shared_up: bfloat16 [2048, 2816], P('expert', 'tensor'), may hold values from -0.125 to 0.125
- shared_down: bfloat16 [2816, 2048], P('tensor', 'expert'), may hold values from -0.109375 to 0.109375
- expert_gate: bfloat16 [16, 2048, 1408], P('expert', None, 'tensor'), may hold values from -0.125 to 0.125
- expert_up: bfloat16 [16, 2048, 1408], P('expert', None, 'tensor'), may hold values from -0.125 to 0.125
- expert_down: bfloat16 [16, 1408, 2048], P('expert', 'tensor'), may hold values from -0.625 to 0.625
- routes: int32 [2048, 6], P('expert'), may hold values from 0 to 15, all different within a row; in each aligned block of 128 rows (0 to 127, 128 to 255, ...) at most 64 rows name the same one
- out_grad: float32 [2048, 2048], P('expert'), may hold values from -6 to 6
Outputs:
- layer_out: float32 [2048, 2048], P('expert')
- x_grad: float32 [2048, 2048], P('expert')
- norm1_gain_grad: float32 [2048], P('expert')
- q_grad: float32 [2048, 3072], P('expert', 'tensor')
- kva_grad: float32 [2048, 576], P('expert')
- kv_gain_grad: float32 [512], P('expert')
- kvb_grad: float32 [512, 4096], P('expert', 'tensor')
- o_grad: float32 [2048, 2048], P('tensor', 'expert')
- norm2_gain_grad: float32 [2048], P('expert')
- router_grad: float32 [2048, 16], P('expert')
- shared_gate_grad: float32 [2048, 2816], P('expert', 'tensor')
- shared_up_grad: float32 [2048, 2816], P('expert', 'tensor')
- shared_down_grad: float32 [2816, 2048], P('tensor', 'expert')
- expert_gate_grad: float32 [16, 2048, 1408], P('expert', None, 'tensor')
- expert_up_grad: float32 [16, 2048, 1408], P('expert', None, 'tensor')
- expert_down_grad: float32 [16, 1408, 2048], P('expert', 'tensor')
Inputs may be any that keep to these rules, and one draw needn't show every extreme that they name: `routes`: each row names 6 different experts; in the rows of one device no expert is named by more than 64 rows, a bound that some block reaches.
All inputs are finite; a program needn't handle non-finite values.
Results may differ from a plain program's by a relative error of at most 0.02.
Values may be sent and summed in bfloat16 or wider, within the bound.
A program may use at most 256 MiB of HBM per device.

v0:
```python
import jax
import jax.numpy as jnp
from jax import lax
from jax.sharding import PartitionSpec as P

D = 2048
DN = 128
DR = 64
DQK = 192
DL = 512
DV = 128
TOPK = 6


norm_eps = 1e-06


def rms_scale(inputs):
    return lax.rsqrt(jnp.mean(inputs * inputs, axis=-1, keepdims=True) + norm_eps)


def rope_tables(length, rot_width):
    half_width = rot_width // 2
    frequency = 10000.0 ** (-jnp.arange(half_width).astype(jnp.float32) / half_width)
    angles = jnp.arange(length).astype(jnp.float32)[:, None] * frequency[None, :]
    return (jnp.cos(angles), jnp.sin(angles))


def rotate(inputs, cosine, sine_part):
    half_width = inputs.shape[-1] // 2
    first_half = inputs[..., :half_width]
    second_half = inputs[..., half_width:]
    return jnp.concatenate(
        [
            first_half * cosine - second_half * sine_part,
            second_half * cosine + first_half * sine_part,
        ],
        axis=-1,
    )


def rotate_back(inputs, cosine, sine_part):
    half_width = inputs.shape[-1] // 2
    first_half = inputs[..., :half_width]
    second_half = inputs[..., half_width:]
    return jnp.concatenate(
        [
            first_half * cosine + second_half * sine_part,
            second_half * cosine - first_half * sine_part,
        ],
        axis=-1,
    )


def silu_grad(pre_act):
    sigmoid_val = jax.nn.sigmoid(pre_act)
    return sigmoid_val * (1.0 + pre_act * (1.0 - sigmoid_val))


def masked_scores(query_blk, key_rows, first_row):
    scores = jnp.einsum(
        "qhd,khd->hqk", query_blk, key_rows, preferred_element_type=jnp.float32
    ) * DQK ** (-0.5)
    row_pos = first_row + jnp.arange(query_blk.shape[0], dtype=jnp.int32)
    col_pos = jnp.arange(key_rows.shape[0], dtype=jnp.int32)
    return jnp.where(col_pos[None, None, :] <= row_pos[None, :, None], scores, -1e30)


def attend(query_rows, key_rows, value_rows):
    seq_len = query_rows.shape[0]
    blk_rows = min(seq_len, 512)

    def one_block(block_index):
        first_row = block_index * blk_rows
        scores = masked_scores(query_rows, key_rows, first_row)
        row_max = jnp.max(scores, axis=-1, keepdims=True)
        log_total = row_max + jnp.log(jnp.sum(jnp.exp(scores - row_max), axis=-1, keepdims=True))
        att_weights = jnp.exp(scores - log_total).astype(jnp.bfloat16)
        mixed_blk = jnp.einsum(
            "hqk,khd->qhd", att_weights, value_rows, preferred_element_type=jnp.float32
        ).astype(jnp.bfloat16)
        return (mixed_blk, log_total)

    mixed_heads, log_totals = lax.map(one_block, jnp.arange(seq_len // blk_rows, dtype=jnp.int32))
    return (mixed_heads.reshape(seq_len, query_rows.shape[1], value_rows.shape[2]), log_totals)


def attend_back(query_rows, key_rows, value_rows, log_totals, mixed_grad):
    seq_len, head_count = (query_rows.shape[0], query_rows.shape[1])
    blk_rows = min(seq_len, 512)

    def one_block(running, block_index):
        key_acc, value_acc = running
        first_row = block_index * blk_rows
        scores = masked_scores(query_rows, key_rows, first_row)
        att_probs = jnp.exp(scores - log_totals[block_index])
        att_weights = att_probs.astype(jnp.bfloat16)
        value_acc = value_acc + jnp.einsum(
            "hqk,qhd->khd", att_weights, mixed_grad, preferred_element_type=jnp.float32
        )
        prob_grad = jnp.einsum(
            "qhd,khd->hqk", mixed_grad, value_rows, preferred_element_type=jnp.float32
        )
        row_delta = jnp.sum(att_probs * prob_grad, axis=-1, keepdims=True)
        score_delta = (att_probs * (prob_grad - row_delta) * DQK ** (-0.5)).astype(jnp.bfloat16)
        query_grad = jnp.einsum(
            "hqk,khd->qhd", score_delta, key_rows, preferred_element_type=jnp.float32
        )
        key_acc = key_acc + jnp.einsum(
            "hqk,qhd->khd", score_delta, query_rows, preferred_element_type=jnp.float32
        )
        return ((key_acc, value_acc), query_grad)

    zero_start = (
        jnp.zeros((seq_len, head_count, DQK), jnp.float32),
        jnp.zeros((seq_len, head_count, DV), jnp.float32),
    )
    (key_grad, value_grad), query_grad = lax.scan(
        one_block, zero_start, jnp.arange(seq_len // blk_rows, dtype=jnp.int32)
    )
    return (query_grad.reshape(seq_len, head_count, DQK), key_grad, value_grad)


def attention_forward(seq_in, gain_one, query_w, latent_w, gain_kv, kvup_w):
    seq_len = seq_in.shape[0]
    head_count = query_w.shape[1] // DQK
    cosine, sine_part = rope_tables(seq_len, DR)
    stat_one = rms_scale(seq_in)
    unit_one = seq_in * stat_one
    normed1 = (unit_one * gain_one.astype(jnp.float32)).astype(jnp.bfloat16)
    query_full = jnp.dot(normed1, query_w, preferred_element_type=jnp.float32).reshape(
        seq_len, head_count, DQK
    )
    query_rows = jnp.concatenate(
        [
            query_full[..., :DN],
            rotate(query_full[..., DN:], cosine[:, None, :], sine_part[:, None, :]),
        ],
        axis=-1,
    ).astype(jnp.bfloat16)
    latent_full = jnp.dot(normed1, latent_w, preferred_element_type=jnp.float32)
    latent_stat = rms_scale(latent_full[:, :DL])
    latent_unit = latent_full[:, :DL] * latent_stat
    latent = (latent_unit * gain_kv.astype(jnp.float32)).astype(jnp.bfloat16)
    rot_key = rotate(latent_full[:, DL:], cosine, sine_part).astype(jnp.bfloat16)
    key_value = (
        jnp.dot(latent, kvup_w, preferred_element_type=jnp.float32)
        .astype(jnp.bfloat16)
        .reshape(seq_len, head_count, DN + DV)
    )
    key_rows = jnp.concatenate(
        [key_value[..., :DN], jnp.broadcast_to(rot_key[:, None, :], (seq_len, head_count, DR))],
        axis=-1,
    )
    value_rows = key_value[..., DN:]
    mixed_heads, log_totals = attend(query_rows, key_rows, value_rows)
    return (
        stat_one,
        unit_one,
        normed1,
        query_rows,
        latent_stat,
        latent_unit,
        latent,
        key_rows,
        value_rows,
        mixed_heads,
        log_totals,
        cosine,
        sine_part,
    )


def on_device(
    layer_in,
    norm1_gain,
    q_weight,
    kva_weight,
    kv_gain,
    kvb_weight,
    o_weight,
    norm2_gain,
    router_weight,
    shared_gate,
    shared_up,
    shared_down,
    expert_gate,
    expert_up,
    expert_down,
    routes,
    out_grad,
):
    groups = lax.axis_size("expert")
    seq_len = layer_in.shape[0]
    local_experts = expert_gate.shape[0]
    expert_count = local_experts * groups
    capacity = seq_len * TOPK * 4 // (3 * expert_count)
    rows_total = expert_count * capacity
    (
        gain_one,
        query_w,
        latent_w,
        gain_kv,
        kvup_w,
        output_w,
        gain_two,
        route_w,
        gate_sh,
        up_sh,
        down_sh,
    ) = (
        lax.all_gather(norm1_gain, "expert", axis=0, tiled=True),
        lax.all_gather(q_weight, "expert", axis=0, tiled=True),
        lax.all_gather(kva_weight, "expert", axis=0, tiled=True),
        lax.all_gather(kv_gain, "expert", axis=0, tiled=True),
        lax.all_gather(kvb_weight, "expert", axis=0, tiled=True),
        lax.all_gather(o_weight, "expert", axis=1, tiled=True),
        lax.all_gather(norm2_gain, "expert", axis=0, tiled=True),
        lax.all_gather(router_weight, "expert", axis=0, tiled=True),
        lax.all_gather(shared_gate, "expert", axis=0, tiled=True),
        lax.all_gather(shared_up, "expert", axis=0, tiled=True),
        lax.all_gather(shared_down, "expert", axis=1, tiled=True),
    )
    (
        stat_one,
        unit_one,
        normed1,
        query_rows,
        latent_stat,
        latent_unit,
        latent,
        key_rows,
        value_rows,
        mixed_heads,
        log_totals,
        cosine,
        sine_part,
    ) = attention_forward(layer_in, gain_one, query_w, latent_w, gain_kv, kvup_w)
    head_count = query_rows.shape[1]
    mixed_flat = mixed_heads.reshape(seq_len, head_count * DV)
    attn_part = jnp.dot(mixed_flat, output_w, preferred_element_type=jnp.float32)
    hidden_state = layer_in + lax.psum(attn_part, "tensor")
    stat_two = rms_scale(hidden_state)
    unit_two = hidden_state * stat_two
    normed2 = (unit_two * gain_two.astype(jnp.float32)).astype(jnp.bfloat16)
    router_probs = jax.nn.softmax(
        jnp.dot(normed2, route_w, preferred_element_type=jnp.float32), axis=-1
    )
    route_onehot = (
        routes[:, :, None] == jnp.arange(expert_count, dtype=jnp.int32)[None, None, :]
    ).astype(jnp.float32)
    route_weight = jnp.einsum("tke,te->tk", route_onehot, router_probs)
    flat_hot = route_onehot.reshape(seq_len * TOPK, expert_count).astype(jnp.int32)
    slot_pos = jnp.sum(jnp.cumsum(flat_hot, axis=0) * flat_hot, axis=-1) - 1
    buffer_pos = routes.reshape(-1) * capacity + slot_pos

    def to_owners(assigned):
        buffer = jnp.zeros((rows_total, D), jnp.bfloat16).at[buffer_pos].set(assigned)
        buffer = buffer.reshape(groups, local_experts * capacity, D)
        arrived = lax.all_to_all(buffer, "expert", split_axis=0, concat_axis=0, tiled=True)
        return (
            arrived.reshape(groups, local_experts, capacity, D)
            .transpose(1, 0, 2, 3)
            .reshape(local_experts, groups * capacity, D)
        )

    def to_sources(results):
        arranged = (
            results.reshape(local_experts, groups, capacity, D)
            .transpose(1, 0, 2, 3)
            .reshape(groups, local_experts * capacity, D)
        )
        arrived = lax.all_to_all(arranged, "expert", split_axis=0, concat_axis=0, tiled=True)
        return arrived.reshape(rows_total, D)[buffer_pos].reshape(seq_len, TOPK, D)

    rows_in = to_owners(jnp.repeat(normed2, TOPK, axis=0))
    pre_gate = jnp.einsum("emd,edf->emf", rows_in, expert_gate, preferred_element_type=jnp.float32)
    pre_up = jnp.einsum("emd,edf->emf", rows_in, expert_up, preferred_element_type=jnp.float32)
    expert_act = (jax.nn.silu(pre_gate) * pre_up).astype(jnp.bfloat16)
    block_out = jnp.einsum(
        "emf,efd->emd", expert_act, expert_down, preferred_element_type=jnp.float32
    ).astype(jnp.bfloat16)
    expert_out = to_sources(block_out)
    routed_part = jnp.einsum(
        "tk,tkd->td", route_weight, expert_out, preferred_element_type=jnp.float32
    )
    shared_pre_gate = jnp.dot(normed2, gate_sh, preferred_element_type=jnp.float32)
    shared_pre_up = jnp.dot(normed2, up_sh, preferred_element_type=jnp.float32)
    shared_act = (jax.nn.silu(shared_pre_gate) * shared_pre_up).astype(jnp.bfloat16)
    shared_part = jnp.dot(shared_act, down_sh, preferred_element_type=jnp.float32)
    layer_out = hidden_state + lax.psum(
        (routed_part + shared_part).astype(jnp.bfloat16), "tensor"
    ).astype(jnp.float32)
    out_rows = out_grad.astype(jnp.bfloat16)
    routed_cot = (
        (route_weight[:, :, None] * out_grad[:, None, :])
        .astype(jnp.bfloat16)
        .reshape(seq_len * TOPK, D)
    )
    cot_in = to_owners(routed_cot)
    route_grad_part = jnp.einsum(
        "tkd,td->tk", expert_out, out_grad, preferred_element_type=jnp.float32
    )
    hidden_grad_ex = jnp.einsum(
        "emd,efd->emf", cot_in, expert_down, preferred_element_type=jnp.float32
    )
    gate_delta = (hidden_grad_ex * pre_up * silu_grad(pre_gate)).astype(jnp.bfloat16)
    up_delta = (hidden_grad_ex * jax.nn.silu(pre_gate)).astype(jnp.bfloat16)
    expert_down_grad = jnp.einsum(
        "emf,emd->efd", expert_act, cot_in, preferred_element_type=jnp.float32
    )
    expert_gate_grad = jnp.einsum(
        "emd,emf->edf", rows_in, gate_delta, preferred_element_type=jnp.float32
    )
    expert_up_grad = jnp.einsum(
        "emd,emf->edf", rows_in, up_delta, preferred_element_type=jnp.float32
    )
    row_block = (
        jnp.einsum("emf,edf->emd", gate_delta, expert_gate, preferred_element_type=jnp.float32)
        + jnp.einsum("emf,edf->emd", up_delta, expert_up, preferred_element_type=jnp.float32)
    ).astype(jnp.bfloat16)
    row_grad = to_sources(row_block)
    shared_down_grad = jnp.dot(shared_act.T, out_rows, preferred_element_type=jnp.float32)
    shared_hidden_grad = jnp.dot(out_rows, down_sh.T, preferred_element_type=jnp.float32)
    shared_gate_delta = (shared_hidden_grad * shared_pre_up * silu_grad(shared_pre_gate)).astype(
        jnp.bfloat16
    )
    shared_up_delta = (shared_hidden_grad * jax.nn.silu(shared_pre_gate)).astype(jnp.bfloat16)
    shared_gate_grad = jnp.dot(normed2.T, shared_gate_delta, preferred_element_type=jnp.float32)
    shared_up_grad = jnp.dot(normed2.T, shared_up_delta, preferred_element_type=jnp.float32)
    normed2_part = (
        jnp.sum(row_grad, axis=1, dtype=jnp.float32)
        + jnp.dot(shared_gate_delta, gate_sh.T, preferred_element_type=jnp.float32)
        + jnp.dot(shared_up_delta, up_sh.T, preferred_element_type=jnp.float32)
    )
    normed2_grad, route_grad = lax.psum((normed2_part, route_grad_part), "tensor")
    prob_grad = jnp.einsum("tk,tke->te", route_grad, route_onehot)
    logit_delta = (
        router_probs * (prob_grad - jnp.sum(router_probs * prob_grad, axis=-1, keepdims=True))
    ).astype(jnp.bfloat16)
    router_grad = jnp.dot(normed2.T, logit_delta, preferred_element_type=jnp.float32)
    normed2_grad = normed2_grad + jnp.dot(
        logit_delta, route_w.T, preferred_element_type=jnp.float32
    )
    norm2_gain_grad = jnp.sum(normed2_grad * unit_two, axis=0)
    scaled_two = normed2_grad * gain_two.astype(jnp.float32)
    hidden_grad = out_grad + stat_two * (
        scaled_two - unit_two * jnp.mean(scaled_two * unit_two, axis=-1, keepdims=True)
    )
    hidden_rows = hidden_grad.astype(jnp.bfloat16)
    o_grad = jnp.dot(mixed_flat.T, hidden_rows, preferred_element_type=jnp.float32)
    mixed_grad = (
        jnp.dot(hidden_rows, output_w.T, preferred_element_type=jnp.float32)
        .astype(jnp.bfloat16)
        .reshape(seq_len, head_count, DV)
    )
    query_grad, key_grad, value_grad = attend_back(
        query_rows, key_rows, value_rows, log_totals, mixed_grad
    )
    query_delta = (
        jnp.concatenate(
            [
                query_grad[..., :DN],
                rotate_back(query_grad[..., DN:], cosine[:, None, :], sine_part[:, None, :]),
            ],
            axis=-1,
        )
        .astype(jnp.bfloat16)
        .reshape(seq_len, head_count * DQK)
    )
    kv_delta = (
        jnp.concatenate([key_grad[..., :DN], value_grad], axis=-1)
        .astype(jnp.bfloat16)
        .reshape(seq_len, head_count * (DN + DV))
    )
    q_grad = jnp.dot(normed1.T, query_delta, preferred_element_type=jnp.float32)
    kvb_grad = jnp.dot(latent.T, kv_delta, preferred_element_type=jnp.float32)
    latent_part = jnp.dot(kv_delta, kvup_w.T, preferred_element_type=jnp.float32)
    rot_part = jnp.sum(key_grad[..., DN:], axis=1)
    normed1_part = jnp.dot(query_delta, query_w.T, preferred_element_type=jnp.float32)
    latent_grad, rot_sum, normed1_query = (
        lax.psum(latent_part.astype(jnp.bfloat16), "tensor").astype(jnp.float32),
        lax.psum(rot_part.astype(jnp.bfloat16), "tensor").astype(jnp.float32),
        lax.psum(normed1_part.astype(jnp.bfloat16), "tensor").astype(jnp.float32),
    )
    kv_gain_grad = jnp.sum(latent_grad * latent_unit, axis=0)
    scaled_lat = latent_grad * gain_kv.astype(jnp.float32)
    latent_back = latent_stat * (
        scaled_lat - latent_unit * jnp.mean(scaled_lat * latent_unit, axis=-1, keepdims=True)
    )
    latent_delta = jnp.concatenate(
        [latent_back, rotate_back(rot_sum, cosine, sine_part)], axis=-1
    ).astype(jnp.bfloat16)
    kva_grad = jnp.dot(normed1.T, latent_delta, preferred_element_type=jnp.float32)
    normed1_grad = normed1_query + jnp.dot(
        latent_delta, latent_w.T, preferred_element_type=jnp.float32
    )
    norm1_gain_grad = jnp.sum(normed1_grad * unit_one, axis=0)
    scaled_one = normed1_grad * gain_one.astype(jnp.float32)
    x_grad = hidden_grad + stat_one * (
        scaled_one - unit_one * jnp.mean(scaled_one * unit_one, axis=-1, keepdims=True)
    )
    (
        norm1_gain_grad,
        q_grad,
        kva_grad,
        kv_gain_grad,
        kvb_grad,
        o_grad,
        norm2_gain_grad,
        router_grad,
        shared_gate_grad,
        shared_up_grad,
        shared_down_grad,
    ) = (
        lax.psum_scatter(norm1_gain_grad, "expert", scatter_dimension=0, tiled=True),
        lax.psum_scatter(q_grad, "expert", scatter_dimension=0, tiled=True),
        lax.psum_scatter(kva_grad, "expert", scatter_dimension=0, tiled=True),
        lax.psum_scatter(kv_gain_grad, "expert", scatter_dimension=0, tiled=True),
        lax.psum_scatter(kvb_grad, "expert", scatter_dimension=0, tiled=True),
        lax.psum_scatter(o_grad, "expert", scatter_dimension=1, tiled=True),
        lax.psum_scatter(norm2_gain_grad, "expert", scatter_dimension=0, tiled=True),
        lax.psum_scatter(router_grad, "expert", scatter_dimension=0, tiled=True),
        lax.psum_scatter(shared_gate_grad, "expert", scatter_dimension=0, tiled=True),
        lax.psum_scatter(shared_up_grad, "expert", scatter_dimension=0, tiled=True),
        lax.psum_scatter(shared_down_grad, "expert", scatter_dimension=1, tiled=True),
    )
    return (
        layer_out,
        x_grad,
        norm1_gain_grad,
        q_grad,
        kva_grad,
        kv_gain_grad,
        kvb_grad,
        o_grad,
        norm2_gain_grad,
        router_grad,
        shared_gate_grad,
        shared_up_grad,
        shared_down_grad,
        expert_gate_grad,
        expert_up_grad,
        expert_down_grad,
    )


def solution(mesh):
    in_specs = (
        P("expert", None),
        P("expert"),
        P("expert", "tensor"),
        P("expert", None),
        P("expert"),
        P("expert", "tensor"),
        P("tensor", "expert"),
        P("expert"),
        P("expert", None),
        P("expert", "tensor"),
        P("expert", "tensor"),
        P("tensor", "expert"),
        P("expert", None, "tensor"),
        P("expert", None, "tensor"),
        P("expert", "tensor", None),
        P("expert", None),
        P("expert", None),
    )
    out_specs = (
        P("expert", None),
        P("expert", None),
        P("expert"),
        P("expert", "tensor"),
        P("expert", None),
        P("expert"),
        P("expert", "tensor"),
        P("tensor", "expert"),
        P("expert"),
        P("expert", None),
        P("expert", "tensor"),
        P("expert", "tensor"),
        P("tensor", "expert"),
        P("expert", None, "tensor"),
        P("expert", None, "tensor"),
        P("expert", "tensor", None),
    )
    return jax.shard_map(
        on_device, mesh=mesh, in_specs=in_specs, out_specs=out_specs, check_vma=False
    )
```

profile of v0, /device:TPU:0, one launch (start us, length us, event | category | flops | bytes accessed | tf_op | source)
XLA Modules:
  0.0 2516.1 jit_solution(2479623936007843046)
XLA Ops:
  10.1 42.8 %all-gather = bf16[16,1,128]{2,1,0:T(2,128)(2,1)S(1)} all-gather(bf16[1,1,128]{2,1,0:T(2,128)(2,1)} %bitcast.188), channel_id=1, replica_groups=mesh['expert'=16,'tensor'=2] {'expert'}, dimensions={0}, use_global_device_ids=true | all-gather | bytes 4352 | tf_op jit(solution)/shard_map/all_gather | solution.py:212
  55.8 37.7 %all-reduce = bf16[512]{0:T(512)(128)(2,1)S(1)} all-reduce(bf16[512]{0:T(512)(128)(2,1)S(1)} %dynamic-update-slice), channel_id=1, replica_groups=mesh['expert'=16,'tensor'=2] {'expert'}, use_global_device_ids=true, to_apply=%add | all-reduce | flops 512 | bytes 2048
  99.8 41.9 %all-gather.12.cloned.1.call-done = bf16[512,2048]{1,0:T(8,128)(2,1)} async-done(((bf16[32,2048]{1,0:T(8,128)(2,1)}), bf16[512,2048]{1,0:T(8,128)(2,1)}) %all-gather.12.cloned.1.call-update) | async-done | bytes 2097168 | tf_op jit(solution)/shard_map/all_gather | solution.py:216
  149.3 87.3 %all-gather.14.cloned.1.call-done = bf16[2048,1536]{1,0:T(8,128)(2,1)} async-done(((bf16[128,1536]{1,0:T(8,128)(2,1)}), bf16[2048,1536]{1,0:T(8,128)(2,1)}) %all-gather.14.cloned.1.call-update) | async-done | bytes 6291472 | tf_op jit(solution)/shard_map/all_gather | solution.py:213
  244.3 82.2 %all-gather.16.cloned.1.call-done = bf16[1024,2048]{1,0:T(8,128)(2,1)} async-done(((bf16[1024,128]{1,0:T(8,128)(2,1)}), bf16[1024,2048]{1,0:T(8,128)(2,1)}) %all-gather.16.cloned.1.call-update) | async-done | bytes 4194320 | tf_op jit(solution)/shard_map/all_gather | solution.py:217
  330.8 38.3 %all-gather.1 = bf16[16,1,128]{2,1,0:T(2,128)(2,1)S(1)} all-gather(bf16[1,1,128]{2,1,0:T(2,128)(2,1)S(1)} %bitcast.189), channel_id=1, replica_groups=mesh['expert'=16,'tensor'=2] {'expert'}, dimensions={0}, use_global_device_ids=true | all-gather | bytes 4352 | tf_op jit(solution)/shard_map/all_gather | solution.py:218
  383.5 10.5 scatter_custom_fusion
  413.2 106.0 %all_gather.40 = bf16[2048,16]{0,1:T(8,128)(2,1)S(1)} all-gather(bf16[128,16]{0,1:T(8,128)(2,1)S(1)} %copy-done.66), channel_id=1, replica_groups=mesh['expert'=16,'tensor'=2] {'expert'}, dimensions={0}, use_global_device_ids=true | all-gather | bytes 69632 | tf_op jit(solution)/shard_map/all_gather | solution.py:219
  525.9 11.3 scatter_custom_fusion.1
  537.2 46.9 %all-to-all-start.2 = ((bf16[16,64,2048]{2,1,0:T(8,128)(2,1)}), bf16[16,64,2048]{2,1,0:T(8,128)(2,1)}, u32[]{:S(2)}, u32[]{:S(2)}) async-start(bf16[16,64,2048]{2,1,0:T(8,128)(2,1)} %bitcast.161), calls=%async_computation.2 | async-start | bytes 8388608 | tf_op jit(solution)/shard_map/all_to_all | solution.py:260
  599.8 78.4 %all-to-all-done.2 = bf16[16,64,2048]{2,1,0:T(8,128)(2,1)} async-done(((bf16[16,64,2048]{2,1,0:T(8,128)(2,1)}), bf16[16,64,2048]{2,1,0:T(8,128)(2,1)}, u32[]{:S(2)}, u32[]{:S(2)}) %all-to-all-start.2) | async-done | bytes 4194336 | tf_op jit(solution)/shard_map/all_to_all | solution.py:260
  696.0 42.3 %all-to-all-start.3 = ((bf16[16,64,2048]{2,1,0:T(8,128)(2,1)}), bf16[16,64,2048]{2,1,0:T(8,128)(2,1)}, u32[]{:S(2)}, u32[]{:S(2)}) async-start(bf16[16,64,2048]{2,1,0:T(8,128)(2,1)} %bitcast.166), calls=%async_computation.3 | async-start | bytes 8388608 | tf_op jit(solution)/shard_map/all_to_all | solution.py:273
  745.5 76.6 %all-to-all-done.3 = bf16[16,64,2048]{2,1,0:T(8,128)(2,1)} async-done(((bf16[16,64,2048]{2,1,0:T(8,128)(2,1)}), bf16[16,64,2048]{2,1,0:T(8,128)(2,1)}, u32[]{:S(2)}, u32[]{:S(2)}) %all-to-all-start.3) | async-done | bytes 4194336 | tf_op jit(solution)/shard_map/all_to_all | solution.py:273
  822.1 52.5 %all-to-all-start.1 = ((bf16[16,64,2048]{2,1,0:T(8,128)(2,1)}), bf16[16,64,2048]{2,1,0:T(8,128)(2,1)}, u32[]{:S(2)}, u32[]{:S(2)}) async-start(bf16[16,64,2048]{2,1,0:T(8,128)(2,1)} %bitcast.165), calls=%async_computation.1 | async-start | bytes 8388608 | tf_op jit(solution)/shard_map/all_to_all | solution.py:273
  883.2 56.7 %all-gather.22.cloned.1.call-done = bf16[1408,2048]{1,0:T(8,128)(2,1)} async-done(((bf16[1408,128]{1,0:T(8,128)(2,1)}), bf16[1408,2048]{1,0:T(8,128)(2,1)}) %all-gather.22.cloned.1.call-update) | async-done | bytes 5767184 | tf_op jit(solution)/shard_map/all_gather | solution.py:222
  945.4 10.1 gather_fusion.1
  1108.2 77.6 %all-reduce.4 = (f32[2048]{0:T(1024)S(1)}, f32[512]{0:T(512)S(1)}, f32[2048]{0:T(1024)S(1)}) all-reduce(f32[2048]{0:T(1024)} %get-tuple-element.63, f32[512]{0:T(512)} %get-tuple-element.65, f32[2048]{0:T(1024)} %get-tuple-element.61), channel_id=2, replica_groups=mesh['expert'=16,'tensor'=2] {'expert'}, use_global_device_ids=true, to_apply=%region_27.28.clone | all-reduce | flops 4608 | bytes 36864
  1192.0 185.2 %reduce-scatter.19.cloned.1.call-done = f32[128,1408]{1,0:T(8,128)} async-done(((f32[2048,1408]{1,0:T(8,128)}), f32[128,1408]{1,0:T(8,128)}) %reduce-scatter.19.cloned.1.call-update) | async-done | bytes 720912 | tf_op jit(solution)/shard_map/reduce_scatter | solution.py:424
  1377.2 248.3 %reduce-scatter.21.cloned.1.call-done = f32[128,1408]{1,0:T(8,128)} async-done(((f32[2048,1408]{1,0:T(8,128)}), f32[128,1408]{1,0:T(8,128)}) %reduce-scatter.21.cloned.1.call-update) | async-done | bytes 720912 | tf_op jit(solution)/shard_map/reduce_scatter | solution.py:425
  1625.5 247.4 %reduce-scatter.23.cloned.1.call-done = f32[1408,128]{1,0:T(8,128)} async-done(((f32[1408,2048]{1,0:T(8,128)}), f32[1408,128]{1,0:T(8,128)}) %reduce-scatter.23.cloned.1.call-update) | async-done | bytes 720912 | tf_op jit(solution)/shard_map/reduce_scatter | solution.py:426
  1872.9 101.7 %reduce-scatter.13.cloned.1.call-done = f32[32,2048]{1,0:T(8,128)} async-done(((f32[512,2048]{1,0:T(8,128)}), f32[32,2048]{1,0:T(8,128)}) %reduce-scatter.13.cloned.1.call-update) | async-done | bytes 262160 | tf_op jit(solution)/shard_map/reduce_scatter | solution.py:420
  1974.5 143.8 %reduce-scatter.11.cloned.1.call-done = f32[128,576]{0,1:T(8,128)} async-done(((f32[2048,576]{0,1:T(8,128)}), f32[128,576]{0,1:T(8,128)}) %reduce-scatter.11.cloned.1.call-update) | async-done | bytes 294928 | tf_op jit(solution)/shard_map/reduce_scatter | solution.py:418
  2118.3 179.5 %reduce-scatter.15.cloned.1.call-done = f32[1024,128]{1,0:T(8,128)} async-done(((f32[1024,2048]{1,0:T(8,128)}), f32[1024,128]{1,0:T(8,128)}) %reduce-scatter.15.cloned.1.call-update) | async-done | bytes 524304 | tf_op jit(solution)/shard_map/reduce_scatter | solution.py:421
  2297.8 211.3 %reduce-scatter.9.cloned.1.call-done = f32[128,1536]{1,0:T(8,128)} async-done(((f32[2048,1536]{1,0:T(8,128)}), f32[128,1536]{1,0:T(8,128)}) %reduce-scatter.9.cloned.1.call-update) | async-done | bytes 786448 | tf_op jit(solution)/shard_map/reduce_scatter | solution.py:417
  (325 shorter events, 282.4 us)
Async XLA Ops:
  7.2 671.0 %copy-start = (bf16[1,704,2048]{2,1,0:T(8,128)(2,1)S(1)}, bf16[1,704,2048]{2,1,0:T(8,128)(2,1)}, u32[]{:S(2)}) copy-start(bf16[1,704,2048]{2,1,0:T(8,128)(2,1)} %param.31) | copy-start | bytes 8650756
  7.2 89.1 %all-gather.10.cloned.1.call-start = ((), (), s32[]{:S(2)}) async-start(), calls=%async_computation.12 | async-start | bytes 2506752 | tf_op jit(solution)/shard_map/all_gather | solution.py:214
  7.9 133.7 %all-gather.12.cloned.1.call-start = ((), (), s32[]{:S(2)}) async-start(), calls=%async_computation.13 | async-start | bytes 2228224 | tf_op jit(solution)/shard_map/all_gather | solution.py:216
  8.7 228.0 %all-gather.14.cloned.1.call-start = ((), (), s32[]{:S(2)}) async-start(), calls=%async_computation.14 | async-start | bytes 6684672 | tf_op jit(solution)/shard_map/all_gather | solution.py:213
  9.4 317.1 %all-gather.16.cloned.1.call-start = ((), (), s32[]{:S(2)}) async-start(), calls=%async_computation.15 | async-start | bytes 4456448 | tf_op jit(solution)/shard_map/all_gather | solution.py:217
  10.0 361.6 %all-reduce.10.cloned.1.call-start = ((), (), s32[]{:S(2)}) async-start(), calls=%async_computation.16 | async-start | bytes 2097152 | tf_op jit(solution)/shard_map/psum | solution.py:242
  394.0 143.2 %all-to-all-start = ((bf16[16,64,2048]{2,1,0:T(8,128)(2,1)}), bf16[16,64,2048]{2,1,0:T(8,128)(2,1)}, u32[]{:S(2)}, u32[]{:S(2)}) async-start(bf16[16,64,2048]{2,1,0:T(8,128)(2,1)} %bitcast.160), calls=%async_computation | async-start | bytes 8388608 | tf_op jit(solution)/shard_map/all_to_all | solution.py:260
  398.5 476.4 %all-gather.18.cloned.1.call-start = ((), (), s32[]{:S(2)}) async-start(), calls=%async_computation.17 | async-start | bytes 6127616 | tf_op jit(solution)/shard_map/all_gather | solution.py:220
  537.2 141.0 %all-to-all-start.2 = ((bf16[16,64,2048]{2,1,0:T(8,128)(2,1)}), bf16[16,64,2048]{2,1,0:T(8,128)(2,1)}, u32[]{:S(2)}, u32[]{:S(2)}) async-start(bf16[16,64,2048]{2,1,0:T(8,128)(2,1)} %bitcast.161), calls=%async_computation.2 | async-start | bytes 8388608 | tf_op jit(solution)/shard_map/all_to_all | solution.py:260
  584.1 294.5 %all-gather.20.cloned.1.call-start = ((), (), s32[]{:S(2)}) async-start(), calls=%async_computation.18 | async-start | bytes 6127616 | tf_op jit(solution)/shard_map/all_gather | solution.py:221
  696.0 126.1 %all-to-all-start.3 = ((bf16[16,64,2048]{2,1,0:T(8,128)(2,1)}), bf16[16,64,2048]{2,1,0:T(8,128)(2,1)}, u32[]{:S(2)}, u32[]{:S(2)}) async-start(bf16[16,64,2048]{2,1,0:T(8,128)(2,1)} %bitcast.166), calls=%async_computation.3 | async-start | bytes 8388608 | tf_op jit(solution)/shard_map/all_to_all | solution.py:273
  738.4 201.5 %all-gather.22.cloned.1.call-start = ((), (), s32[]{:S(2)}) async-start(), calls=%async_computation.19 | async-start | bytes 6127616 | tf_op jit(solution)/shard_map/all_gather | solution.py:222
  822.1 156.3 %all-to-all-start.1 = ((bf16[16,64,2048]{2,1,0:T(8,128)(2,1)}), bf16[16,64,2048]{2,1,0:T(8,128)(2,1)}, u32[]{:S(2)}, u32[]{:S(2)}) async-start(bf16[16,64,2048]{2,1,0:T(8,128)(2,1)} %bitcast.165), calls=%async_computation.1 | async-start | bytes 8388608 | tf_op jit(solution)/shard_map/all_to_all | solution.py:273
  874.6 137.9 %all-reduce.12.cloned.1.call-start = ((), (), s32[]{:S(2)}) async-start(), calls=%async_computation.20 | async-start | bytes 2097152 | tf_op jit(solution)/shard_map/psum | solution.py:336
  978.4 85.8 %all-reduce.14.cloned.1.call-start = ((), (), s32[]{:S(2)}) async-start(), calls=%async_computation.29 | async-start | bytes 2359296 | tf_op jit(solution)/shard_map/psum | solution.py:291
  1034.4 157.6 %reduce-scatter.17.cloned.1.call-start = ((), (), s32[]{:S(2)}) async-start(), calls=%async_computation.25 | async-start | bytes 139264 | tf_op jit(solution)/shard_map/reduce_scatter | solution.py:423
  1035.3 341.9 %reduce-scatter.19.cloned.1.call-start = ((), (), s32[]{:S(2)}) async-start(), calls=%async_computation.26 | async-start | bytes 12255232 | tf_op jit(solution)/shard_map/reduce_scatter | solution.py:424
  1041.3 584.2 %reduce-scatter.21.cloned.1.call-start = ((), (), s32[]{:S(2)}) async-start(), calls=%async_computation.27 | async-start | bytes 12255232 | tf_op jit(solution)/shard_map/reduce_scatter | solution.py:425
  1048.2 824.7 %reduce-scatter.23.cloned.1.call-start = ((), (), s32[]{:S(2)}) async-start(), calls=%async_computation.28 | async-start | bytes 12255232 | tf_op jit(solution)/shard_map/reduce_scatter | solution.py:426
  1055.5 919.1 %reduce-scatter.13.cloned.1.call-start = ((), (), s32[]{:S(2)}) async-start(), calls=%async_computation.23 | async-start | bytes 4456448 | tf_op jit(solution)/shard_map/reduce_scatter | solution.py:420
  1059.4 1058.9 %reduce-scatter.11.cloned.1.call-start = ((), (), s32[]{:S(2)}) async-start(), calls=%async_computation.22 | async-start | bytes 5013504 | tf_op jit(solution)/shard_map/reduce_scatter | solution.py:418
  1069.9 1227.9 %reduce-scatter.15.cloned.1.call-start = ((), (), s32[]{:S(2)}) async-start(), calls=%async_computation.24 | async-start | bytes 8912896 | tf_op jit(solution)/shard_map/reduce_scatter | solution.py:421
  1075.3 1433.8 %reduce-scatter.9.cloned.1.call-start = ((), (), s32[]{:S(2)}) async-start(), calls=%async_computation.21 | async-start | bytes 13369344 | tf_op jit(solution)/shard_map/reduce_scatter | solution.py:417
  1105.9 1403.2 %copy-start.1 = (bf16[1,704,2048]{2,1,0:T(8,128)(2,1)S(1)}, bf16[1,704,2048]{2,1,0:T(8,128)(2,1)}, u32[]{:S(2)}) copy-start(bf16[1,704,2048]{2,1,0:T(8,128)(2,1)} %param.31) | copy-start | bytes 8650756
  (78 other events, 1568.6 us)
Sparse Core Ops, SparseCore 0:
  10.7 69.6 all-gather.9
  83.2 58.4 all-gather.11
  144.4 92.1 all-gather.13
  239.2 87.2 all-gather.15
  330.6 17.5 all-reduce.9
  401.7 138.7 all-gather.17
  587.6 138.9 all-gather.19
  741.9 197.8 all-gather.21
  978.5 19.9 all-reduce.11
  1034.5 20.3 all-reduce.13
  1057.7 78.2 reduce-scatter.16
  1138.7 238.4 reduce-scatter.18
  1380.1 245.3 reduce-scatter.20
  1628.2 244.6 reduce-scatter.22
  1875.6 98.9 reduce-scatter.12
  1980.1 138.1 reduce-scatter.10
  2121.0 176.7 reduce-scatter.14
  2303.9 205.1 reduce-scatter.8
where the time goes:
time: 2520 us
  waiting for transfers between devices  1740 us (69%)
  blocking collectives  310 us (12%)
  matrix products  170 us (7%)
  starting transfers between devices  147 us (6%)
  local copies, waits for them, and re-layouts  89.2 us (4%)
  other arithmetic  36.7 us (1%)
    reduce_scatter x1, waiting for transfers between devices, on_device(): lax.psum_scatter(shared_up_grad, 'expert', scatter_dimension=0, tiled=True)  248 us
    reduce_scatter x1, waiting for transfers between devices, on_device(): lax.psum_scatter(shared_down_grad, 'expert', scatter_dimension=1, tiled=T...  247 us
    reduce_scatter x1, waiting for transfers between devices, on_device(): lax.psum_scatter(q_grad, 'expert', scatter_dimension=0, tiled=True)  211 us
    reduce_scatter x1, waiting for transfers between devices, on_device(): lax.psum_scatter(shared_gate_grad, 'expert', scatter_dimension=0, tiled=T...  185 us
    reduce_scatter x1, waiting for transfers between devices, on_device(): lax.psum_scatter(o_grad, 'expert', scatter_dimension=1, tiled=True)  179 us
    reduce_scatter x1, waiting for transfers between devices, on_device(): lax.psum_scatter(kva_grad, 'expert', scatter_dimension=0, tiled=True)  144 us
    unnamed x2, blocking collectives  115 us
    all_gather x1, blocking collectives, on_device(): lax.all_gather(router_weight, 'expert', axis=0, tiled=True)  106 us
  transfers between devices with their start and end apart: 22, of which 13 were waited for; matrix products, arithmetic and copies ran while one was open for 10% of the time, Pallas kernels for 0%

commit v1 on v0

--- a/solution.py
+++ b/solution.py
@@ -1,15 +1,18 @@
+import functools
+
 import jax
 import jax.numpy as jnp
 from jax import lax
+from jax.experimental import pallas as pl
+from jax.experimental.pallas import tpu as pltpu
 from jax.sharding import PartitionSpec as P
 
-D = 2048
 DN = 128
 DR = 64
 DQK = 192
-DL = 512
 DV = 128
 TOPK = 6
+LANES = 128
 
 
 norm_eps = 1e-06
@@ -40,16 +43,7 @@
 
 
 def rotate_back(inputs, cosine, sine_part):
-    half_width = inputs.shape[-1] // 2
-    first_half = inputs[..., :half_width]
-    second_half = inputs[..., half_width:]
-    return jnp.concatenate(
-        [
-            first_half * cosine + second_half * sine_part,
-            second_half * cosine - first_half * sine_part,
-        ],
-        axis=-1,
-    )
+    return rotate(inputs, cosine, -sine_part)
 
 
 def silu_grad(pre_act):
@@ -57,7 +51,582 @@
     return sigmoid_val * (1.0 + pre_act * (1.0 - sigmoid_val))
 
 
-def masked_scores(query_blk, key_rows, first_row):
+def fdot(left, right):
+    return jnp.dot(left, right, preferred_element_type=jnp.float32)
+
+
+def fsum(spec, left, right):
+    return jnp.einsum(spec, left, right, preferred_element_type=jnp.float32)
+
+
+EXPERT, TENSOR = "expert", "tensor"
+MESH = pl.DeviceIdType.MESH
+DMA = pltpu.SemaphoreType.DMA
+
+
+def guarded(cond, body):
+    if cond is None:
+        body()
+    else:
+        pl.when(cond)(body)
+
+
+def remote(src, dst, send, recv, target):
+    return pltpu.make_async_remote_copy(
+        src_ref=src, dst_ref=dst, send_sem=send, recv_sem=recv, device_id=target, device_id_type=MESH
+    )
+
+
+def part_rows(start, size):
+    return pl.ds(pl.multiple_of(start, size), size)
+
+
+class Place:
+    def __init__(self):
+        self.groups = lax.axis_size(EXPERT)
+        self.chip = lax.axis_index(EXPERT)
+        self.core = lax.axis_index(TENSOR)
+        self.here = lax.rem(self.chip, 4)
+        self.there_x = self.here + 1 - 2 * lax.rem(self.here, 2)
+        self.there_y = self.here + 2 - 4 * (self.here // 2)
+        self.across = 3 - self.here
+        base = self.chip - self.here
+        self.by_x = {EXPERT: base + self.there_x}
+        self.by_y = {EXPERT: base + self.there_y}
+        self.above = {EXPERT: self.chip + 4}
+        self.below = {EXPERT: self.chip - 4}
+        self.mate = {TENSOR: 1 - self.core}
+
+    def partner(self, j):
+        return lax.rem(self.chip + j, self.groups)
+
+
+def level_steps(level, planes, far_first):
+    order = [(0, 0)] + [(d, s) for d in range(1, planes) for s in (-1, 1)]
+    steps = []
+    for distance, side in order[::-1] if far_first else order:
+        lev = level + side * distance
+        steps.append((lev, side, None if distance == 0 else ((lev >= 0) & (lev < planes))))
+    return steps
+
+
+class Swap:
+    reach = 0
+
+    def __init__(self, blocks, vmem_result=False):
+        groups = blocks.shape[0]
+        self.ins = [(blocks, pltpu.VMEM)]
+        self.outs = [
+            (
+                jax.ShapeDtypeStruct(blocks.shape, blocks.dtype),
+                pltpu.VMEM if vmem_result else pl.ANY,
+            )
+        ]
+        self.scratch = [DMA, DMA((groups,)), DMA((groups,))]
+
+    def bind(self, place, ins, outs, scratch):
+        self.place, self.groups = place, place.groups
+        self.source, self.result = ins[0], outs[0]
+        self.own_sem, self.send_sem, self.recv_sem = scratch
+
+    def copy(self, j, src, dst):
+        return remote(
+            self.source.at[src],
+            self.result.at[dst],
+            self.send_sem.at[j],
+            self.recv_sem.at[j],
+            {EXPERT: self.place.partner(j)},
+        )
+
+    def own(self):
+        chip = self.place.chip
+        return pltpu.make_async_copy(self.source.at[chip], self.result.at[chip], self.own_sem)
+
+    def begin(self):
+        self.own().start()
+        for j in range(1, self.groups):
+            self.copy(j, self.place.partner(j), self.place.chip).start()
+
+    def middle(self):
+        return []
+
+    def end(self):
+        self.own().wait()
+        for j in range(1, self.groups):
+            self.copy(j, self.place.chip, self.place.partner(self.groups - j)).wait_recv()
+            self.copy(j, self.place.partner(j), self.place.chip).wait_send()
+
+
+class Gather:
+    def __init__(self, arrays, planes):
+        count, slots = len(arrays), planes * 4
+        self.planes, self.count, self.reach = planes, count, planes
+        self.ins = [(a, pltpu.VMEM) for a in arrays]
+        self.outs = [(jax.ShapeDtypeStruct((slots,) + a.shape, a.dtype), pl.ANY) for a in arrays]
+        by_level, by_slot = DMA((count, planes)), DMA((count, slots))
+        self.scratch = [DMA((count,))] + [by_level] * 5 + [by_slot] + [by_level] * 6 + [by_slot]
+
+    def bind(self, place, ins, outs, scratch):
+        self.place, self.sources, self.results = place, ins, outs
+        self.level = lax.rem(place.chip // 4, self.planes)
+        self.has_up, self.has_down = self.level < self.planes - 1, self.level > 0
+        self.own_sem = scratch[0]
+        self.in_z, self.in_x, self.in_y, self.in_a, self.in_b, self.in_p = scratch[1:7]
+        self.out_up, self.out_down, self.out_x, self.out_y = scratch[7:11]
+        self.out_a, self.out_b, self.out_p = scratch[11:14]
+        self.steps = level_steps(self.level, self.planes, False)
+
+    def move(self, a, slot, part, send, recv, target, own=False, whose=None):
+        half = self.sources[a].shape[0] // 2
+        whose = self.place.core if whose is None else whose
+        if part is None:
+            rows = part_rows(whose * half, half)
+        else:
+            rows = part_rows(whose * half + part * (half // 2), half // 2)
+        dst = self.results[a].at[slot, rows]
+        return remote(self.sources[a].at[rows] if own else dst, dst, send, recv, target)
+
+    def along_z(self, a, lev, own, up):
+        sems = self.out_up if up else self.out_down
+        target = self.place.above if up else self.place.below
+        slot = lev * 4 + self.place.here
+        return self.move(a, slot, None, sems.at[a, lev], self.in_z.at[a, lev], target, own)
+
+    def along_x(self, a, lev, slot, own=False):
+        return self.move(
+            a, slot, None, self.out_x.at[a, lev], self.in_x.at[a, lev], self.place.by_x, own
+        )
+
+    def along_y(self, a, lev, slot, own=False):
+        return self.move(
+            a, slot, None, self.out_y.at[a, lev], self.in_y.at[a, lev], self.place.by_y, own
+        )
+
+    def corner_x(self, a, lev, slot):
+        return self.move(
+            a, slot, 0, self.out_a.at[a, lev], self.in_a.at[a, lev], self.place.by_x
+        )
+
+    def corner_y(self, a, lev, slot):
+        return self.move(
+            a, slot, 1, self.out_b.at[a, lev], self.in_b.at[a, lev], self.place.by_y
+        )
+
+    def share(self, a, slot, whose=None):
+        return self.move(
+            a, slot, None, self.out_p.at[a, slot], self.in_p.at[a, slot], self.place.mate, whose=whose
+        )
+
+    def own(self, a):
+        slot = self.level * 4 + self.place.here
+        return pltpu.make_async_copy(self.sources[a], self.results[a].at[slot], self.own_sem.at[a])
+
+    def begin(self):
+        for a in range(self.count):
+            self.own(a).start()
+        self.first(*self.steps[0])
+
+    def first(self, lev, side, cond):
+        def body():
+            for a in range(self.count):
+                own, slot = side == 0, lev * 4 + self.place.here
+                if side != 0:
+                    self.along_z(a, lev, own, True).wait_recv()
+                if side <= 0:
+                    pl.when(self.has_up)(lambda a=a: self.along_z(a, lev, own, True).start())
+                if side >= 0:
+                    pl.when(self.has_down)(lambda a=a: self.along_z(a, lev, own, False).start())
+                self.along_x(a, lev, slot, own).start()
+                self.along_y(a, lev, slot, own).start()
+                if side != 0:
+                    self.share(a, slot).start()
+
+        guarded(cond, body)
+
+    def second(self, lev, side, cond):
+        def body():
+            for a in range(self.count):
+                slot = lev * 4 + self.place.there_y
+                self.along_y(a, lev, slot).wait_recv()
+                self.corner_x(a, lev, slot).start()
+                self.share(a, slot).start()
+                slot = lev * 4 + self.place.there_x
+                self.along_x(a, lev, slot).wait_recv()
+                self.corner_y(a, lev, slot).start()
+                self.share(a, slot).start()
+
+        guarded(cond, body)
+
+    def third(self, lev, side, cond):
+        def body():
+            for a in range(self.count):
+                slot = lev * 4 + self.place.across
+                self.corner_x(a, lev, slot).wait_recv()
+                self.corner_y(a, lev, slot).wait_recv()
+                self.share(a, slot).start()
+
+        guarded(cond, body)
+
+    def middle(self):
+        steps, calls = self.steps, []
+        for i in range(1, len(steps) + 2):
+
+            def call(i=i):
+                if i < len(steps):
+                    self.first(*steps[i])
+                if 0 <= i - 1 < len(steps):
+                    self.second(*steps[i - 1])
+                if 0 <= i - 2 < len(steps):
+                    self.third(*steps[i - 2])
+
+            calls.append(call)
+        return calls
+
+    def end(self):
+        place = self.place
+
+        def finish(lev, side, cond):
+            def body():
+                for a in range(self.count):
+                    own, slot = side == 0, lev * 4 + place.here
+                    if side <= 0:
+                        pl.when(self.has_up)(
+                            lambda a=a: self.along_z(a, lev, own, True).wait_send()
+                        )
+                    if side >= 0:
+                        pl.when(self.has_down)(
+                            lambda a=a: self.along_z(a, lev, own, False).wait_send()
+                        )
+                    self.along_x(a, lev, slot, own).wait_send()
+                    self.along_y(a, lev, slot, own).wait_send()
+                    self.corner_x(a, lev, lev * 4 + place.there_y).wait_send()
+                    self.corner_y(a, lev, lev * 4 + place.there_x).wait_send()
+                    spots = [] if side == 0 else [slot]
+                    for other in (place.there_y, place.there_x, place.across):
+                        spots.append(lev * 4 + other)
+                    for spot in spots:
+                        self.share(a, spot).wait_send()
+                        self.share(a, spot, 1 - place.core).wait_recv()
+
+            guarded(cond, body)
+
+        for step in self.steps:
+            finish(*step)
+        for a in range(self.count):
+            self.own(a).wait()
+
+
+class NormGather(Gather):
+    def __init__(self, rows, gains, gain_row, planes):
+        super().__init__([jax.ShapeDtypeStruct(rows.shape, jnp.bfloat16)], planes)
+        self.ins = [(rows, pltpu.VMEM)]
+        self.scratch = self.scratch + [pltpu.VMEM(rows.shape, jnp.bfloat16)]
+        self.gains, self.gain_row = gains, gain_row
+
+    def bind(self, place, ins, outs, scratch):
+        super().bind(place, [scratch[-1]], outs, scratch[:-1])
+        self.rows = ins[0]
+
+    def begin(self):
+        self.gains.end()
+        rows = self.rows[...]
+        stat = lax.rsqrt(jnp.mean(rows * rows, axis=-1, keepdims=True) + norm_eps)
+        cols = rows.shape[1] // self.place.groups
+        for j in range(self.place.groups):
+            at = slice(j * cols, (j + 1) * cols)
+            gain = self.gains.result[j, self.gain_row : self.gain_row + 1, :].astype(jnp.float32)
+            self.sources[0][:, at] = (rows[:, at] * stat * gain).astype(jnp.bfloat16)
+        super().begin()
+
+
+class Reduce:
+    def __init__(self, operands, produce, slots, block, width, scratch=(), prepare=None):
+        planes, rows, kind = slots // 4, block // 2, jnp.bfloat16
+        self.planes, self.reach = planes, planes
+        self.ins = [(a, pltpu.VMEM) for a in operands]
+        self.outs = [(jax.ShapeDtypeStruct((block, width), jnp.float32), pltpu.VMEM)]
+        self.own_scratch, self.produce, self.prepare = len(scratch), produce, prepare
+        by_level = DMA((planes,))
+        self.scratch = (
+            list(scratch)
+            + [pltpu.VMEM((slots, block, width), kind), pltpu.VMEM((slots, rows, width), kind)]
+            + [pltpu.VMEM((planes, rows // 2, width), kind)] * 2
+            + [pltpu.VMEM((planes, rows, width), kind)] * 4
+            + [DMA((slots,))]
+            + [by_level] * 6
+            + [DMA, DMA((slots,))]
+            + [by_level] * 5
+            + [DMA]
+        )
+
+    def bind(self, place, ins, outs, scratch):
+        self.place, self.out = place, outs[0]
+        self.refs = list(ins) + list(scratch[: self.own_scratch])
+        scratch = scratch[self.own_scratch :]
+        self.part, self.mine = scratch[:2]
+        self.from_a, self.from_b, self.from_x, self.from_y = scratch[2:6]
+        self.from_up, self.from_down = scratch[6:8]
+        self.in_p, self.in_a, self.in_b, self.in_x, self.in_y = scratch[8:13]
+        self.in_up, self.in_down, self.in_m, self.out_p = scratch[13:17]
+        self.out_a, self.out_b, self.out_x, self.out_y, self.out_z, self.out_m = scratch[17:]
+        self.level = lax.rem(place.chip // 4, self.planes)
+        self.has_up, self.has_down = self.level < self.planes - 1, self.level > 0
+        self.steps = level_steps(self.level, self.planes, True)
+        self.rows = self.part.shape[1] // 2
+        self.half = self.rows // 2
+
+    def swap(self, slot):
+        theirs = part_rows((1 - self.place.core) * self.rows, self.rows)
+        return remote(
+            self.part.at[slot, theirs],
+            self.mine.at[slot],
+            self.out_p.at[slot],
+            self.in_p.at[slot],
+            self.place.mate,
+        )
+
+    def add_into(self, dst, terms, first, size):
+        step = 16
+
+        @pl.loop(0, size // step)
+        def _(i):
+            at = first + i * step
+            total = None
+            for term, shift in terms:
+                block = term[part_rows(at + shift, step), :].astype(jnp.float32)
+                total = block if total is None else total + block
+            dst[part_rows(at, step), :] = total.astype(dst.dtype)
+
+    def send_a(self, lev):
+        src = self.mine.at[lev * 4 + self.place.across, pl.ds(0, self.half)]
+        return remote(
+            src, self.from_a.at[lev], self.out_a.at[lev], self.in_a.at[lev], self.place.by_x
+        )
+
+    def send_b(self, lev):
+        src = self.mine.at[lev * 4 + self.place.across, pl.ds(self.half, self.half)]
+        return remote(
+            src, self.from_b.at[lev], self.out_b.at[lev], self.in_b.at[lev], self.place.by_y
+        )
+
+    def send_y(self, lev):
+        src = self.mine.at[lev * 4 + self.place.there_y]
+        return remote(
+            src, self.from_y.at[lev], self.out_y.at[lev], self.in_y.at[lev], self.place.by_y
+        )
+
+    def send_x(self, lev):
+        src = self.mine.at[lev * 4 + self.place.there_x]
+        return remote(
+            src, self.from_x.at[lev], self.out_x.at[lev], self.in_x.at[lev], self.place.by_x
+        )
+
+    def send_up(self, lev):
+        src = self.mine.at[lev * 4 + self.place.here]
+        return remote(
+            src, self.from_down.at[lev], self.out_z.at[lev], self.in_down.at[lev], self.place.above
+        )
+
+    def send_down(self, lev):
+        src = self.mine.at[lev * 4 + self.place.here]
+        return remote(
+            src, self.from_up.at[lev], self.out_z.at[lev], self.in_up.at[lev], self.place.below
+        )
+
+    def make(self, lev, side, cond):
+        def body():
+            for spot in (self.place.across, self.place.there_y, self.place.there_x, self.place.here):
+                slot = lev * 4 + spot
+                self.produce(self.part, slot, self.refs)
+                self.swap(slot).start()
+
+        guarded(cond, body)
+
+    def join(self, slot):
+        self.swap(slot).wait_recv()
+        mine = self.mine.at[slot]
+        terms = [(mine, 0), (self.part.at[slot], self.place.core * self.rows)]
+        self.add_into(mine, terms, 0, self.rows)
+
+    def first(self, lev, side, cond):
+        def body():
+            self.join(lev * 4 + self.place.across)
+            self.send_a(lev).start()
+            self.send_b(lev).start()
+            self.join(lev * 4 + self.place.there_y)
+            self.join(lev * 4 + self.place.there_x)
+
+        guarded(cond, body)
+
+    def second(self, lev, side, cond):
+        def body():
+            mine = self.mine.at[lev * 4 + self.place.there_y]
+            self.send_a(lev).wait_recv()
+            self.add_into(mine, [(mine, 0), (self.from_a.at[lev], 0)], 0, self.half)
+            self.send_y(lev).start()
+            mine = self.mine.at[lev * 4 + self.place.there_x]
+            self.send_b(lev).wait_recv()
+            self.add_into(mine, [(mine, 0), (self.from_b.at[lev], -self.half)], self.half, self.half)
+            self.send_x(lev).start()
+            self.join(lev * 4 + self.place.here)
+
+        guarded(cond, body)
+
+    def third(self, lev, side, cond):
+        rows, out = self.rows, self.out
+
+        def body():
+            mine = self.mine.at[lev * 4 + self.place.here]
+            self.send_y(lev).wait_recv()
+            self.send_x(lev).wait_recv()
+            terms = [(mine, 0), (self.from_y.at[lev], 0), (self.from_x.at[lev], 0)]
+            if side == 0:
+                own = out.at[part_rows(self.place.core * rows, rows)]
+                self.add_into(own, terms, 0, rows)
+
+                @pl.when(self.has_up)
+                def _():
+                    self.send_down(lev).wait_recv()
+                    self.add_into(own, [(own, 0), (self.from_up.at[lev], 0)], 0, rows)
+
+                @pl.when(self.has_down)
+                def _():
+                    self.send_up(lev).wait_recv()
+                    self.add_into(own, [(own, 0), (self.from_down.at[lev], 0)], 0, rows)
+            else:
+                down = side < 0
+                has_more = self.has_up if down else self.has_down
+                relay = self.send_down if down else self.send_up
+                more = self.from_up if down else self.from_down
+                self.add_into(mine, terms, 0, rows)
+
+                @pl.when(has_more)
+                def _():
+                    relay(lev).wait_recv()
+                    self.add_into(mine, [(mine, 0), (more.at[lev], 0)], 0, rows)
+
+                relay(lev).start()
+
+        guarded(cond, body)
+
+    def begin(self):
+        if self.prepare is not None:
+            self.prepare(self.refs)
+        self.make(*self.steps[0])
+
+    def middle(self):
+        steps, calls = self.steps, []
+        for i in range(len(steps) + 2):
+
+            def call(i=i):
+                if i + 1 < len(steps):
+                    self.make(*steps[i + 1])
+                if i < len(steps):
+                    self.first(*steps[i])
+                if 0 <= i - 1 < len(steps):
+                    self.second(*steps[i - 1])
+                if 0 <= i - 2 < len(steps):
+                    self.third(*steps[i - 2])
+
+            calls.append(call)
+        return calls
+
+    def hand(self, whose):
+        spot = part_rows(whose * self.rows, self.rows)
+        return remote(self.out.at[spot], self.out.at[spot], self.out_m, self.in_m, self.place.mate)
+
+    def end(self):
+        self.hand(self.place.core).start()
+
+        def finish(lev, side, cond):
+            def body():
+                for spot in range(4):
+                    self.swap(lev * 4 + spot).wait_send()
+                for send in (self.send_a, self.send_b, self.send_y, self.send_x):
+                    send(lev).wait_send()
+                if side < 0:
+                    self.send_down(lev).wait_send()
+                if side > 0:
+                    self.send_up(lev).wait_send()
+
+            guarded(cond, body)
+
+        for step in self.steps:
+            finish(*step)
+        self.hand(self.place.core).wait_send()
+        self.hand(1 - self.place.core).wait_recv()
+
+
+def greet(place, ops):
+    barrier = pltpu.get_barrier_semaphore()
+    expected = 1
+
+    def call(target):
+        pl.semaphore_signal(barrier, inc=1, device_id=target, device_id_type=MESH)
+
+    call(place.mate)
+    if any(op.reach == 0 for op in ops):
+        for j in range(1, place.groups):
+            call({EXPERT: place.partner(j)})
+        expected += place.groups - 1
+    else:
+        call(place.by_x)
+        call(place.by_y)
+        planes = max(op.reach for op in ops)
+        level = lax.rem(place.chip // 4, planes)
+        has_up, has_down = level < planes - 1, level > 0
+        pl.when(has_up)(lambda: call(place.above))
+        pl.when(has_down)(lambda: call(place.below))
+        expected += 2 + has_up.astype(jnp.int32) + has_down.astype(jnp.int32)
+    pl.semaphore_wait(barrier, expected)
+
+
+def chip_kernel(ops, *refs):
+    place = Place()
+    n_in = sum(len(op.ins) for op in ops)
+    n_out = sum(len(op.outs) for op in ops)
+    ins, outs, scratch = refs[:n_in], refs[n_in : n_in + n_out], refs[n_in + n_out :]
+    for op in ops:
+        op.bind(place, ins[: len(op.ins)], outs[: len(op.outs)], scratch[: len(op.scratch)])
+        ins, outs = ins[len(op.ins) :], outs[len(op.outs) :]
+        scratch = scratch[len(op.scratch) :]
+    greet(place, ops)
+    for op in ops:
+        op.begin()
+    queues = [op.middle() for op in ops]
+    for i in range(max(len(q) for q in queues)):
+        for queue in queues:
+            if i < len(queue):
+                queue[i]()
+    ended = [op.gains for op in ops if isinstance(op, NormGather)]
+    for op in ops:
+        if op not in ended:
+            op.end()
+
+
+def exchange(ops, ident):
+    ins = [pair for op in ops for pair in op.ins]
+    outs = [pair for op in ops for pair in op.outs]
+    moved = sum(a.size * a.dtype.itemsize for a, _ in ins + outs)
+    results = pl.pallas_call(
+        functools.partial(chip_kernel, ops),
+        out_shape=[shape for shape, _ in outs],
+        in_specs=[pl.BlockSpec(memory_space=space) for _, space in ins],
+        out_specs=[pl.BlockSpec(memory_space=space) for _, space in outs],
+        scratch_shapes=[entry for op in ops for entry in op.scratch],
+        compiler_params=pltpu.CompilerParams(
+            collective_id=ident, has_side_effects=True, vmem_limit_bytes=60 << 20
+        ),
+        cost_estimate=pl.CostEstimate(flops=0, bytes_accessed=moved, transcendentals=0),
+    )(*[a for a, _ in ins])
+    split = []
+    for op in ops:
+        split.append(results[: len(op.outs)])
+        results = results[len(op.outs) :]
+    return split
+
+
+def general_scores(query_blk, key_rows, first_row):
     scores = jnp.einsum(
         "qhd,khd->hqk", query_blk, key_rows, preferred_element_type=jnp.float32
     ) * DQK ** (-0.5)
@@ -72,7 +641,7 @@
 
     def one_block(block_index):
         first_row = block_index * blk_rows
-        scores = masked_scores(query_rows, key_rows, first_row)
+        scores = general_scores(query_rows, key_rows, first_row)
         row_max = jnp.max(scores, axis=-1, keepdims=True)
         log_total = row_max + jnp.log(jnp.sum(jnp.exp(scores - row_max), axis=-1, keepdims=True))
         att_weights = jnp.exp(scores - log_total).astype(jnp.bfloat16)
@@ -92,7 +661,7 @@
     def one_block(running, block_index):
         key_acc, value_acc = running
         first_row = block_index * blk_rows
-        scores = masked_scores(query_rows, key_rows, first_row)
+        scores = general_scores(query_rows, key_rows, first_row)
         att_probs = jnp.exp(scores - log_totals[block_index])
         att_weights = att_probs.astype(jnp.bfloat16)
         value_acc = value_acc + jnp.einsum(
@@ -139,10 +708,10 @@
         axis=-1,
     ).astype(jnp.bfloat16)
     latent_full = jnp.dot(normed1, latent_w, preferred_element_type=jnp.float32)
-    latent_stat = rms_scale(latent_full[:, :DL])
-    latent_unit = latent_full[:, :DL] * latent_stat
+    latent_stat = rms_scale(latent_full[:, : kvup_w.shape[0]])
+    latent_unit = latent_full[:, : kvup_w.shape[0]] * latent_stat
     latent = (latent_unit * gain_kv.astype(jnp.float32)).astype(jnp.bfloat16)
-    rot_key = rotate(latent_full[:, DL:], cosine, sine_part).astype(jnp.bfloat16)
+    rot_key = rotate(latent_full[:, kvup_w.shape[0] :], cosine, sine_part).astype(jnp.bfloat16)
     key_value = (
         jnp.dot(latent, kvup_w, preferred_element_type=jnp.float32)
         .astype(jnp.bfloat16)
@@ -171,7 +740,7 @@
     )
 
 
-def on_device(
+def general(
     layer_in,
     norm1_gain,
     q_weight,
@@ -190,8 +759,8 @@
     routes,
     out_grad,
 ):
-    groups = lax.axis_size("expert")
-    seq_len = layer_in.shape[0]
+    groups = lax.axis_size(EXPERT)
+    seq_len, width = layer_in.shape
     local_experts = expert_gate.shape[0]
     expert_count = local_experts * groups
     capacity = seq_len * TOPK * 4 // (3 * expert_count)
@@ -209,17 +778,17 @@
         up_sh,
         down_sh,
     ) = (
-        lax.all_gather(norm1_gain, "expert", axis=0, tiled=True),
-        lax.all_gather(q_weight, "expert", axis=0, tiled=True),
-        lax.all_gather(kva_weight, "expert", axis=0, tiled=True),
-        lax.all_gather(kv_gain, "expert", axis=0, tiled=True),
-        lax.all_gather(kvb_weight, "expert", axis=0, tiled=True),
-        lax.all_gather(o_weight, "expert", axis=1, tiled=True),
-        lax.all_gather(norm2_gain, "expert", axis=0, tiled=True),
-        lax.all_gather(router_weight, "expert", axis=0, tiled=True),
-        lax.all_gather(shared_gate, "expert", axis=0, tiled=True),
-        lax.all_gather(shared_up, "expert", axis=0, tiled=True),
-        lax.all_gather(shared_down, "expert", axis=1, tiled=True),
+        lax.all_gather(norm1_gain, EXPERT, axis=0, tiled=True),
+        lax.all_gather(q_weight, EXPERT, axis=0, tiled=True),
+        lax.all_gather(kva_weight, EXPERT, axis=0, tiled=True),
+        lax.all_gather(kv_gain, EXPERT, axis=0, tiled=True),
+        lax.all_gather(kvb_weight, EXPERT, axis=0, tiled=True),
+        lax.all_gather(o_weight, EXPERT, axis=1, tiled=True),
+        lax.all_gather(norm2_gain, EXPERT, axis=0, tiled=True),
+        lax.all_gather(router_weight, EXPERT, axis=0, tiled=True),
+        lax.all_gather(shared_gate, EXPERT, axis=0, tiled=True),
+        lax.all_gather(shared_up, EXPERT, axis=0, tiled=True),
+        lax.all_gather(shared_down, EXPERT, axis=1, tiled=True),
     )
     (
         stat_one,
@@ -239,7 +808,7 @@
     head_count = query_rows.shape[1]
     mixed_flat = mixed_heads.reshape(seq_len, head_count * DV)
     attn_part = jnp.dot(mixed_flat, output_w, preferred_element_type=jnp.float32)
-    hidden_state = layer_in + lax.psum(attn_part, "tensor")
+    hidden_state = layer_in + lax.psum(attn_part, TENSOR)
     stat_two = rms_scale(hidden_state)
     unit_two = hidden_state * stat_two
     normed2 = (unit_two * gain_two.astype(jnp.float32)).astype(jnp.bfloat16)
@@ -255,23 +824,23 @@
     buffer_pos = routes.reshape(-1) * capacity + slot_pos
 
     def to_owners(assigned):
-        buffer = jnp.zeros((rows_total, D), jnp.bfloat16).at[buffer_pos].set(assigned)
-        buffer = buffer.reshape(groups, local_experts * capacity, D)
-        arrived = lax.all_to_all(buffer, "expert", split_axis=0, concat_axis=0, tiled=True)
+        buffer = jnp.zeros((rows_total, width), jnp.bfloat16).at[buffer_pos].set(assigned)
+        buffer = buffer.reshape(groups, local_experts * capacity, width)
+        arrived = lax.all_to_all(buffer, EXPERT, split_axis=0, concat_axis=0, tiled=True)
         return (
-            arrived.reshape(groups, local_experts, capacity, D)
+            arrived.reshape(groups, local_experts, capacity, width)
             .transpose(1, 0, 2, 3)
-            .reshape(local_experts, groups * capacity, D)
+            .reshape(local_experts, groups * capacity, width)
         )
 
     def to_sources(results):
         arranged = (
-            results.reshape(local_experts, groups, capacity, D)
+            results.reshape(local_experts, groups, capacity, width)
             .transpose(1, 0, 2, 3)
-            .reshape(groups, local_experts * capacity, D)
-        )
-        arrived = lax.all_to_all(arranged, "expert", split_axis=0, concat_axis=0, tiled=True)
-        return arrived.reshape(rows_total, D)[buffer_pos].reshape(seq_len, TOPK, D)
+            .reshape(groups, local_experts * capacity, width)
+        )
+        arrived = lax.all_to_all(arranged, EXPERT, split_axis=0, concat_axis=0, tiled=True)
+        return arrived.reshape(rows_total, width)[buffer_pos].reshape(seq_len, TOPK, width)
 
     rows_in = to_owners(jnp.repeat(normed2, TOPK, axis=0))
     pre_gate = jnp.einsum("emd,edf->emf", rows_in, expert_gate, preferred_element_type=jnp.float32)
@@ -289,13 +858,13 @@
     shared_act = (jax.nn.silu(shared_pre_gate) * shared_pre_up).astype(jnp.bfloat16)
     shared_part = jnp.dot(shared_act, down_sh, preferred_element_type=jnp.float32)
     layer_out = hidden_state + lax.psum(
-        (routed_part + shared_part).astype(jnp.bfloat16), "tensor"
+        (routed_part + shared_part).astype(jnp.bfloat16), TENSOR
     ).astype(jnp.float32)
     out_rows = out_grad.astype(jnp.bfloat16)
     routed_cot = (
         (route_weight[:, :, None] * out_grad[:, None, :])
         .astype(jnp.bfloat16)
-        .reshape(seq_len * TOPK, D)
+        .reshape(seq_len * TOPK, width)
     )
     cot_in = to_owners(routed_cot)
     route_grad_part = jnp.einsum(
@@ -333,7 +902,7 @@
         + jnp.dot(shared_gate_delta, gate_sh.T, preferred_element_type=jnp.float32)
         + jnp.dot(shared_up_delta, up_sh.T, preferred_element_type=jnp.float32)
     )
-    normed2_grad, route_grad = lax.psum((normed2_part, route_grad_part), "tensor")
+    normed2_grad, route_grad = lax.psum((normed2_part, route_grad_part), TENSOR)
     prob_grad = jnp.einsum("tk,tke->te", route_grad, route_onehot)
     logit_delta = (
         router_probs * (prob_grad - jnp.sum(router_probs * prob_grad, axis=-1, keepdims=True))
@@ -379,9 +948,9 @@
     rot_part = jnp.sum(key_grad[..., DN:], axis=1)
     normed1_part = jnp.dot(query_delta, query_w.T, preferred_element_type=jnp.float32)
     latent_grad, rot_sum, normed1_query = (
-        lax.psum(latent_part.astype(jnp.bfloat16), "tensor").astype(jnp.float32),
-        lax.psum(rot_part.astype(jnp.bfloat16), "tensor").astype(jnp.float32),
-        lax.psum(normed1_part.astype(jnp.bfloat16), "tensor").astype(jnp.float32),
+        lax.psum(latent_part.astype(jnp.bfloat16), TENSOR).astype(jnp.float32),
+        lax.psum(rot_part.astype(jnp.bfloat16), TENSOR).astype(jnp.float32),
+        lax.psum(normed1_part.astype(jnp.bfloat16), TENSOR).astype(jnp.float32),
     )
     kv_gain_grad = jnp.sum(latent_grad * latent_unit, axis=0)
     scaled_lat = latent_grad * gain_kv.astype(jnp.float32)
@@ -413,17 +982,17 @@
         shared_up_grad,
         shared_down_grad,
     ) = (
-        lax.psum_scatter(norm1_gain_grad, "expert", scatter_dimension=0, tiled=True),
-        lax.psum_scatter(q_grad, "expert", scatter_dimension=0, tiled=True),
-        lax.psum_scatter(kva_grad, "expert", scatter_dimension=0, tiled=True),
-        lax.psum_scatter(kv_gain_grad, "expert", scatter_dimension=0, tiled=True),
-        lax.psum_scatter(kvb_grad, "expert", scatter_dimension=0, tiled=True),
-        lax.psum_scatter(o_grad, "expert", scatter_dimension=1, tiled=True),
-        lax.psum_scatter(norm2_gain_grad, "expert", scatter_dimension=0, tiled=True),
-        lax.psum_scatter(router_grad, "expert", scatter_dimension=0, tiled=True),
-        lax.psum_scatter(shared_gate_grad, "expert", scatter_dimension=0, tiled=True),
-        lax.psum_scatter(shared_up_grad, "expert", scatter_dimension=0, tiled=True),
-        lax.psum_scatter(shared_down_grad, "expert", scatter_dimension=1, tiled=True),
+        lax.psum_scatter(norm1_gain_grad, EXPERT, scatter_dimension=0, tiled=True),
+        lax.psum_scatter(q_grad, EXPERT, scatter_dimension=0, tiled=True),
+        lax.psum_scatter(kva_grad, EXPERT, scatter_dimension=0, tiled=True),
+        lax.psum_scatter(kv_gain_grad, EXPERT, scatter_dimension=0, tiled=True),
+        lax.psum_scatter(kvb_grad, EXPERT, scatter_dimension=0, tiled=True),
+        lax.psum_scatter(o_grad, EXPERT, scatter_dimension=1, tiled=True),
+        lax.psum_scatter(norm2_gain_grad, EXPERT, scatter_dimension=0, tiled=True),
+        lax.psum_scatter(router_grad, EXPERT, scatter_dimension=0, tiled=True),
+        lax.psum_scatter(shared_gate_grad, EXPERT, scatter_dimension=0, tiled=True),
+        lax.psum_scatter(shared_up_grad, EXPERT, scatter_dimension=0, tiled=True),
+        lax.psum_scatter(shared_down_grad, EXPERT, scatter_dimension=1, tiled=True),
     )
     return (
         layer_out,
@@ -445,43 +1014,478 @@
     )
 
 
+def fits(groups, heads, block, width):
+    return groups % heads == 0 and heads % 4 == 0 and block % 64 == 0 and 4 * groups * block * width <= 24 << 20
+
+
+def masked_scores(query_rows, key_rows):
+    scores = fsum("sqd,skd->sqk", query_rows, key_rows) * DQK ** (-0.5)
+    places = jnp.arange(query_rows.shape[1], dtype=jnp.int32)
+    return jnp.where(places[None, None, :] <= places[None, :, None], scores, -1e30)
+
+
+def to_blocks(grad_rows, groups):
+    rows, width = grad_rows.shape
+    return grad_rows.reshape(rows, groups, width // groups).transpose(1, 0, 2).astype(jnp.bfloat16)
+
+
+def from_blocks(blocks):
+    groups, rows, width = blocks.shape
+    return blocks.transpose(1, 0, 2).reshape(rows, groups * width)
+
+
+def widen(rows, width):
+    return jnp.pad(rows, [(0, 0)] * (rows.ndim - 1) + [(0, width - rows.shape[-1])])
+
+
+def by_heads(
+    layer_in,
+    norm1_gain,
+    q_weight,
+    kva_weight,
+    kv_gain,
+    kvb_weight,
+    o_weight,
+    norm2_gain,
+    router_weight,
+    shared_gate,
+    shared_up,
+    shared_down,
+    expert_gate,
+    expert_up,
+    expert_down,
+    routes,
+    out_grad,
+):
+    groups = lax.axis_size(EXPERT)
+    chip = lax.axis_index(EXPERT)
+    seq_len, width = layer_in.shape
+    capacity = seq_len * TOPK * 4 // (3 * groups)
+    heads = q_weight.shape[1] // DQK
+    copies = groups // heads
+    head = lax.rem(chip, heads)
+    own_cols = kva_weight.shape[0]
+    lat_rows, lat_width = kvb_weight.shape[0], kvb_weight.shape[0] * groups
+    hidden = shared_gate.shape[1] // groups
+    bf16 = jnp.bfloat16
+
+    kv_block = lat_rows * (DN + DV) // own_cols
+    head_parts = jnp.concatenate(
+        [
+            q_weight.reshape(own_cols, heads, DQK).transpose(1, 2, 0),
+            kvb_weight.reshape(lat_rows, heads, DN + DV)
+            .transpose(1, 0, 2)
+            .reshape(heads, kv_block, own_cols),
+            o_weight.reshape(heads, DV, own_cols),
+        ],
+        axis=1,
+    )
+    shared_parts = jnp.concatenate(
+        [
+            shared_gate.reshape(own_cols, groups, hidden).transpose(1, 2, 0),
+            shared_up.reshape(own_cols, groups, hidden).transpose(1, 2, 0),
+            shared_down.reshape(groups, hidden, own_cols),
+        ],
+        axis=1,
+    )
+    small = jnp.concatenate(
+        [
+            router_weight.T,
+            norm1_gain[None, :],
+            norm2_gain[None, :],
+            widen(kv_gain[None, :], own_cols),
+        ],
+        axis=0,
+    )
+    small = jnp.pad(small, [(0, -small.shape[0] % 16), (0, 0)])
+    at_kv = DQK
+    at_o = at_kv + kv_block
+    at_gate = at_o + DV
+    planes, all_planes = heads // 4, groups // 4
+    small_swap = Swap(jnp.broadcast_to(small[None], (groups,) + small.shape), True)
+    (small_all,), (got,), (latent_w,), (normed1_all,) = exchange(
+        [
+            small_swap,
+            Swap(jnp.tile(head_parts, (copies, 1, 1))),
+            Gather([kva_weight], all_planes),
+            NormGather(layer_in, small_swap, groups, planes),
+        ],
+        1,
+    )
+    query_wt = from_blocks(got[:, :at_kv])
+    kvup_w = got[:, at_kv:at_o].reshape(lat_width, DN + DV)
+    output_w = from_blocks(got[:, at_o:at_gate])
+    route_wt = from_blocks(small_all[:, :groups])
+    gain_one = small_all[:, groups].reshape(width).astype(jnp.float32)
+    gain_two = small_all[:, groups + 1].reshape(width).astype(jnp.float32)
+    gain_kv = small_all[:, groups + 2, :lat_rows].reshape(lat_width).astype(jnp.float32)
+    latent_w = latent_w.reshape(width, kva_weight.shape[1])
+    stat_one = rms_scale(layer_in)
+    unit_one = layer_in * stat_one
+    normed1_all = normed1_all.reshape(heads * seq_len, width)
+
+    cosine, sine_part = rope_tables(seq_len, DR)
+    by_seq = (heads, seq_len, -1)
+    query_full = fsum("td,qd->tq", normed1_all, query_wt).reshape(by_seq)
+    query_rows = jnp.concatenate(
+        [query_full[..., :DN], rotate(query_full[..., DN:], cosine, sine_part)], axis=-1
+    ).astype(bf16)
+    latent_full = fdot(normed1_all, latent_w)
+    latent_stat = rms_scale(latent_full[:, :lat_width])
+    latent_unit = latent_full[:, :lat_width] * latent_stat
+    latent = (latent_unit * gain_kv).astype(bf16)
+    rot_key = rotate(latent_full[:, lat_width:].reshape(by_seq), cosine, sine_part).astype(bf16)
+    key_value = fdot(latent, kvup_w).astype(bf16).reshape(by_seq)
+    key_rows = jnp.concatenate([key_value[..., :DN], rot_key], axis=-1)
+    value_rows = key_value[..., DN:]
+    scores = masked_scores(query_rows, key_rows)
+    row_max = jnp.max(scores, axis=-1, keepdims=True)
+    log_totals = row_max + jnp.log(jnp.sum(jnp.exp(scores - row_max), axis=-1, keepdims=True))
+    att_probs = jnp.exp(scores - log_totals)
+    att_weights = att_probs.astype(bf16)
+    mixed = fsum("sqk,skd->sqd", att_weights, value_rows).astype(bf16)
+    mixed_flat = mixed.reshape(heads * seq_len, DV)
+    out_rows = out_grad.astype(bf16)
+
+    def attn_part(part, slot, refs):
+        product = fdot(refs[0][slot], refs[1][...])
+        part[slot] = product.astype(bf16)
+
+    (shared_got,), (out_all,), (attn_sum,) = exchange(
+        [
+            Swap(shared_parts),
+            Gather([out_rows], all_planes),
+            Reduce([mixed, output_w], attn_part, heads, seq_len, width),
+        ],
+        2,
+    )
+    gate_sht = from_blocks(shared_got[:, :hidden])
+    up_sht = from_blocks(shared_got[:, hidden : 2 * hidden])
+    down_sh = from_blocks(shared_got[:, 2 * hidden :])
+    out_flat = out_all.reshape(groups * seq_len, width)
+    hidden_state = layer_in + attn_sum
+
+    stat_two = rms_scale(hidden_state)
+    unit_two = hidden_state * stat_two
+    normed2 = (unit_two * gain_two).astype(bf16)
+    router_probs = jax.nn.softmax(fsum("td,ed->te", normed2, route_wt), axis=-1)
+    experts = jnp.arange(groups, dtype=jnp.int32)
+    chosen = jnp.any(routes[:, :, None] == experts[None, None, :], axis=1)
+    marked = widen(jnp.where(chosen, router_probs, -1.0), -(-groups // LANES) * LANES)
+    ((normed2_all, marked_all),) = exchange([Gather([normed2, marked], all_planes)], 3)
+    here = lax.dynamic_index_in_dim(marked_all, chip, 2, keepdims=False)
+    normed2_flat = normed2_all.reshape(groups * seq_len, width)
+
+    routed = here >= 0.0
+    order = jnp.cumsum(routed.astype(jnp.int32), axis=1) - 1
+    slots = jnp.arange(capacity, dtype=jnp.int32)
+    picks = (routed[:, None, :] & (order[:, None, :] == slots[None, :, None])).astype(bf16)
+    weight_rows = jnp.sum(picks.astype(jnp.float32) * here[:, None, :], axis=-1).reshape(-1, 1)
+    rows_in = fsum("skt,std->skd", picks, normed2_all).astype(bf16).reshape(-1, width)
+    grad_rows = fsum("skt,std->skd", picks, out_all).reshape(-1, width)
+    cot_in = (weight_rows * grad_rows).astype(bf16)
+    gate_w, up_w, down_w = expert_gate[0], expert_up[0], expert_down[0]
+    pre_gate = fdot(rows_in, gate_w)
+    pre_up = fdot(rows_in, up_w)
+    expert_act = (jax.nn.silu(pre_gate) * pre_up).astype(bf16)
+    block_out = fdot(expert_act, down_w).astype(bf16).astype(jnp.float32)
+    hidden_grad_ex = fsum("md,fd->mf", cot_in, down_w)
+    gate_delta = (hidden_grad_ex * pre_up * silu_grad(pre_gate)).astype(bf16)
+    up_delta = (hidden_grad_ex * jax.nn.silu(pre_gate)).astype(bf16)
+    expert_down_grad = fsum("mf,md->fd", expert_act, cot_in)[None]
+    expert_gate_grad = fsum("md,mf->df", rows_in, gate_delta)[None]
+    expert_up_grad = fsum("md,mf->df", rows_in, up_delta)[None]
+    row_block = (
+        fsum("mf,df->md", gate_delta, gate_w) + fsum("mf,df->md", up_delta, up_w)
+    ).astype(bf16)
+    route_grad_rows = jnp.sum(grad_rows * block_out, axis=-1).reshape(groups, capacity)
+    by_slot = (groups, capacity, width)
+    out_block = (weight_rows * block_out).astype(bf16).reshape(by_slot)
+    route_grad = jnp.sum(picks.astype(jnp.float32) * route_grad_rows[:, :, None], axis=1)
+    route_part = (route_grad[:, :, None] * (experts == chip)).astype(bf16)
+    route_part = widen(route_part, marked.shape[1])
+
+    shared_pre_gate = fsum("fd,td->ft", gate_sht, normed2_flat)
+    shared_pre_up = fsum("fd,td->ft", up_sht, normed2_flat)
+    shared_act = (jax.nn.silu(shared_pre_gate) * shared_pre_up).astype(bf16)
+    shared_hidden_grad = fsum("fd,td->ft", down_sh, out_flat)
+    shared_gate_delta = (shared_hidden_grad * shared_pre_up * silu_grad(shared_pre_gate)).astype(bf16)
+    shared_up_delta = (shared_hidden_grad * jax.nn.silu(shared_pre_gate)).astype(bf16)
+    shared_grads = jnp.concatenate(
+        [
+            to_blocks(fdot(shared_gate_delta, normed2_flat), groups),
+            to_blocks(fdot(shared_up_delta, normed2_flat), groups),
+            to_blocks(fdot(shared_act, out_flat), groups),
+        ],
+        axis=1,
+    )
+    room = -(-hidden // 16) * 16
+
+    def stacked(pieces):
+        return jnp.concatenate(
+            [jnp.pad(x, [(0, room - hidden)] + [(0, 0)] * (x.ndim - 1)) for x in pieces], axis=0
+        )
+
+    def left_side(pieces):
+        rows = stacked(pieces).reshape(-1, groups, seq_len).transpose(1, 0, 2)
+        return jnp.concatenate([picks, rows], axis=1)
+
+    def expert_parts(part, slot, refs):
+        for k, start in ((0, 0), (1, width)):
+            left, own, held = refs[k], refs[2 + k], refs[7 + k]
+            held[:capacity] = own[slot]
+            for col in range(0, width, 512):
+                product = lax.dot_general(
+                    left[slot],
+                    held[:, col : col + 512],
+                    (((0,), (0,)), ((), ())),
+                    preferred_element_type=jnp.float32,
+                )
+                part[slot, :, start + col : start + col + 512] = product.astype(bf16)
+        part[slot, :, 2 * width :] = refs[6][slot]
+
+    def hold_shared(refs):
+        refs[7][capacity:] = refs[4][...]
+        refs[8][capacity:] = refs[5][...]
+
+    ((summed,),) = exchange(
+        [
+            Reduce(
+                [
+                    left_side([shared_act]),
+                    left_side([shared_gate_delta, shared_up_delta]),
+                    out_block,
+                    row_block.reshape(by_slot),
+                    stacked([down_sh]),
+                    stacked([gate_sht, up_sht]),
+                    route_part,
+                ],
+                expert_parts,
+                groups,
+                seq_len,
+                2 * width + marked.shape[1],
+                [
+                    pltpu.VMEM((capacity + room, width), bf16),
+                    pltpu.VMEM((capacity + 2 * room, width), bf16),
+                ],
+                hold_shared,
+            )
+        ],
+        4,
+    )
+    layer_out = hidden_state + summed[:, :width]
+    prob_grad = summed[:, 2 * width : 2 * width + groups]
+    logit_delta = (
+        router_probs * (prob_grad - jnp.sum(router_probs * prob_grad, axis=-1, keepdims=True))
+    ).astype(bf16)
+    normed2_grad = summed[:, width : 2 * width] + fdot(logit_delta, route_wt)
+    router_gradt = fsum("te,td->ed", logit_delta, normed2)
+    norm2_gain_grad = jnp.sum(normed2_grad * unit_two, axis=0)
+    scaled_two = normed2_grad * gain_two
+    hidden_grad = out_grad + stat_two * (
+        scaled_two - unit_two * jnp.mean(scaled_two * unit_two, axis=-1, keepdims=True)
+    )
+
+    hidden_rows = hidden_grad.astype(bf16)
+    ((hidden_all,),) = exchange([Gather([hidden_rows], planes)], 5)
+    hidden_all = hidden_all.reshape(heads * seq_len, width)
+    o_grad = fdot(lax.optimization_barrier(mixed_flat.T), hidden_all)
+    mixed_grad = fsum("td,vd->tv", hidden_all, output_w).astype(bf16).reshape(by_seq)
+    value_grad = fsum("sqk,sqd->skd", att_weights, mixed_grad)
+    dprob = fsum("sqd,skd->sqk", mixed_grad, value_rows)
+    row_delta = jnp.sum(att_probs * dprob, axis=-1, keepdims=True)
+    score_delta = (att_probs * (dprob - row_delta) * DQK ** (-0.5)).astype(bf16)
+    query_grad = fsum("sqk,skd->sqd", score_delta, key_rows)
+    key_grad = fsum("sqk,sqd->skd", score_delta, query_rows)
+    query_delta = (
+        jnp.concatenate(
+            [query_grad[..., :DN], rotate_back(query_grad[..., DN:], cosine, sine_part)], axis=-1
+        )
+        .astype(bf16)
+    )
+    kv_delta = (
+        jnp.concatenate([key_grad[..., :DN], value_grad], axis=-1)
+        .astype(bf16)
+    )
+
+    def back_part(part, slot, refs):
+        for col in range(0, width, 512):
+            product = fdot(refs[0][slot], refs[1][:, col : col + 512])
+            part[slot, :, col : col + 512] = product.astype(bf16)
+        product = fdot(refs[2][slot], refs[3][...])
+        part[slot, :, width : width + lat_width] = product.astype(bf16)
+        part[slot, :, width + lat_width :] = refs[4][slot]
+
+    (owned_early,), (back,) = exchange(
+        [
+            Swap(jnp.concatenate([shared_grads, to_blocks(o_grad, groups)], axis=1)),
+            Reduce(
+                [
+                    query_delta,
+                    query_wt,
+                    kv_delta,
+                    kvup_w.T,
+                    widen(key_grad[..., DN:], LANES).astype(bf16),
+                ],
+                back_part,
+                heads,
+                seq_len,
+                width + lat_width + LANES,
+            ),
+        ],
+        6,
+    )
+    normed1_query = back[:, :width]
+    latent_grad = back[:, width : width + lat_width]
+    rot_sum = back[:, width + lat_width : width + lat_width + DR]
+
+    def own_rows(rows):
+        return lax.dynamic_slice_in_dim(rows, head * seq_len, seq_len, 0)
+
+    own_unit, own_stat = own_rows(latent_unit), own_rows(latent_stat)
+    kv_gain_grad = jnp.sum(latent_grad * own_unit, axis=0)
+    scaled_lat = latent_grad * gain_kv
+    latent_back = own_stat * (
+        scaled_lat - own_unit * jnp.mean(scaled_lat * own_unit, axis=-1, keepdims=True)
+    )
+    latent_delta = jnp.concatenate(
+        [latent_back, rotate_back(rot_sum, cosine, sine_part)], axis=-1
+    ).astype(bf16)
+    query_delta_t = lax.optimization_barrier(query_delta.reshape(heads * seq_len, DQK).T)
+    kv_flat = kv_delta.reshape(heads * seq_len, DN + DV)
+    latent_t = lax.optimization_barrier(latent.T)
+    (owned_heads,), (latent_delta_all,) = exchange(
+        [
+            Swap(
+                jnp.concatenate(
+                    [
+                        to_blocks(fdot(query_delta_t, normed1_all), groups),
+                        fdot(latent_t, kv_flat).astype(bf16).reshape(groups, kv_block, own_cols),
+                    ],
+                    axis=1,
+                )
+            ),
+            Gather([latent_delta], planes),
+        ],
+        7,
+    )
+    latent_delta_all = latent_delta_all.reshape(heads * seq_len, -1)
+    normed1_grad = normed1_query + fsum("tl,dl->td", latent_delta, latent_w)
+    norm1_gain_grad = jnp.sum(normed1_grad * unit_one, axis=0)
+    scaled_one = normed1_grad * gain_one
+    x_grad = hidden_grad + stat_one * (
+        scaled_one - unit_one * jnp.mean(scaled_one * unit_one, axis=-1, keepdims=True)
+    )
+
+    share = latent_delta_all.shape[1] // heads
+    latent_share = lax.dynamic_slice_in_dim(latent_delta_all, head * share, share, 1)
+    kva_blocks = to_blocks(fdot(lax.optimization_barrier(latent_share.T), normed1_all), groups)
+
+    def by_owner(row):
+        return widen(row.reshape(groups, 1, -1), own_cols)
+
+    small_grads = jnp.concatenate(
+        [
+            router_gradt.reshape(groups, groups, own_cols).transpose(1, 0, 2),
+            by_owner(norm1_gain_grad),
+            by_owner(norm2_gain_grad),
+            by_owner(kv_gain_grad),
+        ],
+        axis=1,
+    )
+    small_grads = jnp.pad(small_grads, [(0, 0), (0, -small_grads.shape[1] % 8), (0, 0)])
+    kva_blocks = jnp.pad(kva_blocks, [(0, 0), (0, -share % 16), (0, 0)])
+    (owned_share,), (owned_small,) = exchange([Swap(kva_blocks), Swap(small_grads)], 8)
+    small_sums = jnp.sum(owned_small, axis=0)
+
+    def over_copies(blocks):
+        blocks = blocks.astype(jnp.float32).reshape((copies, heads) + blocks.shape[1:])
+        return jnp.sum(blocks, axis=0)
+
+    of_heads = over_copies(owned_heads)
+    q_grad = of_heads[:, :at_kv].transpose(2, 0, 1).reshape(own_cols, heads * DQK)
+    kvb_grad = (
+        of_heads[:, at_kv:]
+        .reshape(heads, lat_rows, DN + DV)
+        .transpose(1, 0, 2)
+        .reshape(lat_rows, heads * (DN + DV))
+    )
+    own_o_grad = over_copies(owned_early[:, 3 * hidden :]).reshape(heads * DV, own_cols)
+    kva_grad = over_copies(owned_share)[:, :share].reshape(heads * share, own_cols).T
+    of_shared = owned_early[:, : 3 * hidden].astype(jnp.float32)
+
+    def columns(blocks):
+        return blocks.reshape(groups * hidden, own_cols)
+
+    shared_gate_grad = columns(of_shared[:, :hidden]).T
+    shared_up_grad = columns(of_shared[:, hidden : 2 * hidden]).T
+    shared_down_grad = columns(of_shared[:, 2 * hidden :])
+    router_grad = small_sums[:groups].T
+    return (
+        layer_out,
+        x_grad,
+        small_sums[groups],
+        q_grad,
+        kva_grad,
+        small_sums[groups + 2, :lat_rows],
+        kvb_grad,
+        own_o_grad,
+        small_sums[groups + 1],
+        router_grad,
+        shared_gate_grad,
+        shared_up_grad,
+        shared_down_grad,
+        expert_gate_grad,
+        expert_up_grad,
+        expert_down_grad,
+    )
+
+
+def on_device(layer_in, *rest):
+    groups, heads = lax.axis_size(EXPERT), rest[1].shape[1] // DQK
+    one_each = rest[11].shape[0] == 1
+    if one_each and fits(groups, heads, *layer_in.shape):
+        return by_heads(layer_in, *rest)
+    return general(layer_in, *rest)
+
+
 def solution(mesh):
     in_specs = (
-        P("expert", None),
-        P("expert"),
-        P("expert", "tensor"),
-        P("expert", None),
-        P("expert"),
-        P("expert", "tensor"),
-        P("tensor", "expert"),
-        P("expert"),
-        P("expert", None),
-        P("expert", "tensor"),
-        P("expert", "tensor"),
-        P("tensor", "expert"),
-        P("expert", None, "tensor"),
-        P("expert", None, "tensor"),
-        P("expert", "tensor", None),
-        P("expert", None),
-        P("expert", None),
+        P(EXPERT, None),
+        P(EXPERT),
+        P(EXPERT, TENSOR),
+        P(EXPERT, None),
+        P(EXPERT),
+        P(EXPERT, TENSOR),
+        P(TENSOR, EXPERT),
+        P(EXPERT),
+        P(EXPERT, None),
+        P(EXPERT, TENSOR),
+        P(EXPERT, TENSOR),
+        P(TENSOR, EXPERT),
+        P(EXPERT, None, TENSOR),
+        P(EXPERT, None, TENSOR),
+        P(EXPERT, TENSOR, None),
+        P(EXPERT, None),
+        P(EXPERT, None),
     )
     out_specs = (
-        P("expert", None),
-        P("expert", None),
-        P("expert"),
-        P("expert", "tensor"),
-        P("expert", None),
-        P("expert"),
-        P("expert", "tensor"),
-        P("tensor", "expert"),
-        P("expert"),
-        P("expert", None),
-        P("expert", "tensor"),
-        P("expert", "tensor"),
-        P("tensor", "expert"),
-        P("expert", None, "tensor"),
-        P("expert", None, "tensor"),
-        P("expert", "tensor", None),
+        P(EXPERT, None),
+        P(EXPERT, None),
+        P(EXPERT),
+        P(EXPERT, TENSOR),
+        P(EXPERT, None),
+        P(EXPERT),
+        P(EXPERT, TENSOR),
+        P(TENSOR, EXPERT),
+        P(EXPERT),
+        P(EXPERT, None),
+        P(EXPERT, TENSOR),
+        P(EXPERT, TENSOR),
+        P(TENSOR, EXPERT),
+        P(EXPERT, None, TENSOR),
+        P(EXPERT, None, TENSOR),
+        P(EXPERT, TENSOR, None),
     )
     return jax.shard_map(
         on_device, mesh=mesh, in_specs=in_specs, out_specs=out_specs, check_vma=False

time: 2520 us -> 737 us (0.29)
  waiting for transfers between devices: 1740 us -> 0 us
  Pallas kernels: 0 us -> 445 us
  blocking collectives: 310 us -> 0 us
  starting transfers between devices: 147 us -> 0 us
  matrix products: 170 us -> 117 us
    reduce_scatter x8 -> x0, waiting for transfers between devices: 1320 us -> none  [the longest x1 248 us: on_device(): lax.psum_scatter(shared_up_grad, 'expert', scatter_dimension=0, tiled=True)]
    pallas_call x0 -> x8, Pallas kernels: none -> 445 us  [exchange(): pl.pallas_call(functools.partial(chip_kernel, ops), out_shape=[shape for...]
    all_gather x7 -> x0, waiting for transfers between devices: 268 us -> none  [the longest x1 87.3 us: on_device(): lax.all_gather(q_weight, 'expert', axis=0, tiled=True)]
    all_gather x3 -> x0, blocking collectives: 187 us -> none  [the longest x1 106 us: on_device(): lax.all_gather(router_weight, 'expert', axis=0, tiled=True)]
    all_to_all x4 -> x0, waiting for transfers between devices: 155 us -> none  [the longest x2 78.5 us: to_owners(): lax.all_to_all(buffer, 'expert', split_axis=0, concat_axis=0, tiled=True)]
    all_to_all x4 -> x0, starting transfers between devices: 146 us -> none  [the longest x2 94.8 us: to_sources(): lax.all_to_all(arranged, 'expert', split_axis=0, concat_axis=0, tiled=True)]
    unnamed x2 -> x0, blocking collectives: 115 us -> none
    dot_general x43 -> x35, matrix products: 170 us -> 117 us  [the longest x22 66.9 us: fsum(): return jnp.einsum(spec, left, right, preferred_element_type=jnp.float32)]
  transfers between devices with their start and end apart: 22 -> 0, of which waited for: 13 -> 0; matrix products, arithmetic and copies ran while one was open for 10% -> 0% of each run, Pallas kernels for 0% -> 0%
where the time goes in v1:
time: 737 us; the launch traced here: 726 us
  Pallas kernels  445 us (60%)
  matrix products  117 us (16%)
  local copies, waits for them, and re-layouts  110 us (15%)
  other arithmetic  51.3 us (7%)
    pallas_call x8, Pallas kernels, exchange(): pl.pallas_call(functools.partial(chip_kernel, ops), out_shape=[shape for...  445 us
    dot_general x22, matrix products, fsum(): return jnp.einsum(spec, left, right, preferred_element_type=jnp.float32)  66.9 us
    dot_general x13, matrix products, fdot(): return jnp.dot(left, right, preferred_element_type=jnp.float32)  50.4 us
    dot_general x4, local copies, waits for them, and re-layouts, fdot(): return jnp.dot(left, right, preferred_element_type=jnp.float32)  37.3 us
    unnamed x154, local copies, waits for them, and re-layouts  26 us

profile of v1, /device:TPU:0, one launch (start us, length us, event | category | flops | bytes accessed | tf_op | source)
XLA Modules:
  0.0 725.7 jit_solution(928127550008611386)
XLA Ops:
  19.7 77.6 %shard_map.288 = (bf16[16,32,128]{2,1,0:T(8,128)(2,1)}, bf16[16,384,128]{2,1,0:T(8,128)(2,1)}, bf16[16,128,576]{2,1,0:T(8,128)(2,1)}, bf16[8,128,2048]{2,1,0:T(8,128)(2,1)}) custom-call(bf16[16,32,128]{2,1,0:T(8,128)(2,1)} %broadcast_in_dim.33.refs_0_, bf16[16,384,128]{2,1,0:T(8,128)(2,1)} %bitcast.285, bf16[128,576]{1,0:T(8,128)(2,1)} %copy.217.refs_2_, ...), custom_call_target="tpu_custom_call" | custom-call | bytes 11157504 | tf_op jit(solution)/shard_map/pallas_call | solution.py:611
  116.3 5.3 fusion.102
  151.5 6.3 copy.254
  157.8 86.1 %shard_map.289 = (bf16[16,264,128]{2,1,0:T(8,128)(2,1)}, bf16[16,128,2048]{2,1,0:T(8,128)(2,1)}, f32[128,2048]{1,0:T(8,128)}) custom-call(bf16[16,264,128]{2,1,0:T(8,128)(2,1)} %pad_maximum_fusion.1.refs_0_, bf16[128,2048]{1,0:T(8,128)(2,1)} %convert_element_type.273.refs_1_, bf16[8,128,128]{2,1,0:T(8,128)(2,1)} %convolution_convert_fusion.11.refs_2_, ...), custom_call_target="tpu_custom_call" | custom-call | bytes 12910592 | tf_op jit(solution)/shard_map/pallas_call | solution.py:611
  250.2 6.9 fusion.92
  258.2 12.3 %copy.240 = bf16[2048,2048]{1,0:T(8,128)(2,1)} copy(bf16[2048,2048]{0,1:T(8,128)(2,1)} %bitcast.271) | data formatting | bytes 16777216 | tf_op jit(solution)/shard_map/dot_general | solution.py:55
  270.4 51.9 %shard_map.290 = (bf16[16,128,2048]{2,1,0:T(8,128)(2,1)}, f32[16,128,128]{2,1,0:T(8,128)}) custom-call(bf16[128,2048]{1,0:T(8,128)(2,1)} %copy-done.13, f32[128,128]{1,0:T(8,128)} %pad.54.refs_1_), custom_call_target="tpu_custom_call" | custom-call | bytes 10027008 | tf_op jit(solution)/shard_map/pallas_call | solution.py:611
  324.5 4.8 fusion.46
  336.1 6.3 fusion.28
  350.1 4.9 multiply_convert_fusion.3
  355.1 5.7 fusion.2
  374.1 5.9 multiply_convert_fusion.1
  380.0 5.0 convolution_bitcast_fusion.2
  385.0 4.9 convolution_bitcast_fusion
  389.9 5.1 convolution_bitcast_fusion.1
  398.6 5.4 add_convert_fusion
  404.0 94.9 %shard_map.291 = f32[128,4224]{1,0:T(8,128)} custom-call(bf16[16,160,128]{2,1,0:T(8,128)(2,1)} %pad_maximum_fusion.5.refs_0_, bf16[16,256,128]{2,1,0:T(8,128)(2,1)} %pad_maximum_fusion.2.refs_1_, bf16[16,64,2048]{2,1,0:T(8,128)(2,1)} %bitcast.280, bf16[16,64,2048]{2,1,0:T(8,128)(2,1)} %bitcast.289, bf16[96,2048]{1,0:T(8,128)(2,1)} %pad.58.refs_4_, ...), custom_call_target="tpu_custom_call" | custom-call | bytes 13959168 | tf_op jit(solution)/shard_map/pallas_call | solution.py:611
  506.8 26.5 %shard_map.292 = bf16[8,128,2048]{2,1,0:T(8,128)(2,1)} custom-call(bf16[128,2048]{1,0:T(8,128)(2,1)} %get-tuple-element.120.refs_0_), custom_call_target="tpu_custom_call" | custom-call | bytes 4718592 | tf_op jit(solution)/shard_map/pallas_call | solution.py:611
  553.0 6.4 copy.242
  563.1 12.3 %copy.239 = bf16[2048,2048]{1,0:T(8,128)(2,1)} copy(bf16[2048,2048]{0,1:T(8,128)(2,1)} %bitcast.267) | data formatting | bytes 16777216 | tf_op jit(solution)/shard_map/dot_general | solution.py:55
  575.5 6.2 fusion.27
  585.7 53.9 %shard_map.293 = (bf16[16,392,128]{2,1,0:T(8,128)(2,1)}, f32[128,2688]{1,0:T(8,128)}) custom-call(bf16[16,392,128]{2,1,0:T(8,128)(2,1)} %pad_maximum_fusion.refs_0_, bf16[8,128,192]{2,1,0:T(8,128)(2,1)} %pad_maximum_fusion.6.refs_1_, bf16[192,2048]{1,0:T(8,128)(2,1)} %bitcast.295, bf16[8,128,256]{2,1,0:T(8,128)(2,1)} %pad_maximum_fusion.7.refs_3_, ...), custom_call_target="tpu_custom_call" | custom-call | bytes 6815744 | tf_op jit(solution)/shard_map/pallas_call | solution.py:611
  654.4 35.4 %shard_map.294 = (bf16[16,256,128]{2,1,0:T(8,128)(2,1)}, bf16[8,128,576]{2,1,0:T(8,128)(2,1)}) custom-call(bf16[16,256,128]{2,1,0:T(8,128)(2,1)} %pad_maximum_fusion.3.refs_0_, bf16[128,576]{1,0:T(8,128)(2,1)} %copy-done.26), custom_call_target="tpu_custom_call" | custom-call | bytes 3424256 | tf_op jit(solution)/shard_map/pallas_call | solution.py:611
  696.8 19.0 %shard_map.295 = (bf16[16,80,128]{2,1,0:T(8,128)(2,1)}, f32[16,24,128]{2,1,0:T(8,128)}) custom-call(bf16[16,80,128]{2,1,0:T(8,128)(2,1)} %pad.63.refs_0_, f32[16,24,128]{2,1,0:T(8,128)} %pad.65.refs_1_), custom_call_target="tpu_custom_call" | custom-call | bytes 1048576 | tf_op jit(solution)/shard_map/pallas_call | solution.py:611
  (297 shorter events, 174.7 us)
Async XLA Ops:
  0.6 354.4 %copy-start = (bf16[1,704,2048]{2,1,0:T(8,128)(2,1)S(1)}, bf16[1,704,2048]{2,1,0:T(8,128)(2,1)}, u32[]{:S(2)}) copy-start(bf16[1,704,2048]{2,1,0:T(8,128)(2,1)} %param.31) | copy-start | bytes 8650756
  1.2 7.4 %copy-start.56 = (f32[128]{0:T(128)}, f32[128]{0:T(128)S(1)}, u32[]{:S(2)}) copy-start(f32[128]{0:T(128)S(1)} %iota_convert_fusion) | copy-start | bytes 1540
  1.2 7.4 %copy-start.58 = (f32[32]{0:T(128)}, f32[32]{0:T(128)S(1)}, u32[]{:S(2)}) copy-start(f32[32]{0:T(128)S(1)} %multiply_power_fusion) | copy-start | bytes 388
  8.6 121.6 %copy-start.39 = (f32[128,32]{1,0:T(8,128)}, f32[128,32]{1,0:T(8,128)S(1)}, u32[]{:S(2)}) copy-start(f32[128,32]{1,0:T(8,128)S(1)} %get-tuple-element.161) | copy-start | bytes 49156
  133.7 12.7 %copy-start.47 = (bf16[8,128,32]{1,2,0:T(8,128)(2,1)}, bf16[8,128,32]{1,2,0:T(8,128)(2,1)S(1)}, u32[]{:S(2)}) copy-start(bf16[8,128,32]{1,2,0:T(8,128)(2,1)S(1)} %copy.222) | copy-start | bytes 196612
  134.8 11.6 %copy-start.49 = (bf16[8,128,32]{1,2,0:T(8,128)(2,1)}, bf16[8,128,32]{1,2,0:T(8,128)(2,1)S(1)}, u32[]{:S(2)}) copy-start(bf16[8,128,32]{1,2,0:T(8,128)(2,1)S(1)} %copy.223) | copy-start | bytes 196612
  143.8 7.7 %copy-start.20 = (bf16[1024,256]{1,0:T(8,128)(2,1)}, bf16[1024,256]{1,0:T(8,128)(2,1)S(1)}, u32[]{:S(2)}) copy-start(bf16[1024,256]{1,0:T(8,128)(2,1)S(1)} %convolution_convert_fusion.3) | copy-start | bytes 1572868
  157.8 86.1 %copy-start.6 = (f32[128,2048]{1,0:T(8,128)S(1)}, f32[128,2048]{1,0:T(8,128)}, u32[]{:S(2)}) copy-start(f32[128,2048]{1,0:T(8,128)} %refs_3_.1) | copy-start | bytes 3145732
  246.6 10.5 %copy-start.13 = (bf16[128,2048]{1,0:T(8,128)(2,1)}, bf16[128,2048]{1,0:T(8,128)(2,1)S(1)}, u32[]{:S(2)}) copy-start(bf16[128,2048]{1,0:T(8,128)(2,1)S(1)} %multiply_convert_fusion.6.refs_0_) | copy-start | bytes 1572868
  249.2 7.9 %copy-start.22 = (bf16[16,11,8,128]{3,2,1,0:T(8,128)(2,1)}, bf16[16,11,8,128]{3,2,1,0:T(8,128)(2,1)S(1)}, u32[]{:S(2)}) copy-start(bf16[16,11,8,128]{3,2,1,0:T(8,128)(2,1)S(1)} %get-tuple-element.143) | copy-start | bytes 1081348
  249.2 7.9 %copy-start.31 = (bf16[16,11,8,128]{3,2,1,0:T(8,128)(2,1)}, bf16[16,11,8,128]{3,2,1,0:T(8,128)(2,1)S(1)}, u32[]{:S(2)}) copy-start(bf16[16,11,8,128]{3,2,1,0:T(8,128)(2,1)S(1)} %get-tuple-element.144) | copy-start | bytes 1081348
  329.3 25.7 %copy-start.3 = (f32[16,64,2048]{2,1,0:T(8,128)}, f32[16,64,2048]{2,1,0:T(8,128)S(1)}, u32[]{:S(2)}) copy-start(f32[16,64,2048]{2,1,0:T(8,128)S(1)} %fusion.46) | copy-start | bytes 25165828
  336.0 7.3 %copy-start.27 = (bf16[88,2048]{1,0:T(8,128)(2,1)}, bf16[88,2048]{1,0:T(8,128)(2,1)S(1)}, u32[]{:S(2)}) copy-start(bf16[88,2048]{1,0:T(8,128)(2,1)S(1)} %get-tuple-element.133) | copy-start | bytes 1081348
  404.0 96.0 %copy-start.14 = (bf16[128,2048]{1,0:T(8,128)(2,1)S(1)}, bf16[128,2048]{1,0:T(8,128)(2,1)}, u32[]{:S(2)}) copy-start(bf16[128,2048]{1,0:T(8,128)(2,1)} %copy-done.13) | copy-start | bytes 1572868
  404.0 97.8 %copy-start.12 = (f32[128,2048]{1,0:T(8,128)S(1)}, f32[128,2048]{1,0:T(8,128)}, u32[]{:S(2)}) copy-start(f32[128,2048]{1,0:T(8,128)} %copy-done.11) | copy-start | bytes 3145732
  404.0 97.8 %copy-start.55 = (bf16[16,32,128]{2,1,0:T(8,128)(2,1)S(1)}, bf16[16,32,128]{2,1,0:T(8,128)(2,1)}, u32[]{:S(2)}) copy-start(bf16[16,32,128]{2,1,0:T(8,128)(2,1)} %get-tuple-element.34) | copy-start | bytes 393220
  563.1 12.3 %copy-start.30 = (bf16[88,2048]{1,0:T(8,128)(2,1)S(1)}, bf16[88,2048]{1,0:T(8,128)(2,1)}, u32[]{:S(2)}) copy-start(bf16[88,2048]{1,0:T(8,128)(2,1)} %copy-done.29) | copy-start | bytes 1081348
  585.7 55.1 %copy-start.61 = (f32[128]{0:T(128)S(1)}, f32[128]{0:T(128)}, u32[]{:S(2)}) copy-start(f32[128]{0:T(128)} %dynamic-slice.3) | copy-start | bytes 1540
  585.7 56.4 %copy-start.57 = (f32[128]{0:T(128)S(1)}, f32[128]{0:T(128)}, u32[]{:S(2)}) copy-start(f32[128]{0:T(128)} %copy-done.56) | copy-start | bytes 1540
  585.7 56.4 %copy-start.59 = (f32[32]{0:T(128)S(1)}, f32[32]{0:T(128)}, u32[]{:S(2)}) copy-start(f32[32]{0:T(128)} %copy-done.58) | copy-start | bytes 388
  585.7 57.7 %copy-start.7 = (f32[128,2048]{1,0:T(8,128)S(1)}, f32[128,2048]{1,0:T(8,128)}, u32[]{:S(2)}) copy-start(f32[128,2048]{1,0:T(8,128)} %refs_3_.1) | copy-start | bytes 3145732
  585.7 57.7 %copy-start.46 = (f32[16,1,128]{2,1,0:T(1,128)S(1)}, f32[16,1,128]{2,1,0:T(1,128)}, u32[]{:S(2)}) copy-start(f32[16,1,128]{2,1,0:T(1,128)} %get-tuple-element.151) | copy-start | bytes 24580
  696.8 27.9 %slice-start = ((f32[8,256,128]{2,1,0:T(8,128)}), f32[8,64,128]{2,1,0:T(8,128)S(1)}, s32[]{:S(2)}) async-start(f32[8,256,128]{2,1,0:T(8,128)} %convert_reduce_fusion), calls=%async_computation | async-start | bytes 524288 | tf_op jit(solution)/shard_map/slice | solution.py:1408
  716.7 8.8 %copy-start.1 = (bf16[1,704,2048]{2,1,0:T(8,128)(2,1)S(1)}, bf16[1,704,2048]{2,1,0:T(8,128)(2,1)}, u32[]{:S(2)}) copy-start(bf16[1,704,2048]{2,1,0:T(8,128)(2,1)} %param.31) | copy-start | bytes 8650756
  (48 other events, 196.3 us)

commit v2 on v1

--- a/solution.py
+++ b/solution.py
@@ -53,6 +53,12 @@
 
 def fdot(left, right):
     return jnp.dot(left, right, preferred_element_type=jnp.float32)
+
+
+def dot_nt(left, right):
+    return lax.dot_general(
+        left, right, (((1,), (1,)), ((), ())), preferred_element_type=jnp.float32
+    )
 
 
 def fsum(spec, left, right):
@@ -113,8 +119,9 @@
 class Swap:
     reach = 0
 
-    def __init__(self, blocks, vmem_result=False):
+    def __init__(self, blocks, vmem_result=False, pace=2):
         groups = blocks.shape[0]
+        self.pace = groups if vmem_result else pace
         self.ins = [(blocks, pltpu.VMEM)]
         self.outs = [
             (
@@ -142,13 +149,17 @@
         chip = self.place.chip
         return pltpu.make_async_copy(self.source.at[chip], self.result.at[chip], self.own_sem)
 
+    def send(self, first):
+        for j in range(first, min(first + self.pace, self.groups)):
+            self.copy(j, self.place.partner(j), self.place.chip).start()
+
     def begin(self):
         self.own().start()
-        for j in range(1, self.groups):
-            self.copy(j, self.place.partner(j), self.place.chip).start()
+        self.send(1)
 
     def middle(self):
-        return []
+        firsts = range(1 + self.pace, self.groups, self.pace)
+        return [functools.partial(self.send, first) for first in firsts]
 
     def end(self):
         self.own().wait()
@@ -340,12 +351,16 @@
 
 
 class Reduce:
-    def __init__(self, operands, produce, slots, block, width, scratch=(), prepare=None):
+    def __init__(
+        self, operands, produce, slots, block, width, scratch=(), prepare=None, extra=(), prelude=None
+    ):
         planes, rows, kind = slots // 4, block // 2, jnp.bfloat16
         self.planes, self.reach = planes, planes
         self.ins = [(a, pltpu.VMEM) for a in operands]
         self.outs = [(jax.ShapeDtypeStruct((block, width), jnp.float32), pltpu.VMEM)]
+        self.outs += [(shape, pltpu.VMEM) for shape in extra]
         self.own_scratch, self.produce, self.prepare = len(scratch), produce, prepare
+        self.prelude = prelude
         by_level = DMA((planes,))
         self.scratch = (
             list(scratch)
@@ -361,7 +376,7 @@
 
     def bind(self, place, ins, outs, scratch):
         self.place, self.out = place, outs[0]
-        self.refs = list(ins) + list(scratch[: self.own_scratch])
+        self.refs = list(ins) + list(outs[1:]) + list(scratch[: self.own_scratch])
         scratch = scratch[self.own_scratch :]
         self.part, self.mine = scratch[:2]
         self.from_a, self.from_b, self.from_x, self.from_y = scratch[2:6]
@@ -512,10 +527,14 @@
     def begin(self):
         if self.prepare is not None:
             self.prepare(self.refs)
-        self.make(*self.steps[0])
+        if self.prelude is None:
+            self.make(*self.steps[0])
 
     def middle(self):
         steps, calls = self.steps, []
+        if self.prelude is not None:
+            calls += self.prelude(self.refs)
+            calls.append(lambda: self.make(*steps[0]))
         for i in range(len(steps) + 2):
 
             def call(i=i):
@@ -1015,7 +1034,7 @@
 
 
 def fits(groups, heads, block, width):
-    return groups % heads == 0 and heads % 4 == 0 and block % 64 == 0 and 4 * groups * block * width <= 24 << 20
+    return groups % heads == 0 and heads % 4 == 0 and block % 64 == 0 and width == groups * LANES and 4 * groups * block * width <= 24 << 20
 
 
 def masked_scores(query_rows, key_rows):
@@ -1026,7 +1045,8 @@
 
 def to_blocks(grad_rows, groups):
     rows, width = grad_rows.shape
-    return grad_rows.reshape(rows, groups, width // groups).transpose(1, 0, 2).astype(jnp.bfloat16)
+    kept = lax.optimization_barrier(grad_rows.astype(jnp.bfloat16))
+    return kept.reshape(rows, groups, width // groups).transpose(1, 0, 2)
 
 
 def from_blocks(blocks):
@@ -1069,12 +1089,13 @@
     hidden = shared_gate.shape[1] // groups
     bf16 = jnp.bfloat16
 
-    kv_block = lat_rows * (DN + DV) // own_cols
+    kv_halves = (DN + DV) // own_cols
+    kv_block = lat_rows * kv_halves
     head_parts = jnp.concatenate(
         [
             q_weight.reshape(own_cols, heads, DQK).transpose(1, 2, 0),
-            kvb_weight.reshape(lat_rows, heads, DN + DV)
-            .transpose(1, 0, 2)
+            kvb_weight.reshape(lat_rows, heads, kv_halves, own_cols)
+            .transpose(1, 2, 0, 3)
             .reshape(heads, kv_block, own_cols),
             o_weight.reshape(heads, DV, own_cols),
         ],
@@ -1103,18 +1124,22 @@
     at_gate = at_o + DV
     planes, all_planes = heads // 4, groups // 4
     small_swap = Swap(jnp.broadcast_to(small[None], (groups,) + small.shape), True)
-    (small_all,), (got,), (latent_w,), (normed1_all,) = exchange(
+    (small_all,), (latent_w,), (got,), (normed1_all,) = exchange(
         [
             small_swap,
+            Gather([kva_weight], all_planes),
             Swap(jnp.tile(head_parts, (copies, 1, 1))),
-            Gather([kva_weight], all_planes),
             NormGather(layer_in, small_swap, groups, planes),
         ],
         1,
     )
     query_wt = from_blocks(got[:, :at_kv])
-    kvup_w = got[:, at_kv:at_o].reshape(lat_width, DN + DV)
-    output_w = from_blocks(got[:, at_o:at_gate])
+    kvup_w = (
+        got[:, at_kv:at_o]
+        .reshape(groups, kv_halves, lat_rows, own_cols)
+        .transpose(0, 2, 1, 3)
+        .reshape(lat_width, DN + DV)
+    )
     route_wt = from_blocks(small_all[:, :groups])
     gain_one = small_all[:, groups].reshape(width).astype(jnp.float32)
     gain_two = small_all[:, groups + 1].reshape(width).astype(jnp.float32)
@@ -1122,43 +1147,111 @@
     latent_w = latent_w.reshape(width, kva_weight.shape[1])
     stat_one = rms_scale(layer_in)
     unit_one = layer_in * stat_one
-    normed1_all = normed1_all.reshape(heads * seq_len, width)
 
     cosine, sine_part = rope_tables(seq_len, DR)
+    turn_cos = jnp.concatenate([cosine, cosine], axis=-1)
+    turn_sin = jnp.concatenate([-sine_part, sine_part], axis=-1)
     by_seq = (heads, seq_len, -1)
-    query_full = fsum("td,qd->tq", normed1_all, query_wt).reshape(by_seq)
-    query_rows = jnp.concatenate(
-        [query_full[..., :DN], rotate(query_full[..., DN:], cosine, sine_part)], axis=-1
-    ).astype(bf16)
-    latent_full = fdot(normed1_all, latent_w)
-    latent_stat = rms_scale(latent_full[:, :lat_width])
-    latent_unit = latent_full[:, :lat_width] * latent_stat
-    latent = (latent_unit * gain_kv).astype(bf16)
-    rot_key = rotate(latent_full[:, lat_width:].reshape(by_seq), cosine, sine_part).astype(bf16)
-    key_value = fdot(latent, kvup_w).astype(bf16).reshape(by_seq)
-    key_rows = jnp.concatenate([key_value[..., :DN], rot_key], axis=-1)
-    value_rows = key_value[..., DN:]
-    scores = masked_scores(query_rows, key_rows)
-    row_max = jnp.max(scores, axis=-1, keepdims=True)
-    log_totals = row_max + jnp.log(jnp.sum(jnp.exp(scores - row_max), axis=-1, keepdims=True))
-    att_probs = jnp.exp(scores - log_totals)
-    att_weights = att_probs.astype(bf16)
-    mixed = fsum("sqk,skd->sqd", att_weights, value_rows).astype(bf16)
-    mixed_flat = mixed.reshape(heads * seq_len, DV)
+    fold = 2
+
+    def attend_forward(refs):
+        rows_in, parts, lat_w, kv_gain_ref, cos_ref, sin_ref = refs[:6]
+        query_out, key_out, value_out, prob_out, lat_out, latent_out, mixed_out, out_w = refs[6:14]
+        query_w, kv_w = refs[14:]
+
+        def assemble():
+            for j in range(groups):
+                at = slice(j * own_cols, (j + 1) * own_cols)
+                query_w[:, at] = parts[j, :at_kv]
+                out_w[:, at] = parts[j, at_o:at_gate]
+                down = slice(j * lat_rows, (j + 1) * lat_rows)
+                for half in range(kv_halves):
+                    start = at_kv + half * lat_rows
+                    across = slice(half * own_cols, (half + 1) * own_cols)
+                    kv_w[down, across] = parts[j, start : start + lat_rows]
+
+        def rotated(block):
+            flipped = jnp.concatenate([block[:, DR // 2 :], block[:, : DR // 2]], axis=-1)
+            cos_rows = jnp.concatenate([cos_ref[...]] * fold, axis=0)
+            sin_rows = jnp.concatenate([sin_ref[...]] * fold, axis=0)
+            return (block * cos_rows + flipped * sin_rows).astype(bf16)
+
+        def some(first):
+            rows = rows_in[first : first + fold].reshape(fold * seq_len, width)
+            query = dot_nt(rows, query_w[...])
+            query_plain, query_turn = query[:, :DN].astype(bf16), rotated(query[:, DN:])
+            full = fdot(rows, lat_w[...])
+            plain = full[:, :lat_width]
+            latent = (plain * rms_scale(plain) * kv_gain_ref[...]).astype(bf16)
+            key_turn = rotated(full[:, lat_width:])
+            key_value = fdot(latent, kv_w[...]).astype(bf16)
+            latent_out[first : first + fold] = latent.reshape(fold, seq_len, lat_width)
+            lat_out[first : first + fold] = plain.reshape(fold, seq_len, lat_width)
+            ahead = lax.broadcasted_iota(jnp.int32, (seq_len, seq_len), 1) > lax.broadcasted_iota(
+                jnp.int32, (seq_len, seq_len), 0
+            )
+            for k in range(fold):
+                at, seq = slice(k * seq_len, (k + 1) * seq_len), first + k
+                scores = dot_nt(query_plain[at], key_value[at, :DN])
+                scores += dot_nt(query_turn[at], key_turn[at])
+                scores = jnp.where(ahead, -1e30, scores * DQK ** (-0.5))
+                row_max = jnp.max(scores, axis=-1, keepdims=True)
+                total = jnp.sum(jnp.exp(scores - row_max), axis=-1, keepdims=True)
+                probs = jnp.exp(scores - (row_max + jnp.log(total)))
+                values = key_value[at, DN:]
+                prob_out[seq] = probs
+                mixed_out[seq] = fdot(probs.astype(bf16), values).astype(bf16)
+                query_out[seq, :, :DN], query_out[seq, :, DN:] = query_plain[at], query_turn[at]
+                key_out[seq, :, :DN], key_out[seq, :, DN:] = key_value[at, :DN], key_turn[at]
+                value_out[seq] = values
+
+        steps = [functools.partial(some, first) for first in range(0, heads, fold)]
+        return [assemble] + steps
+
     out_rows = out_grad.astype(bf16)
 
     def attn_part(part, slot, refs):
-        product = fdot(refs[0][slot], refs[1][...])
-        part[slot] = product.astype(bf16)
-
-    (shared_got,), (out_all,), (attn_sum,) = exchange(
+        for col in range(0, width, 512):
+            product = fdot(refs[12][slot], refs[13][:, col : col + 512])
+            part[slot, :, col : col + 512] = product.astype(bf16)
+
+    def shaped(last, kind):
+        return jax.ShapeDtypeStruct((heads, seq_len, last), kind)
+
+    (out_all,), (shared_got,), attended = exchange(
         [
+            Gather([out_rows], all_planes),
             Swap(shared_parts),
-            Gather([out_rows], all_planes),
-            Reduce([mixed, output_w], attn_part, heads, seq_len, width),
+            Reduce(
+                [normed1_all, got, latent_w, gain_kv[None, :], turn_cos, turn_sin],
+                attn_part,
+                heads,
+                seq_len,
+                width,
+                [pltpu.VMEM((DQK, width), bf16), pltpu.VMEM((lat_width, DN + DV), bf16)],
+                extra=[
+                    shaped(DQK, bf16),
+                    shaped(DQK, bf16),
+                    shaped(DV, bf16),
+                    shaped(seq_len, jnp.float32),
+                    shaped(lat_width, jnp.float32),
+                    shaped(lat_width, bf16),
+                    shaped(DV, bf16),
+                    jax.ShapeDtypeStruct((DV, width), bf16),
+                ],
+                prelude=attend_forward,
+            ),
         ],
         2,
     )
+    attn_sum, query_rows, key_rows, value_rows, att_probs, lat_plain, latent, mixed, output_w = (
+        attended
+    )
+    att_weights = att_probs.astype(bf16)
+    mixed_flat = mixed.reshape(heads * seq_len, DV)
+    normed1_all = normed1_all.reshape(heads * seq_len, width)
+    latent = latent.reshape(heads * seq_len, lat_width)
+
     gate_sht = from_blocks(shared_got[:, :hidden])
     up_sht = from_blocks(shared_got[:, hidden : 2 * hidden])
     down_sh = from_blocks(shared_got[:, 2 * hidden :])
@@ -1316,9 +1409,8 @@
         part[slot, :, width : width + lat_width] = product.astype(bf16)
         part[slot, :, width + lat_width :] = refs[4][slot]
 
-    (owned_early,), (back,) = exchange(
+    (back,), (owned_early,) = exchange(
         [
-            Swap(jnp.concatenate([shared_grads, to_blocks(o_grad, groups)], axis=1)),
             Reduce(
                 [
                     query_delta,
@@ -1332,6 +1424,7 @@
                 seq_len,
                 width + lat_width + LANES,
             ),
+            Swap(jnp.concatenate([shared_grads, to_blocks(o_grad, groups)], axis=1), pace=3),
         ],
         6,
     )
@@ -1339,10 +1432,9 @@
     latent_grad = back[:, width : width + lat_width]
     rot_sum = back[:, width + lat_width : width + lat_width + DR]
 
-    def own_rows(rows):
-        return lax.dynamic_slice_in_dim(rows, head * seq_len, seq_len, 0)
-
-    own_unit, own_stat = own_rows(latent_unit), own_rows(latent_stat)
+    own_plain = lax.dynamic_index_in_dim(lat_plain, head, 0, keepdims=False)
+    own_stat = rms_scale(own_plain)
+    own_unit = own_plain * own_stat
     kv_gain_grad = jnp.sum(latent_grad * own_unit, axis=0)
     scaled_lat = latent_grad * gain_kv
     latent_back = own_stat * (
@@ -1354,20 +1446,15 @@
     query_delta_t = lax.optimization_barrier(query_delta.reshape(heads * seq_len, DQK).T)
     kv_flat = kv_delta.reshape(heads * seq_len, DN + DV)
     latent_t = lax.optimization_barrier(latent.T)
-    (owned_heads,), (latent_delta_all,) = exchange(
-        [
-            Swap(
-                jnp.concatenate(
-                    [
-                        to_blocks(fdot(query_delta_t, normed1_all), groups),
-                        fdot(latent_t, kv_flat).astype(bf16).reshape(groups, kv_block, own_cols),
-                    ],
-                    axis=1,
-                )
-            ),
-            Gather([latent_delta], planes),
-        ],
-        7,
+    kvb_blocks = (
+        lax.optimization_barrier(fdot(latent_t, kv_flat).astype(bf16))
+        .reshape(groups, lat_rows, kv_halves, own_cols)
+        .transpose(0, 2, 1, 3)
+        .reshape(groups, kv_block, own_cols)
+    )
+    head_grads = jnp.concatenate([to_blocks(fdot(query_delta_t, normed1_all), groups), kvb_blocks], 1)
+    (latent_delta_all,), (owned_heads,) = exchange(
+        [Gather([latent_delta], planes), Swap(head_grads, pace=4)], 7
     )
     latent_delta_all = latent_delta_all.reshape(heads * seq_len, -1)
     normed1_grad = normed1_query + fsum("tl,dl->td", latent_delta, latent_w)
@@ -1406,8 +1493,8 @@
     q_grad = of_heads[:, :at_kv].transpose(2, 0, 1).reshape(own_cols, heads * DQK)
     kvb_grad = (
         of_heads[:, at_kv:]
-        .reshape(heads, lat_rows, DN + DV)
-        .transpose(1, 0, 2)
+        .reshape(heads, kv_halves, lat_rows, own_cols)
+        .transpose(2, 0, 1, 3)
         .reshape(lat_rows, heads * (DN + DV))
     )
     own_o_grad = over_copies(owned_early[:, 3 * hidden :]).reshape(heads * DV, own_cols)

time: 737 us -> 647 us (0.88)
  local copies, waits for them, and re-layouts: 110 us -> 47.5 us
  matrix products: 117 us -> 101 us
    dot_general x4 -> x0, local copies, waits for them, and re-layouts: 37.3 us -> none  [fdot(): return jnp.dot(left, right, preferred_element_type=jnp.float32)]
    unnamed x154 -> x135, local copies, waits for them, and re-layouts: 26 us -> 14.8 us
    dot_general x13 -> x11, matrix products: 50.4 us -> 40.7 us  [fdot(): return jnp.dot(left, right, preferred_element_type=jnp.float32)]
    pallas_call x8, Pallas kernels: 445 us -> 438 us  [exchange(): pl.pallas_call(functools.partial(chip_kernel, ops), out_shape=[shape for...]
    dot_general x22 -> x19, matrix products: 66.9 us -> 60.6 us  [fsum(): return jnp.einsum(spec, left, right, preferred_element_type=jnp.float32)]
where the time goes in v2:
time: 647 us; the launch traced here: 636 us
  Pallas kernels  438 us (68%)
  matrix products  101 us (16%)
  local copies, waits for them, and re-layouts  47.5 us (7%)
  other arithmetic  47.5 us (7%)
    pallas_call x8, Pallas kernels, exchange(): pl.pallas_call(functools.partial(chip_kernel, ops), out_shape=[shape for...  438 us
    dot_general x19, matrix products, fsum(): return jnp.einsum(spec, left, right, preferred_element_type=jnp.float32)  60.6 us
    dot_general x11, matrix products, fdot(): return jnp.dot(left, right, preferred_element_type=jnp.float32)  40.7 us
    unnamed x135, local copies, waits for them, and re-layouts  14.8 us

profile of v2, /device:TPU:0, one launch (start us, length us, event | category | flops | bytes accessed | tf_op | source)
XLA Modules:
  0.0 636.4 jit_solution(2980477258212315206)
XLA Ops:
  19.2 61.4 %shard_map.288 = (bf16[16,32,128]{2,1,0:T(8,128)(2,1)}, bf16[16,128,576]{2,1,0:T(8,128)(2,1)}, bf16[16,384,128]{2,1,0:T(8,128)(2,1)}, bf16[8,128,2048]{2,1,0:T(8,128)(2,1)}) custom-call(bf16[16,32,128]{2,1,0:T(8,128)(2,1)} %broadcast_in_dim.21.refs_0_, bf16[128,576]{1,0:T(8,128)(2,1)} %copy.177.refs_1_, bf16[16,384,128]{2,1,0:T(8,128)(2,1)} %bitcast.296, ...), custom_call_target="tpu_custom_call" | custom-call | bytes 11157504 | tf_op jit(solution)/shard_map/pallas_call | solution.py:630
  88.5 98.2 %shard_map.289 = (bf16[16,128,2048]{2,1,0:T(8,128)(2,1)}, bf16[16,264,128]{2,1,0:T(8,128)(2,1)}, f32[128,2048]{1,0:T(8,128)}, bf16[8,128,192]{2,1,0:T(8,128)(2,1...) custom-call(bf16[128,2048]{1,0:T(8,128)(2,1)} %convert_element_type., ...), custom_call_target="tpu_custom_call" | custom-call | bytes 25823232 | tf_op jit(solution)/shard_map/pallas_call | solution.py:630
  197.9 6.9 %fusion.68 = f32[88,2048]{1,0:T(8,128)} fusion(bf16[2048,2048]{1,0:T(8,128)(2,1)} %bitcast.281, bf16[16,11,8,128]{3,2,1,0:T(8,128)(2,1)S(1)} %get-tuple-element.152), kind=kOutput, calls=%fused_computation.187 | convolution fusion | flops 738197504 | bytes 9469952 | tf_op jit(solution)/shard_map/fd,td->ft/dot_general | solution.py:65
  206.0 52.1 %shard_map.290 = (bf16[16,128,2048]{2,1,0:T(8,128)(2,1)}, f32[16,128,128]{2,1,0:T(8,128)}) custom-call(bf16[128,2048]{1,0:T(8,128)(2,1)} %copy-done.12, f32[128,128]{1,0:T(8,128)} %pad.54.refs_1_), custom_call_target="tpu_custom_call" | custom-call | bytes 10027008 | tf_op jit(solution)/shard_map/pallas_call | solution.py:630
  260.4 6.2 fusion.69
  279.7 14.5 %fusion.12 = f32[1024,704]{0,1:T(8,128)S(1)} fusion(bf16[1024,2048]{1,0:T(8,128)(2,1)S(1)} %bitcast.290, bf16[1,2048,704]{1,2,0:T(8,128)(2,1)S(1)} %copy-done.52), kind=kOutput, calls=%fused_computation.22 | convolution fusion | flops 2952790016 | bytes 9961472 | tf_op jit(solution)/shard_map/dot_general | solution.py:55
  294.3 4.9 multiply_convert_fusion.3
  300.5 5.7 fusion.2
  308.0 4.0 multiply_convert_fusion
  315.0 4.5 fusion.3
  319.5 5.9 multiply_convert_fusion.1
  325.4 5.0 convolution_bitcast_fusion.2
  330.4 4.9 convolution_bitcast_fusion
  335.3 5.3 convolution_bitcast_fusion.1
  340.6 3.5 fusion.10
  344.2 5.4 add_convert_fusion
  349.6 95.0 %shard_map.291 = f32[128,4224]{1,0:T(8,128)} custom-call(bf16[16,160,128]{2,1,0:T(8,128)(2,1)} %pad_maximum_fusion.5.refs_0_, bf16[16,256,128]{2,1,0:T(8,128)(2,1)} %pad_maximum_fusion.2.refs_1_, bf16[16,64,2048]{2,1,0:T(8,128)(2,1)} %bitcast.289, bf16[16,64,2048]{2,1,0:T(8,128)(2,1)} %bitcast.297, bf16[96,2048]{1,0:T(8,128)(2,1)} %pad.58.refs_4_, ...), custom_call_target="tpu_custom_call" | custom-call | bytes 13959168 | tf_op jit(solution)/shard_map/pallas_call | solution.py:630
  453.1 26.8 %shard_map.292 = bf16[8,128,2048]{2,1,0:T(8,128)(2,1)} custom-call(bf16[128,2048]{1,0:T(8,128)(2,1)} %get-tuple-element.134.refs_0_), custom_call_target="tpu_custom_call" | custom-call | bytes 4718592 | tf_op jit(solution)/shard_map/pallas_call | solution.py:630
  480.0 3.6 convolution_convert_fusion.10
  494.1 3.2 convolution_convert_fusion.2
  500.5 55.3 %shard_map.293 = (f32[128,2688]{1,0:T(8,128)}, bf16[16,392,128]{2,1,0:T(8,128)(2,1)}) custom-call(bf16[8,128,192]{2,1,0:T(8,128)(2,1)} %pad_maximum_fusion.6.refs_0_, bf16[192,2048]{1,0:T(8,128)(2,1)} %copy_bitcast_fusion.refs_1_, bf16[8,128,256]{2,1,0:T(8,128)(2,1)} %pad_maximum_fusion.7.refs_2_, bf16[256,512]{1,0:T(8,128)(2,1)} %bitcast.324, ...), custom_call_target="tpu_custom_call" | custom-call | bytes 6815744 | tf_op jit(solution)/shard_map/pallas_call | solution.py:630
  559.7 3.2 multiply_reduce_fusion.1
  570.6 29.5 %shard_map.294 = (bf16[8,128,576]{2,1,0:T(8,128)(2,1)}, bf16[16,256,128]{2,1,0:T(8,128)(2,1)}) custom-call(bf16[128,576]{1,0:T(8,128)(2,1)} %copy-done.20, bf16[16,256,128]{2,1,0:T(8,128)(2,1)} %pad_maximum_fusion.3.refs_1_), custom_call_target="tpu_custom_call" | custom-call | bytes 3424256 | tf_op jit(solution)/shard_map/pallas_call | solution.py:630
  606.4 19.5 %shard_map.295 = (bf16[16,80,128]{2,1,0:T(8,128)(2,1)}, f32[16,24,128]{2,1,0:T(8,128)}) custom-call(bf16[16,80,128]{2,1,0:T(8,128)(2,1)} %pad.63.refs_0_, f32[16,24,128]{2,1,0:T(8,128)} %pad.65.refs_1_), custom_call_target="tpu_custom_call" | custom-call | bytes 1048576 | tf_op jit(solution)/shard_map/pallas_call | solution.py:630
  (259 shorter events, 109.5 us)
Async XLA Ops:
  0.6 299.8 %copy-start = (bf16[1,704,2048]{2,1,0:T(8,128)(2,1)S(1)}, bf16[1,704,2048]{2,1,0:T(8,128)(2,1)}, u32[]{:S(2)}) copy-start(bf16[1,704,2048]{2,1,0:T(8,128)(2,1)} %param.31) | copy-start | bytes 8650756
  1.2 7.0 %copy-start.43 = (f32[128]{0:T(128)}, f32[128]{0:T(128)S(1)}, u32[]{:S(2)}) copy-start(f32[128]{0:T(128)S(1)} %iota_convert_fusion) | copy-start | bytes 1540
  88.5 100.0 %copy-start.6 = (f32[128,2048]{1,0:T(8,128)S(1)}, f32[128,2048]{1,0:T(8,128)}, u32[]{:S(2)}) copy-start(f32[128,2048]{1,0:T(8,128)} %refs_3_.1) | copy-start | bytes 3145732
  191.1 13.7 %copy-start.12 = (bf16[128,2048]{1,0:T(8,128)(2,1)}, bf16[128,2048]{1,0:T(8,128)(2,1)S(1)}, u32[]{:S(2)}) copy-start(bf16[128,2048]{1,0:T(8,128)(2,1)S(1)} %multiply_convert_fusion.5.refs_0_) | copy-start | bytes 1572868
  196.9 7.9 %copy-start.17 = (bf16[16,11,8,128]{3,2,1,0:T(8,128)(2,1)}, bf16[16,11,8,128]{3,2,1,0:T(8,128)(2,1)S(1)}, u32[]{:S(2)}) copy-start(bf16[16,11,8,128]{3,2,1,0:T(8,128)(2,1)S(1)} %get-tuple-element.153) | copy-start | bytes 1081348
  196.9 8.0 %copy-start.23 = (bf16[16,11,8,128]{3,2,1,0:T(8,128)(2,1)}, bf16[16,11,8,128]{3,2,1,0:T(8,128)(2,1)S(1)}, u32[]{:S(2)}) copy-start(bf16[16,11,8,128]{3,2,1,0:T(8,128)(2,1)S(1)} %get-tuple-element.154) | copy-start | bytes 1081348
  204.9 55.5 %copy-start.18 = (bf16[16,11,8,128]{3,2,1,0:T(8,128)(2,1)S(1)}, bf16[16,11,8,128]{3,2,1,0:T(8,128)(2,1)}, u32[]{:S(2)}) copy-start(bf16[16,11,8,128]{3,2,1,0:T(8,128)(2,1)} %copy-done.17) | copy-start | bytes 1081348
  279.1 15.1 %copy-start.8 = (bf16[16,64,2048]{2,1,0:T(8,128)(2,1)}, bf16[16,64,2048]{2,1,0:T(8,128)(2,1)S(1)}, u32[]{:S(2)}) copy-start(bf16[16,64,2048]{2,1,0:T(8,128)(2,1)S(1)} %convolution_convert_fusion.1) | copy-start | bytes 12582916
  279.7 14.6 %copy-start.54 = (bf16[1,2048,704]{1,2,0:T(8,128)(2,1)S(1)}, bf16[1,2048,704]{1,2,0:T(8,128)(2,1)}, u32[]{:S(2)}) copy-start(bf16[1,2048,704]{1,2,0:T(8,128)(2,1)} %param.30) | copy-start | bytes 8650756
  349.6 95.0 %copy-start.39 = (f32[128]{0:T(128)S(1)}, f32[128]{0:T(128)}, u32[]{:S(2)}) copy-start(f32[128]{0:T(128)} %get-tuple-element.166) | copy-start | bytes 1540
  349.6 95.0 %copy-start.42 = (f32[128]{0:T(128)S(1)}, f32[128]{0:T(128)}, u32[]{:S(2)}) copy-start(f32[128]{0:T(128)} %copy-done.41) | copy-start | bytes 1540
  349.6 96.2 %copy-start.13 = (bf16[128,2048]{1,0:T(8,128)(2,1)S(1)}, bf16[128,2048]{1,0:T(8,128)(2,1)}, u32[]{:S(2)}) copy-start(bf16[128,2048]{1,0:T(8,128)(2,1)} %copy-done.12) | copy-start | bytes 1572868
  349.6 98.0 %copy-start.11 = (f32[128,2048]{1,0:T(8,128)S(1)}, f32[128,2048]{1,0:T(8,128)}, u32[]{:S(2)}) copy-start(f32[128,2048]{1,0:T(8,128)} %copy-done.10) | copy-start | bytes 3145732
  349.6 98.0 %copy-start.37 = (bf16[16,32,128]{2,1,0:T(8,128)(2,1)S(1)}, bf16[16,32,128]{2,1,0:T(8,128)(2,1)}, u32[]{:S(2)}) copy-start(bf16[16,32,128]{2,1,0:T(8,128)(2,1)} %get-tuple-element.42) | copy-start | bytes 393220
  349.6 98.0 %copy-start.49 = (f32[128]{0:T(128)S(1)}, f32[128]{0:T(128)}, u32[]{:S(2)}) copy-start(f32[128]{0:T(128)} %copy-done.48) | copy-start | bytes 1540
  453.1 26.8 %copy-start.56 = (bf16[128,2048]{1,0:T(8,128)(2,1)S(1)}, bf16[128,2048]{1,0:T(8,128)(2,1)}, u32[]{:S(2)}) copy-start(bf16[128,2048]{1,0:T(8,128)(2,1)} %get-tuple-element.49) | copy-start | bytes 1572868
  498.6 57.1 %copy-start.38 = (f32[512]{0:T(512)S(1)}, f32[512]{0:T(512)}, u32[]{:S(2)}) copy-start(f32[512]{0:T(512)} %reshape.442) | copy-start | bytes 6148
  498.6 57.1 %copy-start.50 = (f32[128]{0:T(128)S(1)}, f32[128]{0:T(128)}, u32[]{:S(2)}) copy-start(f32[128]{0:T(128)} %add_rsqrt_fusion) | copy-start | bytes 1540
  499.6 58.7 %copy-start.44 = (f32[128]{0:T(128)S(1)}, f32[128]{0:T(128)}, u32[]{:S(2)}) copy-start(f32[128]{0:T(128)} %copy-done.43) | copy-start | bytes 1540
  499.6 58.7 %copy-start.46 = (f32[32]{0:T(128)S(1)}, f32[32]{0:T(128)}, u32[]{:S(2)}) copy-start(f32[32]{0:T(128)} %copy-done.45) | copy-start | bytes 388
  500.5 59.1 %copy-start.7 = (f32[128,2048]{1,0:T(8,128)S(1)}, f32[128,2048]{1,0:T(8,128)}, u32[]{:S(2)}) copy-start(f32[128,2048]{1,0:T(8,128)} %refs_3_.1) | copy-start | bytes 3145732
  500.5 59.2 %copy-start.47 = (f32[128]{0:T(128)S(1)}, f32[128]{0:T(128)}, u32[]{:S(2)}) copy-start(f32[128]{0:T(128)} %add_rsqrt_fusion.1) | copy-start | bytes 1540
  606.4 28.4 %slice-start.2 = ((f32[8,256,128]{2,1,0:T(8,128)}), f32[8,64,128]{2,1,0:T(8,128)S(1)}, s32[]{:S(2)}) async-start(f32[8,256,128]{2,1,0:T(8,128)} %convert_reduce_fusion), calls=%async_computation.2 | async-start | bytes 524288 | tf_op jit(solution)/shard_map/slice | solution.py:1495
  626.9 9.1 %copy-start.1 = (bf16[1,704,2048]{2,1,0:T(8,128)(2,1)S(1)}, bf16[1,704,2048]{2,1,0:T(8,128)(2,1)}, u32[]{:S(2)}) copy-start(bf16[1,704,2048]{2,1,0:T(8,128)(2,1)} %param.31) | copy-start | bytes 8650756
  (40 other events, 144.8 us)

commit v3 on v2

--- a/solution.py
+++ b/solution.py
@@ -61,6 +61,12 @@
     )
 
 
+def dot_tn(left, right):
+    return lax.dot_general(
+        left, right, (((0,), (0,)), ((), ())), preferred_element_type=jnp.float32
+    )
+
+
 def fsum(spec, left, right):
     return jnp.einsum(spec, left, right, preferred_element_type=jnp.float32)
 
@@ -68,13 +74,6 @@
 EXPERT, TENSOR = "expert", "tensor"
 MESH = pl.DeviceIdType.MESH
 DMA = pltpu.SemaphoreType.DMA
-
-
-def guarded(cond, body):
-    if cond is None:
-        body()
-    else:
-        pl.when(cond)(body)
 
 
 def remote(src, dst, send, recv, target):
@@ -107,13 +106,13 @@
         return lax.rem(self.chip + j, self.groups)
 
 
-def level_steps(level, planes, far_first):
-    order = [(0, 0)] + [(d, s) for d in range(1, planes) for s in (-1, 1)]
-    steps = []
-    for distance, side in order[::-1] if far_first else order:
-        lev = level + side * distance
-        steps.append((lev, side, None if distance == 0 else ((lev >= 0) & (lev < planes))))
-    return steps
+def level_at(level, planes, t):
+    if planes < 4:
+        return lax.rem(level + t, planes)
+    flip = level // 2
+    near = lax.rem(level + flip, 2)
+    order = t + near * (1 - 2 * t) if t < 2 else t
+    return order * (1 - 2 * flip) + 3 * flip
 
 
 class Swap:
@@ -169,11 +168,12 @@
 
 
 class Gather:
-    def __init__(self, arrays, planes):
+    def __init__(self, arrays, planes, vmem_result=False):
         count, slots = len(arrays), planes * 4
         self.planes, self.count, self.reach = planes, count, planes
         self.ins = [(a, pltpu.VMEM) for a in arrays]
-        self.outs = [(jax.ShapeDtypeStruct((slots,) + a.shape, a.dtype), pl.ANY) for a in arrays]
+        space = pltpu.VMEM if vmem_result else pl.ANY
+        self.outs = [(jax.ShapeDtypeStruct((slots,) + a.shape, a.dtype), space) for a in arrays]
         by_level, by_slot = DMA((count, planes)), DMA((count, slots))
         self.scratch = [DMA((count,))] + [by_level] * 5 + [by_slot] + [by_level] * 6 + [by_slot]
 
@@ -185,7 +185,7 @@
         self.in_z, self.in_x, self.in_y, self.in_a, self.in_b, self.in_p = scratch[1:7]
         self.out_up, self.out_down, self.out_x, self.out_y = scratch[7:11]
         self.out_a, self.out_b, self.out_p = scratch[11:14]
-        self.steps = level_steps(self.level, self.planes, False)
+        self.landed = False
 
     def move(self, a, slot, part, send, recv, target, own=False, whose=None):
         half = self.sources[a].shape[0] // 2
@@ -235,96 +235,90 @@
     def begin(self):
         for a in range(self.count):
             self.own(a).start()
-        self.first(*self.steps[0])
-
-    def first(self, lev, side, cond):
-        def body():
-            for a in range(self.count):
-                own, slot = side == 0, lev * 4 + self.place.here
-                if side != 0:
-                    self.along_z(a, lev, own, True).wait_recv()
-                if side <= 0:
-                    pl.when(self.has_up)(lambda a=a: self.along_z(a, lev, own, True).start())
-                if side >= 0:
-                    pl.when(self.has_down)(lambda a=a: self.along_z(a, lev, own, False).start())
-                self.along_x(a, lev, slot, own).start()
-                self.along_y(a, lev, slot, own).start()
-                if side != 0:
-                    self.share(a, slot).start()
-
-        guarded(cond, body)
-
-    def second(self, lev, side, cond):
-        def body():
-            for a in range(self.count):
-                slot = lev * 4 + self.place.there_y
-                self.along_y(a, lev, slot).wait_recv()
-                self.corner_x(a, lev, slot).start()
+        self.first(0)
+
+    def relays(self, a, t, act):
+        lev = level_at(self.level, self.planes, t)
+        up, down = self.has_up, self.has_down
+        if t > 0:
+            up, down = up & (lev < self.level), down & (lev > self.level)
+        pl.when(up)(lambda: act(self.along_z(a, lev, t == 0, True)))
+        pl.when(down)(lambda: act(self.along_z(a, lev, t == 0, False)))
+
+    def first(self, t):
+        lev = level_at(self.level, self.planes, t)
+        for a in range(self.count):
+            own, slot = t == 0, lev * 4 + self.place.here
+            if not own:
+                self.along_z(a, lev, own, True).wait_recv()
+            self.relays(a, t, lambda copy: copy.start())
+            self.along_x(a, lev, slot, own).start()
+            self.along_y(a, lev, slot, own).start()
+            if not own:
                 self.share(a, slot).start()
-                slot = lev * 4 + self.place.there_x
-                self.along_x(a, lev, slot).wait_recv()
-                self.corner_y(a, lev, slot).start()
-                self.share(a, slot).start()
-
-        guarded(cond, body)
-
-    def third(self, lev, side, cond):
-        def body():
-            for a in range(self.count):
-                slot = lev * 4 + self.place.across
-                self.corner_x(a, lev, slot).wait_recv()
-                self.corner_y(a, lev, slot).wait_recv()
-                self.share(a, slot).start()
-
-        guarded(cond, body)
+
+    def second(self, t):
+        lev = level_at(self.level, self.planes, t)
+        for a in range(self.count):
+            slot = lev * 4 + self.place.there_y
+            self.along_y(a, lev, slot).wait_recv()
+            self.corner_x(a, lev, slot).start()
+            self.share(a, slot).start()
+            slot = lev * 4 + self.place.there_x
+            self.along_x(a, lev, slot).wait_recv()
+            self.corner_y(a, lev, slot).start()
+            self.share(a, slot).start()
+
+    def third(self, t):
+        lev = level_at(self.level, self.planes, t)
+        for a in range(self.count):
+            slot = lev * 4 + self.place.across
+            self.corner_x(a, lev, slot).wait_recv()
+            self.corner_y(a, lev, slot).wait_recv()
+            self.share(a, slot).start()
+
+    def advance(self, i):
+        if i < self.planes:
+            self.first(i)
+        if 0 <= i - 1 < self.planes:
+            self.second(i - 1)
+        if 0 <= i - 2 < self.planes:
+            self.third(i - 2)
 
     def middle(self):
-        steps, calls = self.steps, []
-        for i in range(1, len(steps) + 2):
-
-            def call(i=i):
-                if i < len(steps):
-                    self.first(*steps[i])
-                if 0 <= i - 1 < len(steps):
-                    self.second(*steps[i - 1])
-                if 0 <= i - 2 < len(steps):
-                    self.third(*steps[i - 2])
-
-            calls.append(call)
-        return calls
+        return [functools.partial(self.advance, i) for i in range(1, self.planes + 2)]
 
     def end(self):
         place = self.place
-
-        def finish(lev, side, cond):
-            def body():
-                for a in range(self.count):
-                    own, slot = side == 0, lev * 4 + place.here
-                    if side <= 0:
-                        pl.when(self.has_up)(
-                            lambda a=a: self.along_z(a, lev, own, True).wait_send()
-                        )
-                    if side >= 0:
-                        pl.when(self.has_down)(
-                            lambda a=a: self.along_z(a, lev, own, False).wait_send()
-                        )
-                    self.along_x(a, lev, slot, own).wait_send()
-                    self.along_y(a, lev, slot, own).wait_send()
-                    self.corner_x(a, lev, lev * 4 + place.there_y).wait_send()
-                    self.corner_y(a, lev, lev * 4 + place.there_x).wait_send()
-                    spots = [] if side == 0 else [slot]
-                    for other in (place.there_y, place.there_x, place.across):
-                        spots.append(lev * 4 + other)
-                    for spot in spots:
-                        self.share(a, spot).wait_send()
-                        self.share(a, spot, 1 - place.core).wait_recv()
-
-            guarded(cond, body)
-
-        for step in self.steps:
-            finish(*step)
+        if not self.landed:
+            for t in range(self.planes):
+                self.receive(t)
+        for t in range(self.planes):
+            lev = level_at(self.level, self.planes, t)
+            for a in range(self.count):
+                own, slot = t == 0, lev * 4 + place.here
+                self.relays(a, t, lambda copy: copy.wait_send())
+                self.along_x(a, lev, slot, own).wait_send()
+                self.along_y(a, lev, slot, own).wait_send()
+                self.corner_x(a, lev, lev * 4 + place.there_y).wait_send()
+                self.corner_y(a, lev, lev * 4 + place.there_x).wait_send()
+                for other in [place.there_y, place.there_x, place.across]:
+                    self.share(a, lev * 4 + other).wait_send()
+                if not own:
+                    self.share(a, slot).wait_send()
+
+    def ready(self, slot, other):
         for a in range(self.count):
-            self.own(a).wait()
+            if other:
+                self.share(a, slot, 1 - self.place.core).wait_recv()
+            else:
+                self.own(a).wait()
+
+    def receive(self, t):
+        place, lev = self.place, level_at(self.level, self.planes, t)
+        self.ready(lev * 4 + place.here, t > 0)
+        for spot in (place.there_y, place.there_x, place.across):
+            self.ready(lev * 4 + spot, True)
 
 
 class NormGather(Gather):
@@ -352,7 +346,7 @@
 
 class Reduce:
     def __init__(
-        self, operands, produce, slots, block, width, scratch=(), prepare=None, extra=(), prelude=None
+        self, operands, produce, slots, block, width, scratch=(), prepare=None, extra=(), prelude=None, delay=0
     ):
         planes, rows, kind = slots // 4, block // 2, jnp.bfloat16
         self.planes, self.reach = planes, planes
@@ -360,11 +354,12 @@
         self.outs = [(jax.ShapeDtypeStruct((block, width), jnp.float32), pltpu.VMEM)]
         self.outs += [(shape, pltpu.VMEM) for shape in extra]
         self.own_scratch, self.produce, self.prepare = len(scratch), produce, prepare
-        self.prelude = prelude
+        self.prelude, self.delay = prelude, delay
         by_level = DMA((planes,))
         self.scratch = (
             list(scratch)
-            + [pltpu.VMEM((slots, block, width), kind), pltpu.VMEM((slots, rows, width), kind)]
+            + [pltpu.VMEM((slots, block, width) if produce else (8, LANES), kind)]
+            + [pltpu.VMEM((slots, rows, width), kind)]
             + [pltpu.VMEM((planes, rows // 2, width), kind)] * 2
             + [pltpu.VMEM((planes, rows, width), kind)] * 4
             + [DMA((slots,))]
@@ -378,7 +373,8 @@
         self.place, self.out = place, outs[0]
         self.refs = list(ins) + list(outs[1:]) + list(scratch[: self.own_scratch])
         scratch = scratch[self.own_scratch :]
-        self.part, self.mine = scratch[:2]
+        self.part = scratch[0] if self.produce else ins[0]
+        self.mine = scratch[1]
         self.from_a, self.from_b, self.from_x, self.from_y = scratch[2:6]
         self.from_up, self.from_down = scratch[6:8]
         self.in_p, self.in_a, self.in_b, self.in_x, self.in_y = scratch[8:13]
@@ -386,7 +382,6 @@
         self.out_a, self.out_b, self.out_x, self.out_y, self.out_z, self.out_m = scratch[17:]
         self.level = lax.rem(place.chip // 4, self.planes)
         self.has_up, self.has_down = self.level < self.planes - 1, self.level > 0
-        self.steps = level_steps(self.level, self.planes, True)
         self.rows = self.part.shape[1] // 2
         self.half = self.rows // 2
 
@@ -448,14 +443,15 @@
             src, self.from_up.at[lev], self.out_z.at[lev], self.in_up.at[lev], self.place.below
         )
 
-    def make(self, lev, side, cond):
-        def body():
-            for spot in (self.place.across, self.place.there_y, self.place.there_x, self.place.here):
-                slot = lev * 4 + spot
+    def plane(self, i):
+        return level_at(self.level, self.planes, self.planes - 1 - i)
+
+    def make(self, i):
+        for spot in (self.place.across, self.place.there_y, self.place.there_x, self.place.here):
+            slot = self.plane(i) * 4 + spot
+            if self.produce is not None:
                 self.produce(self.part, slot, self.refs)
-                self.swap(slot).start()
-
-        guarded(cond, body)
+            self.swap(slot).start()
 
     def join(self, slot):
         self.swap(slot).wait_recv()
@@ -463,92 +459,73 @@
         terms = [(mine, 0), (self.part.at[slot], self.place.core * self.rows)]
         self.add_into(mine, terms, 0, self.rows)
 
-    def first(self, lev, side, cond):
-        def body():
-            self.join(lev * 4 + self.place.across)
-            self.send_a(lev).start()
-            self.send_b(lev).start()
-            self.join(lev * 4 + self.place.there_y)
-            self.join(lev * 4 + self.place.there_x)
-
-        guarded(cond, body)
-
-    def second(self, lev, side, cond):
-        def body():
-            mine = self.mine.at[lev * 4 + self.place.there_y]
-            self.send_a(lev).wait_recv()
-            self.add_into(mine, [(mine, 0), (self.from_a.at[lev], 0)], 0, self.half)
-            self.send_y(lev).start()
-            mine = self.mine.at[lev * 4 + self.place.there_x]
-            self.send_b(lev).wait_recv()
-            self.add_into(mine, [(mine, 0), (self.from_b.at[lev], -self.half)], self.half, self.half)
-            self.send_x(lev).start()
-            self.join(lev * 4 + self.place.here)
-
-        guarded(cond, body)
-
-    def third(self, lev, side, cond):
-        rows, out = self.rows, self.out
-
-        def body():
-            mine = self.mine.at[lev * 4 + self.place.here]
-            self.send_y(lev).wait_recv()
-            self.send_x(lev).wait_recv()
-            terms = [(mine, 0), (self.from_y.at[lev], 0), (self.from_x.at[lev], 0)]
-            if side == 0:
-                own = out.at[part_rows(self.place.core * rows, rows)]
-                self.add_into(own, terms, 0, rows)
-
-                @pl.when(self.has_up)
-                def _():
-                    self.send_down(lev).wait_recv()
-                    self.add_into(own, [(own, 0), (self.from_up.at[lev], 0)], 0, rows)
-
-                @pl.when(self.has_down)
-                def _():
-                    self.send_up(lev).wait_recv()
-                    self.add_into(own, [(own, 0), (self.from_down.at[lev], 0)], 0, rows)
-            else:
-                down = side < 0
-                has_more = self.has_up if down else self.has_down
-                relay = self.send_down if down else self.send_up
-                more = self.from_up if down else self.from_down
-                self.add_into(mine, terms, 0, rows)
-
-                @pl.when(has_more)
-                def _():
-                    relay(lev).wait_recv()
-                    self.add_into(mine, [(mine, 0), (more.at[lev], 0)], 0, rows)
-
-                relay(lev).start()
-
-        guarded(cond, body)
+    def first(self, i):
+        lev = self.plane(i)
+        self.join(lev * 4 + self.place.across)
+        self.send_a(lev).start()
+        self.send_b(lev).start()
+        self.join(lev * 4 + self.place.there_y)
+        self.join(lev * 4 + self.place.there_x)
+
+    def second(self, i):
+        lev = self.plane(i)
+        mine = self.mine.at[lev * 4 + self.place.there_y]
+        self.send_a(lev).wait_recv()
+        self.add_into(mine, [(mine, 0), (self.from_a.at[lev], 0)], 0, self.half)
+        self.send_y(lev).start()
+        mine = self.mine.at[lev * 4 + self.place.there_x]
+        self.send_b(lev).wait_recv()
+        self.add_into(mine, [(mine, 0), (self.from_b.at[lev], -self.half)], self.half, self.half)
+        self.send_x(lev).start()
+        self.join(lev * 4 + self.place.here)
+
+    def third(self, i):
+        rows, out, lev = self.rows, self.out, self.plane(i)
+        mine = self.mine.at[lev * 4 + self.place.here]
+        self.send_y(lev).wait_recv()
+        self.send_x(lev).wait_recv()
+        terms = [(mine, 0), (self.from_y.at[lev], 0), (self.from_x.at[lev], 0)]
+        own = i == self.planes - 1
+        total = out.at[part_rows(self.place.core * rows, rows)] if own else mine
+        self.add_into(total, terms, 0, rows)
+
+        def more(cond, send, arrived):
+            @pl.when(cond)
+            def _():
+                send(lev).wait_recv()
+                self.add_into(total, [(total, 0), (arrived.at[lev], 0)], 0, rows)
+
+        if own:
+            more(self.has_up, self.send_down, self.from_up)
+            more(self.has_down, self.send_up, self.from_down)
+        else:
+            more(self.has_up & (lev < self.level), self.send_down, self.from_up)
+            more(self.has_down & (lev > self.level), self.send_up, self.from_down)
+            pl.when(lev < self.level)(lambda: self.send_down(lev).start())
+            pl.when(lev > self.level)(lambda: self.send_up(lev).start())
 
     def begin(self):
         if self.prepare is not None:
             self.prepare(self.refs)
         if self.prelude is None:
-            self.make(*self.steps[0])
+            self.make(0)
+
+    def advance(self, i):
+        if i + 1 < self.planes:
+            self.make(i + 1)
+        if i < self.planes:
+            self.first(i)
+        if 0 <= i - 1 < self.planes:
+            self.second(i - 1)
+        if 0 <= i - 2 < self.planes:
+            self.third(i - 2)
 
     def middle(self):
-        steps, calls = self.steps, []
+        calls = []
         if self.prelude is not None:
-            calls += self.prelude(self.refs)
-            calls.append(lambda: self.make(*steps[0]))
-        for i in range(len(steps) + 2):
-
-            def call(i=i):
-                if i + 1 < len(steps):
-                    self.make(*steps[i + 1])
-                if i < len(steps):
-                    self.first(*steps[i])
-                if 0 <= i - 1 < len(steps):
-                    self.second(*steps[i - 1])
-                if 0 <= i - 2 < len(steps):
-                    self.third(*steps[i - 2])
-
-            calls.append(call)
-        return calls
+            calls += [lambda: None] * self.delay + self.prelude(self.refs)
+            calls.append(functools.partial(self.make, 0))
+        return calls + [functools.partial(self.advance, i) for i in range(self.planes + 2)]
 
     def hand(self, whose):
         spot = part_rows(whose * self.rows, self.rows)
@@ -557,23 +534,202 @@
     def end(self):
         self.hand(self.place.core).start()
 
-        def finish(lev, side, cond):
-            def body():
-                for spot in range(4):
-                    self.swap(lev * 4 + spot).wait_send()
-                for send in (self.send_a, self.send_b, self.send_y, self.send_x):
-                    send(lev).wait_send()
-                if side < 0:
-                    self.send_down(lev).wait_send()
-                if side > 0:
-                    self.send_up(lev).wait_send()
-
-            guarded(cond, body)
-
-        for step in self.steps:
-            finish(*step)
+        for i in range(self.planes):
+            lev = self.plane(i)
+            for spot in range(4):
+                self.swap(lev * 4 + spot).wait_send()
+            for send in (self.send_a, self.send_b, self.send_y, self.send_x):
+                send(lev).wait_send()
+            if i < self.planes - 1:
+                pl.when(lev < self.level)(lambda lev=lev: self.send_down(lev).wait_send())
+                pl.when(lev > self.level)(lambda lev=lev: self.send_up(lev).wait_send())
         self.hand(self.place.core).wait_send()
         self.hand(1 - self.place.core).wait_recv()
+
+
+class Experts:
+    def __init__(self, gather, out_all, weights, shared_w, capacity):
+        slots, seq, width = out_all.shape
+        hidden, room, bf16 = weights[0].shape[1], shared_w.shape[1], jnp.bfloat16
+        self.gather, self.capacity, self.room, self.reach = gather, capacity, room, gather.reach
+        self.slots, self.seq, self.width, self.hidden = slots, seq, width, hidden
+        rows = (slots, capacity)
+        turn = (room, slots * seq)
+
+        def shape(dims, kind=bf16):
+            return jax.ShapeDtypeStruct(dims, kind)
+
+        self.ins = [(a, pl.ANY) for a in [out_all] + weights] + [(shared_w, pltpu.VMEM)]
+        self.outs = [
+            (shape((slots, seq, width + LANES)), pltpu.VMEM),
+            (shape(rows + (width,)), pltpu.VMEM),
+            (shape(rows + (seq,)), pltpu.VMEM),
+            (shape(turn), pltpu.VMEM),
+            (shape((3, room, width)), pltpu.VMEM),
+            (shape(rows + (width,)), pl.ANY),
+            (shape(rows + (width,)), pl.ANY),
+        ] + [(shape(rows + (hidden,)), pltpu.VMEM)] * 3
+        self.scratch = (
+            [pltpu.VMEM(out_all.shape, bf16)]
+            + [pltpu.VMEM(w.shape, bf16) for w in weights]
+            + [pltpu.VMEM((4 * capacity, width), bf16)] * 4
+            + [
+                pltpu.VMEM((4 * capacity, LANES), jnp.float32),
+                pltpu.VMEM((capacity + 2 * room, width), bf16),
+                pltpu.VMEM((4, capacity + 2 * room, seq), bf16),
+                pltpu.VMEM((3, room, width), jnp.float32),
+                DMA((4,)),
+                DMA((2,)),
+            ]
+        )
+
+    def bind(self, place, ins, outs, scratch):
+        self.place = place
+        self.out_hbm, self.hbm_weights, self.shared_w = ins[0], ins[1:4], ins[4]
+        self.part, self.out_block, self.picks, self.act_turn, self.shared_grads = outs[:5]
+        self.rows_hbm, self.cot_hbm, self.act, self.gate_delta, self.up_delta = outs[5:]
+        self.out_rows, self.gate, self.up, self.down = scratch[:4]
+        self.rows, self.cot, self.grads, self.back = scratch[4:8]
+        self.weight, self.held, self.left, self.total, self.load_sem, self.save_sem = scratch[8:]
+        self.level = lax.rem(place.chip // 4, self.gather.planes)
+
+    def loads(self):
+        pairs = zip([self.out_hbm, *self.hbm_weights], [self.out_rows, self.gate, self.up, self.down])
+        return [
+            pltpu.make_async_copy(src, dst, self.load_sem.at[k]) for k, (src, dst) in enumerate(pairs)
+        ]
+
+    def saves(self, lev):
+        at = pl.ds(lev * 4 * self.capacity, 4 * self.capacity)
+        pairs = [(self.rows, self.rows_hbm), (self.cot, self.cot_hbm)]
+        return [
+            pltpu.make_async_copy(
+                src.reshape(4, self.capacity, self.width), dst.at[pl.ds(lev * 4, 4)], self.save_sem.at[k]
+            )
+            for k, (src, dst) in enumerate(pairs)
+        ]
+
+    def begin(self):
+        for load in self.loads():
+            load.start()
+        self.total[...] = jnp.zeros_like(self.total)
+        self.held[self.capacity :] = self.shared_w[:2].reshape(2 * self.room, self.width)
+
+    def choose(self, lev, t):
+        marked, seq, cap = self.gather.results[1], self.seq, self.capacity
+        below = lax.broadcasted_iota(jnp.int32, (seq, seq), 0)
+        upto = (below <= lax.broadcasted_iota(jnp.int32, (seq, seq), 1)).astype(jnp.bfloat16)
+        place_in = lax.broadcasted_iota(jnp.int32, (cap, seq), 0).astype(jnp.float32)
+        if t > 0:
+            for save in self.saves(lev):
+                save.wait()
+        for j in range(4):
+            slot, at = lev * 4 + j, slice(j * cap, (j + 1) * cap)
+            turned = marked[slot].T
+            here = jnp.sum(jnp.where(below == self.place.chip, turned, 0.0), axis=0, keepdims=True)
+            routed = jnp.where(here >= 0.0, 1.0, 0.0)
+            order = fdot(jnp.broadcast_to(routed, (8, seq)).astype(jnp.bfloat16), upto)[:1] - 1.0
+            hit = jnp.where(order == place_in, routed, 0.0)
+            weight = jnp.sum(hit * here, axis=-1, keepdims=True)
+            pick = hit.astype(jnp.bfloat16)
+            self.picks[slot] = pick
+            self.left[j, :cap] = pick
+            self.weight[at] = jnp.broadcast_to(weight, (cap, LANES))
+            for col in range(0, self.width, 512):
+                cols = slice(col, col + 512)
+                own = fdot(pick, self.gather.results[0][slot, :, cols])
+                self.rows[at, cols] = own.astype(jnp.bfloat16)
+                grad = fdot(pick, self.out_rows[slot, :, cols])
+                self.grads[at, cols] = grad.astype(jnp.bfloat16)
+                self.cot[at, cols] = (weight * grad).astype(jnp.bfloat16)
+        for save in self.saves(lev):
+            save.start()
+
+    def hidden_units(self, lev):
+        slots, chunk = pl.ds(lev * 4, 4), 256
+        for start in range(0, self.hidden, chunk):
+            cols = slice(start, min(start + chunk, self.hidden))
+            shape = (4, self.capacity, cols.stop - cols.start)
+            gate = fdot(self.rows[...], self.gate[:, cols])
+            up = fdot(self.rows[...], self.up[:, cols])
+            grad = dot_nt(self.cot[...], self.down[cols])
+            sig = jax.nn.sigmoid(gate)
+            gated = gate * sig
+            self.act[slots, :, cols] = (gated * up).astype(jnp.bfloat16).reshape(shape)
+            slope = sig * (1.0 + gate * (1.0 - sig))
+            self.gate_delta[slots, :, cols] = (grad * up * slope).astype(jnp.bfloat16).reshape(shape)
+            self.up_delta[slots, :, cols] = (grad * gated).astype(jnp.bfloat16).reshape(shape)
+
+    def shared_units(self, lev):
+        seq4, room = 4 * self.seq, self.room
+        tokens = self.gather.results[0][pl.ds(lev * 4, 4)].reshape(seq4, self.width)
+        grads = self.out_rows[pl.ds(lev * 4, 4)].reshape(seq4, self.width)
+        both = dot_nt(self.shared_w[:2].reshape(2 * room, self.width), tokens)
+        gate, up = both[:room], both[room:]
+        grad = dot_nt(self.shared_w[2], grads)
+        sig = jax.nn.sigmoid(gate)
+        act = (gate * sig * up).astype(jnp.bfloat16)
+        gate_delta = (grad * up * (sig * (1.0 + gate * (1.0 - sig)))).astype(jnp.bfloat16)
+        up_delta = (grad * gate * sig).astype(jnp.bfloat16)
+        self.act_turn[:, part_rows(lev * seq4, seq4)] = act
+        for j in range(4):
+            at = slice(j * self.seq, (j + 1) * self.seq)
+            self.left[j, self.capacity : self.capacity + room] = gate_delta[:, at]
+            self.left[j, self.capacity + room :] = up_delta[:, at]
+        for col in range(0, self.width, 512):
+            cols = slice(col, col + 512)
+            self.total[0, :, cols] += fdot(gate_delta, tokens[:, cols])
+            self.total[1, :, cols] += fdot(up_delta, tokens[:, cols])
+            self.total[2, :, cols] += fdot(act, grads[:, cols])
+
+    def outward(self, lev):
+        slots, cap, count = pl.ds(lev * 4, 4), self.capacity, 4 * self.capacity
+        act = self.act[slots].reshape(count, self.hidden)
+        gate_delta = self.gate_delta[slots].reshape(count, self.hidden)
+        up_delta = self.up_delta[slots].reshape(count, self.hidden)
+        weight = self.weight[:, :1]
+        route = jnp.zeros((count, 1), jnp.float32)
+        for col in range(0, self.width, 512):
+            cols = slice(col, col + 512)
+            out = fdot(act, self.down[:, cols]).astype(jnp.bfloat16).astype(jnp.float32)
+            route += jnp.sum(out * self.grads[:, cols].astype(jnp.float32), axis=-1, keepdims=True)
+            out = (weight * out).astype(jnp.bfloat16)
+            self.out_block[slots, :, cols] = out.reshape(4, cap, 512)
+            back = dot_nt(gate_delta, self.gate[cols]) + dot_nt(up_delta, self.up[cols])
+            self.back[:, cols] = back.astype(jnp.bfloat16)
+        lane = lax.broadcasted_iota(jnp.int32, (count, LANES), 1)
+        routes = jnp.where(lane == self.place.chip, route, 0.0).astype(jnp.bfloat16)
+        for j in range(4):
+            slot, at = lev * 4 + j, slice(j * cap, (j + 1) * cap)
+            self.held[:cap] = self.back[at]
+            left = self.left[j]
+            for col in range(0, self.width, 512):
+                cols = slice(col, col + 512)
+                self.part[slot, :, cols] = dot_tn(left, self.held[:, cols]).astype(jnp.bfloat16)
+            self.part[slot, :, self.width :] = dot_tn(left[:cap], routes[at]).astype(jnp.bfloat16)
+
+    def advance(self, i):
+        if 0 <= i - 2 < self.gather.planes:
+            self.outward(level_at(self.level, self.gather.planes, i - 2))
+        if 0 <= i - 1 < self.gather.planes:
+            t = i - 1
+            lev = level_at(self.level, self.gather.planes, t)
+            if t == 0:
+                self.gather.landed = True
+                for load in self.loads():
+                    load.wait()
+            self.gather.receive(t)
+            self.choose(lev, t)
+            self.hidden_units(lev)
+            self.shared_units(lev)
+
+    def middle(self):
+        return [functools.partial(self.advance, i) for i in range(self.gather.planes + 2)]
+
+    def end(self):
+        for save in self.saves(level_at(self.level, self.gather.planes, self.gather.planes - 1)):
+            save.wait()
+        self.shared_grads[...] = self.total[...].astype(jnp.bfloat16)
 
 
 def greet(place, ops):
@@ -1034,7 +1190,8 @@
 
 
 def fits(groups, heads, block, width):
-    return groups % heads == 0 and heads % 4 == 0 and block % 64 == 0 and width == groups * LANES and 4 * groups * block * width <= 24 << 20
+    whole = groups in (4, 8, 16) and heads in (4, 8, 16) and groups % heads == 0
+    return whole and block % 64 == 0 and width == groups * LANES
 
 
 def masked_scores(query_rows, key_rows):
@@ -1133,13 +1290,6 @@
         ],
         1,
     )
-    query_wt = from_blocks(got[:, :at_kv])
-    kvup_w = (
-        got[:, at_kv:at_o]
-        .reshape(groups, kv_halves, lat_rows, own_cols)
-        .transpose(0, 2, 1, 3)
-        .reshape(lat_width, DN + DV)
-    )
     route_wt = from_blocks(small_all[:, :groups])
     gain_one = small_all[:, groups].reshape(width).astype(jnp.float32)
     gain_two = small_all[:, groups + 1].reshape(width).astype(jnp.float32)
@@ -1154,10 +1304,17 @@
     by_seq = (heads, seq_len, -1)
     fold = 2
 
+    def rotated(block, cos_ref, sin_ref, sign):
+        flipped = jnp.concatenate([block[:, DR // 2 :], block[:, : DR // 2]], axis=-1)
+        reps = block.shape[0] // seq_len
+        cos_rows = jnp.concatenate([cos_ref[...]] * reps, axis=0)
+        sin_rows = jnp.concatenate([sin_ref[...]] * reps, axis=0)
+        return (block * cos_rows + sign * flipped * sin_rows).astype(bf16)
+
     def attend_forward(refs):
         rows_in, parts, lat_w, kv_gain_ref, cos_ref, sin_ref = refs[:6]
-        query_out, key_out, value_out, prob_out, lat_out, latent_out, mixed_out, out_w = refs[6:14]
-        query_w, kv_w = refs[14:]
+        query_out, key_out, value_out, prob_out, lat_out, latent_out, mixed_out = refs[6:13]
+        out_w, query_w, kv_w = refs[13:]
 
         def assemble():
             for j in range(groups):
@@ -1170,20 +1327,14 @@
                     across = slice(half * own_cols, (half + 1) * own_cols)
                     kv_w[down, across] = parts[j, start : start + lat_rows]
 
-        def rotated(block):
-            flipped = jnp.concatenate([block[:, DR // 2 :], block[:, : DR // 2]], axis=-1)
-            cos_rows = jnp.concatenate([cos_ref[...]] * fold, axis=0)
-            sin_rows = jnp.concatenate([sin_ref[...]] * fold, axis=0)
-            return (block * cos_rows + flipped * sin_rows).astype(bf16)
-
         def some(first):
             rows = rows_in[first : first + fold].reshape(fold * seq_len, width)
             query = dot_nt(rows, query_w[...])
-            query_plain, query_turn = query[:, :DN].astype(bf16), rotated(query[:, DN:])
+            query_plain, query_turn = query[:, :DN].astype(bf16), rotated(query[:, DN:], cos_ref, sin_ref, 1.0)
             full = fdot(rows, lat_w[...])
             plain = full[:, :lat_width]
             latent = (plain * rms_scale(plain) * kv_gain_ref[...]).astype(bf16)
-            key_turn = rotated(full[:, lat_width:])
+            key_turn = rotated(full[:, lat_width:], cos_ref, sin_ref, 1.0)
             key_value = fdot(latent, kv_w[...]).astype(bf16)
             latent_out[first : first + fold] = latent.reshape(fold, seq_len, lat_width)
             lat_out[first : first + fold] = plain.reshape(fold, seq_len, lat_width)
@@ -1228,7 +1379,6 @@
                 heads,
                 seq_len,
                 width,
-                [pltpu.VMEM((DQK, width), bf16), pltpu.VMEM((lat_width, DN + DV), bf16)],
                 extra=[
                     shaped(DQK, bf16),
                     shaped(DQK, bf16),
@@ -1238,16 +1388,16 @@
                     shaped(lat_width, bf16),
                     shaped(DV, bf16),
                     jax.ShapeDtypeStruct((DV, width), bf16),
+                    jax.ShapeDtypeStruct((DQK, width), bf16),
+                    jax.ShapeDtypeStruct((lat_width, DN + DV), bf16),
                 ],
                 prelude=attend_forward,
             ),
         ],
         2,
     )
-    attn_sum, query_rows, key_rows, value_rows, att_probs, lat_plain, latent, mixed, output_w = (
-        attended
-    )
-    att_weights = att_probs.astype(bf16)
+    attn_sum, query_rows, key_rows, value_rows, att_probs, lat_plain, latent, mixed = attended[:8]
+    output_w, query_wt, kvup_w = attended[8:]
     mixed_flat = mixed.reshape(heads * seq_len, DV)
     normed1_all = normed1_all.reshape(heads * seq_len, width)
     latent = latent.reshape(heads * seq_len, lat_width)
@@ -1255,7 +1405,6 @@
     gate_sht = from_blocks(shared_got[:, :hidden])
     up_sht = from_blocks(shared_got[:, hidden : 2 * hidden])
     down_sh = from_blocks(shared_got[:, 2 * hidden :])
-    out_flat = out_all.reshape(groups * seq_len, width)
     hidden_state = layer_in + attn_sum
 
     stat_two = rms_scale(hidden_state)
@@ -1265,113 +1414,60 @@
     experts = jnp.arange(groups, dtype=jnp.int32)
     chosen = jnp.any(routes[:, :, None] == experts[None, None, :], axis=1)
     marked = widen(jnp.where(chosen, router_probs, -1.0), -(-groups // LANES) * LANES)
-    ((normed2_all, marked_all),) = exchange([Gather([normed2, marked], all_planes)], 3)
-    here = lax.dynamic_index_in_dim(marked_all, chip, 2, keepdims=False)
-    normed2_flat = normed2_all.reshape(groups * seq_len, width)
-
-    routed = here >= 0.0
-    order = jnp.cumsum(routed.astype(jnp.int32), axis=1) - 1
-    slots = jnp.arange(capacity, dtype=jnp.int32)
-    picks = (routed[:, None, :] & (order[:, None, :] == slots[None, :, None])).astype(bf16)
-    weight_rows = jnp.sum(picks.astype(jnp.float32) * here[:, None, :], axis=-1).reshape(-1, 1)
-    rows_in = fsum("skt,std->skd", picks, normed2_all).astype(bf16).reshape(-1, width)
-    grad_rows = fsum("skt,std->skd", picks, out_all).reshape(-1, width)
-    cot_in = (weight_rows * grad_rows).astype(bf16)
-    gate_w, up_w, down_w = expert_gate[0], expert_up[0], expert_down[0]
-    pre_gate = fdot(rows_in, gate_w)
-    pre_up = fdot(rows_in, up_w)
-    expert_act = (jax.nn.silu(pre_gate) * pre_up).astype(bf16)
-    block_out = fdot(expert_act, down_w).astype(bf16).astype(jnp.float32)
-    hidden_grad_ex = fsum("md,fd->mf", cot_in, down_w)
-    gate_delta = (hidden_grad_ex * pre_up * silu_grad(pre_gate)).astype(bf16)
-    up_delta = (hidden_grad_ex * jax.nn.silu(pre_gate)).astype(bf16)
+    room = -(-hidden // 16) * 16
+
+    def stacked(blocks):
+        return jnp.pad(blocks, [(0, room - hidden), (0, 0)])
+
+    token_gather = Gather([normed2, marked], all_planes, True)
+    experts_op = Experts(
+        token_gather,
+        out_all,
+        [expert_gate[0], expert_up[0], expert_down[0]],
+        jnp.stack([stacked(gate_sht), stacked(up_sht), stacked(down_sh)]),
+        capacity,
+    )
+    _, expert_results = exchange([token_gather, experts_op], 3)
+    grad_parts, out_block, picks, shared_act, shared_sums = expert_results[:5]
+    rows_in, cot_in, expert_act, gate_delta, up_delta = (
+        x.reshape(groups * capacity, -1) for x in expert_results[5:]
+    )
     expert_down_grad = fsum("mf,md->fd", expert_act, cot_in)[None]
     expert_gate_grad = fsum("md,mf->df", rows_in, gate_delta)[None]
     expert_up_grad = fsum("md,mf->df", rows_in, up_delta)[None]
-    row_block = (
-        fsum("mf,df->md", gate_delta, gate_w) + fsum("mf,df->md", up_delta, up_w)
-    ).astype(bf16)
-    route_grad_rows = jnp.sum(grad_rows * block_out, axis=-1).reshape(groups, capacity)
-    by_slot = (groups, capacity, width)
-    out_block = (weight_rows * block_out).astype(bf16).reshape(by_slot)
-    route_grad = jnp.sum(picks.astype(jnp.float32) * route_grad_rows[:, :, None], axis=1)
-    route_part = (route_grad[:, :, None] * (experts == chip)).astype(bf16)
-    route_part = widen(route_part, marked.shape[1])
-
-    shared_pre_gate = fsum("fd,td->ft", gate_sht, normed2_flat)
-    shared_pre_up = fsum("fd,td->ft", up_sht, normed2_flat)
-    shared_act = (jax.nn.silu(shared_pre_gate) * shared_pre_up).astype(bf16)
-    shared_hidden_grad = fsum("fd,td->ft", down_sh, out_flat)
-    shared_gate_delta = (shared_hidden_grad * shared_pre_up * silu_grad(shared_pre_gate)).astype(bf16)
-    shared_up_delta = (shared_hidden_grad * jax.nn.silu(shared_pre_gate)).astype(bf16)
-    shared_grads = jnp.concatenate(
-        [
-            to_blocks(fdot(shared_gate_delta, normed2_flat), groups),
-            to_blocks(fdot(shared_up_delta, normed2_flat), groups),
-            to_blocks(fdot(shared_act, out_flat), groups),
-        ],
-        axis=1,
-    )
-    room = -(-hidden // 16) * 16
-
-    def stacked(pieces):
-        return jnp.concatenate(
-            [jnp.pad(x, [(0, room - hidden)] + [(0, 0)] * (x.ndim - 1)) for x in pieces], axis=0
-        )
-
-    def left_side(pieces):
-        rows = stacked(pieces).reshape(-1, groups, seq_len).transpose(1, 0, 2)
-        return jnp.concatenate([picks, rows], axis=1)
-
-    def expert_parts(part, slot, refs):
-        for k, start in ((0, 0), (1, width)):
-            left, own, held = refs[k], refs[2 + k], refs[7 + k]
-            held[:capacity] = own[slot]
-            for col in range(0, width, 512):
-                product = lax.dot_general(
-                    left[slot],
-                    held[:, col : col + 512],
-                    (((0,), (0,)), ((), ())),
-                    preferred_element_type=jnp.float32,
-                )
-                part[slot, :, start + col : start + col + 512] = product.astype(bf16)
-        part[slot, :, 2 * width :] = refs[6][slot]
+    shared_grads = (
+        shared_sums[:, :hidden]
+        .reshape(3 * hidden, groups, own_cols)
+        .transpose(1, 0, 2)
+    )
+    out_left = jnp.concatenate(
+        [picks, shared_act.reshape(room, groups, seq_len).transpose(1, 0, 2)], axis=1
+    )
+
+    def expert_part(part, slot, refs):
+        left, own, held = refs[0], refs[1], refs[-1]
+        held[:capacity] = own[slot]
+        for col in range(0, width, 512):
+            product = lax.dot_general(
+                left[slot],
+                held[:, col : col + 512],
+                (((0,), (0,)), ((), ())),
+                preferred_element_type=jnp.float32,
+            )
+            part[slot, :, col : col + 512] = product.astype(bf16)
 
     def hold_shared(refs):
-        refs[7][capacity:] = refs[4][...]
-        refs[8][capacity:] = refs[5][...]
+        refs[-1][capacity:] = refs[2][...]
 
     ((summed,),) = exchange(
-        [
-            Reduce(
-                [
-                    left_side([shared_act]),
-                    left_side([shared_gate_delta, shared_up_delta]),
-                    out_block,
-                    row_block.reshape(by_slot),
-                    stacked([down_sh]),
-                    stacked([gate_sht, up_sht]),
-                    route_part,
-                ],
-                expert_parts,
-                groups,
-                seq_len,
-                2 * width + marked.shape[1],
-                [
-                    pltpu.VMEM((capacity + room, width), bf16),
-                    pltpu.VMEM((capacity + 2 * room, width), bf16),
-                ],
-                hold_shared,
-            )
-        ],
-        4,
-    )
-    layer_out = hidden_state + summed[:, :width]
-    prob_grad = summed[:, 2 * width : 2 * width + groups]
+        [Reduce([grad_parts], None, groups, seq_len, width + marked.shape[1])], 4
+    )
+    normed2_sum = summed[:, :width]
+    prob_grad = summed[:, width : width + groups]
     logit_delta = (
         router_probs * (prob_grad - jnp.sum(router_probs * prob_grad, axis=-1, keepdims=True))
     ).astype(bf16)
-    normed2_grad = summed[:, width : 2 * width] + fdot(logit_delta, route_wt)
+    normed2_grad = normed2_sum + fdot(logit_delta, route_wt)
     router_gradt = fsum("te,td->ed", logit_delta, normed2)
     norm2_gain_grad = jnp.sum(normed2_grad * unit_two, axis=0)
     scaled_two = normed2_grad * gain_two
@@ -1380,54 +1476,92 @@
     )
 
     hidden_rows = hidden_grad.astype(bf16)
-    ((hidden_all,),) = exchange([Gather([hidden_rows], planes)], 5)
-    hidden_all = hidden_all.reshape(heads * seq_len, width)
-    o_grad = fdot(lax.optimization_barrier(mixed_flat.T), hidden_all)
-    mixed_grad = fsum("td,vd->tv", hidden_all, output_w).astype(bf16).reshape(by_seq)
-    value_grad = fsum("sqk,sqd->skd", att_weights, mixed_grad)
-    dprob = fsum("sqd,skd->sqk", mixed_grad, value_rows)
-    row_delta = jnp.sum(att_probs * dprob, axis=-1, keepdims=True)
-    score_delta = (att_probs * (dprob - row_delta) * DQK ** (-0.5)).astype(bf16)
-    query_grad = fsum("sqk,skd->sqd", score_delta, key_rows)
-    key_grad = fsum("sqk,sqd->skd", score_delta, query_rows)
-    query_delta = (
-        jnp.concatenate(
-            [query_grad[..., :DN], rotate_back(query_grad[..., DN:], cosine, sine_part)], axis=-1
-        )
-        .astype(bf16)
-    )
-    kv_delta = (
-        jnp.concatenate([key_grad[..., :DN], value_grad], axis=-1)
-        .astype(bf16)
-    )
+    hidden_gather = Gather([hidden_rows], planes, True)
+
+    def attend_backward(refs):
+        rows_in, keys, values, probs, out_w, cos_ref, sin_ref = refs[:7]
+        query_to, kv_to, turn_to = refs[9:]
+        place, hidden_in = hidden_gather.place, hidden_gather.results[0]
+
+        def some(level, first, second, own):
+            slots = [level * 4 + first, level * 4 + second]
+            hidden_gather.ready(slots[0], not own)
+            hidden_gather.ready(slots[1], True)
+            rows = jnp.concatenate([hidden_in[slot] for slot in slots], axis=0)
+            mixed_grads = dot_nt(rows, out_w[...]).astype(bf16)
+            for k in range(2):
+                slot = slots[k]
+                mixed_grad = mixed_grads[k * seq_len : (k + 1) * seq_len]
+                prob = probs[slot]
+                value_grad = dot_tn(prob.astype(bf16), mixed_grad)
+                dprob = dot_nt(mixed_grad, values[slot])
+                row_delta = jnp.sum(prob * dprob, axis=-1, keepdims=True)
+                score_delta = (prob * (dprob - row_delta) * DQK ** (-0.5)).astype(bf16)
+                query_grad = fdot(score_delta, keys[slot])
+                key_grad = dot_tn(score_delta, rows_in[slot])
+                query_to[slot, :, :DN] = query_grad[:, :DN].astype(bf16)
+                query_to[slot, :, DN:] = rotated(query_grad[:, DN:], cos_ref, sin_ref, -1.0)
+                kv_to[slot, :, :DN] = key_grad[:, :DN].astype(bf16)
+                kv_to[slot, :, DN:] = value_grad.astype(bf16)
+                turn_to[slot, :, :DR] = key_grad[:, DN:].astype(bf16)
+                turn_to[slot, :, DR:] = jnp.zeros((seq_len, LANES - DR), bf16)
+
+        level, calls = hidden_gather.level, []
+        hidden_gather.landed = True
+        for far in range(planes):
+            where = lax.rem(level + far, planes)
+            calls.append(functools.partial(some, where, place.here, place.there_x, far == 0))
+            calls.append(functools.partial(some, where, place.there_y, place.across, False))
+        return calls
 
     def back_part(part, slot, refs):
         for col in range(0, width, 512):
-            product = fdot(refs[0][slot], refs[1][:, col : col + 512])
+            product = fdot(refs[9][slot], refs[7][:, col : col + 512])
             part[slot, :, col : col + 512] = product.astype(bf16)
-        product = fdot(refs[2][slot], refs[3][...])
+        product = dot_nt(refs[10][slot], refs[8][...])
         part[slot, :, width : width + lat_width] = product.astype(bf16)
-        part[slot, :, width + lat_width :] = refs[4][slot]
-
-    (back,), (owned_early,) = exchange(
+        part[slot, :, width + lat_width :] = refs[11][slot]
+
+    ((hidden_all,), (out_sum,), (back, query_delta, kv_delta), (owned_early,)) = exchange(
         [
+            hidden_gather,
+            Reduce(
+                [out_left, out_block, stacked(down_sh)],
+                expert_part,
+                groups,
+                seq_len,
+                width,
+                [pltpu.VMEM((capacity + room, width), bf16)],
+                hold_shared,
+            ),
             Reduce(
                 [
-                    query_delta,
+                    query_rows,
+                    key_rows,
+                    value_rows,
+                    att_probs,
+                    output_w,
+                    turn_cos,
+                    turn_sin,
                     query_wt,
-                    kv_delta,
-                    kvup_w.T,
-                    widen(key_grad[..., DN:], LANES).astype(bf16),
+                    kvup_w,
                 ],
                 back_part,
                 heads,
                 seq_len,
                 width + lat_width + LANES,
+                [pltpu.VMEM((heads, seq_len, LANES), bf16)],
+                extra=[shaped(DQK, bf16), shaped(DN + DV, bf16)],
+                prelude=attend_backward,
+                delay=2,
             ),
-            Swap(jnp.concatenate([shared_grads, to_blocks(o_grad, groups)], axis=1), pace=3),
+            Swap(shared_grads),
         ],
-        6,
-    )
+        5,
+    )
+    layer_out = hidden_state + out_sum
+    hidden_all = hidden_all.reshape(heads * seq_len, width)
+    o_grad = fdot(lax.optimization_barrier(mixed_flat.T), hidden_all)
     normed1_query = back[:, :width]
     latent_grad = back[:, width : width + lat_width]
     rot_sum = back[:, width + lat_width : width + lat_width + DR]
@@ -1452,7 +1586,14 @@
         .transpose(0, 2, 1, 3)
         .reshape(groups, kv_block, own_cols)
     )
-    head_grads = jnp.concatenate([to_blocks(fdot(query_delta_t, normed1_all), groups), kvb_blocks], 1)
+    head_grads = jnp.concatenate(
+        [
+            to_blocks(fdot(query_delta_t, normed1_all), groups),
+            kvb_blocks,
+            to_blocks(o_grad, groups),
+        ],
+        axis=1,
+    )
     (latent_delta_all,), (owned_heads,) = exchange(
         [Gather([latent_delta], planes), Swap(head_grads, pace=4)], 7
     )
@@ -1492,12 +1633,12 @@
     of_heads = over_copies(owned_heads)
     q_grad = of_heads[:, :at_kv].transpose(2, 0, 1).reshape(own_cols, heads * DQK)
     kvb_grad = (
-        of_heads[:, at_kv:]
+        of_heads[:, at_kv:at_o]
         .reshape(heads, kv_halves, lat_rows, own_cols)
         .transpose(2, 0, 1, 3)
         .reshape(lat_rows, heads * (DN + DV))
     )
-    own_o_grad = over_copies(owned_early[:, 3 * hidden :]).reshape(heads * DV, own_cols)
+    own_o_grad = of_heads[:, at_o:].reshape(heads * DV, own_cols)
     kva_grad = over_copies(owned_share)[:, :share].reshape(heads * share, own_cols).T
     of_shared = owned_early[:, : 3 * hidden].astype(jnp.float32)
 

time: 647 us -> 580 us (0.90)
  matrix products: 101 us -> 35.4 us
  Pallas kernels: 438 us -> 465 us
  other arithmetic: 47.5 us -> 26.4 us
  local copies, waits for them, and re-layouts: 47.5 us -> 40.5 us
    dot_general x19 -> x6, matrix products: 60.6 us -> 23.7 us  [fsum(): return jnp.einsum(spec, left, right, preferred_element_type=jnp.float32)]
    dot_general x11 -> x5, matrix products: 40.7 us -> 11.8 us  [fdot(): return jnp.dot(left, right, preferred_element_type=jnp.float32)]
    pallas_call x8 -> x7, Pallas kernels: 438 us -> 465 us  [exchange(): pl.pallas_call(functools.partial(chip_kernel, ops), out_shape=[shape for...]
    convert_element_type x7 -> x0, other arithmetic: 9.63 us -> none  [the longest x2 8.54 us: by_heads(): cot_in = (weight_rows * grad_rows).astype(bf16)]
    unnamed x135 -> x65, local copies, waits for them, and re-layouts: 14.8 us -> 16.7 us
where the time goes in v3:
time: 580 us; the launch traced here: 569 us
  Pallas kernels  465 us (80%)
  local copies, waits for them, and re-layouts  40.5 us (7%)
  matrix products  35.4 us (6%)
  other arithmetic  26.4 us (5%)
    pallas_call x7, Pallas kernels, exchange(): pl.pallas_call(functools.partial(chip_kernel, ops), out_shape=[shape for...  465 us
    dot_general x6, matrix products, fsum(): return jnp.einsum(spec, left, right, preferred_element_type=jnp.float32)  23.7 us
    unnamed x65, local copies, waits for them, and re-layouts  16.7 us
    dot_general x5, matrix products, fdot(): return jnp.dot(left, right, preferred_element_type=jnp.float32)  11.8 us

profile of v3, /device:TPU:0, one launch (start us, length us, event | category | flops | bytes accessed | tf_op | source)
XLA Modules:
  0.0 568.8 jit_solution(6437735886208575723)
XLA Ops:
  7.1 64.7 %shard_map.288 = (bf16[16,32,128]{2,1,0:T(8,128)(2,1)}, bf16[16,128,576]{2,1,0:T(8,128)(2,1)}, bf16[16,384,128]{2,1,0:T(8,128)(2,1)}, bf16[8,128,2048]{2,1,0:T(8,128)(2,1)}) custom-call(bf16[16,32,128]{2,1,0:T(8,128)(2,1)} %broadcast_in_dim.21.refs_0_, bf16[128,576]{1,0:T(8,128)(2,1)} %copy.128.refs_1_, bf16[16,384,128]{2,1,0:T(8,128)(2,1)} %bitcast.194, ...), custom_call_target="tpu_custom_call" | custom-call | bytes 11157504 | tf_op jit(solution)/shard_map/pallas_call | solution.py:786
  75.6 91.0 %shard_map.289 = (bf16[16,128,2048]{2,1,0:T(8,128)(2,1)}, bf16[16,264,128]{2,1,0:T(8,128)(2,1)}, f32[128,2048]{1,0:T(8,128)}, bf16[8,128,192]{2,1,0:T(8,128)(2,1...) custom-call(bf16[128,2048]{1,0:T(8,128)(2,1)} %convert_element_type., ...), custom_call_target="tpu_custom_call" | custom-call | bytes 26871808 | tf_op jit(solution)/shard_map/pallas_call | solution.py:786
  166.7 1.5 multiply_reduce_fusion.5
  173.5 4.6 copy.133
  178.1 4.6 copy.134
  182.6 85.6 %shard_map.290 = (bf16[16,128,2048]{2,1,0:T(8,128)(2,1)}, f32[16,128,128]{2,1,0:T(8,128)}, bf16[16,128,2176]{2,1,0:T(8,128)(2,1)}, bf16[16,64,2048]{2,1,0:T(8,12...) custom-call(bf16[128,2048]{1,0:T(8,128)(2,1)} %copy-done.1, ...), custom_call_target="tpu_custom_call" | custom-call | bytes 55902208 | tf_op jit(solution)/shard_map/pallas_call | solution.py:786
  268.3 9.0 %convolution_bitcast_fusion.2 = f32[1,704,2048]{2,1,0:T(8,128)} fusion(bf16[16,64,704]{2,1,0:T(8,128)(2,1)} %get-tuple-element.88, bf16[16,64,2048]{2,1,0:T(8,128)(2,1)} %get-tuple-element.89), kind=kOutput, calls=%fused_computation.2 | convolution fusion | flops 2952790016 | bytes 11403264 | tf_op jit(solution)/shard_map/mf,md->fd/dot_general | solution.py:71
  277.2 5.1 convolution_bitcast_fusion
  282.3 5.1 convolution_bitcast_fusion.1
  288.4 48.3 %shard_map.291 = f32[128,2176]{1,0:T(8,128)} custom-call(bf16[16,128,2176]{2,1,0:T(8,128)(2,1)} %get-tuple-element.60.refs_0_), custom_call_target="tpu_custom_call" | custom-call | bytes 10027008 | tf_op jit(solution)/shard_map/pallas_call | solution.py:786
  337.8 1.8 multiply_reduce_fusion
  339.6 1.5 fusion.13
  342.7 114.5 %shard_map.292 = (bf16[8,128,2048]{2,1,0:T(8,128)(2,1)}, f32[128,2048]{1,0:T(8,128)}, f32[128,2688]{1,0:T(8,128)}, bf16[8,128,192]{2,1,0:T(8,128)(2,1)}, bf16[8,...) custom-call(bf16[128,2048]{1,0:T(8,128)(2,1)} %get-tuple-element.160.refs_0_, ...), custom_call_target="tpu_custom_call" | custom-call | bytes 18677760 | tf_op jit(solution)/shard_map/pallas_call | solution.py:786
  457.2 3.4 convolution_convert_fusion
  463.2 3.0 convolution_convert_fusion.1
  468.6 2.2 pad_maximum_fusion.refs_1_
  477.1 38.1 %shard_map.293 = (bf16[8,128,576]{2,1,0:T(8,128)(2,1)}, bf16[16,384,128]{2,1,0:T(8,128)(2,1)}) custom-call(bf16[128,576]{1,0:T(8,128)(2,1)} %pad_maximum_fusion.5.refs_0_, bf16[16,384,128]{2,1,0:T(8,128)(2,1)} %pad_maximum_fusion.refs_1_), custom_call_target="tpu_custom_call" | custom-call | bytes 4472832 | tf_op jit(solution)/shard_map/pallas_call | solution.py:786
  515.2 1.9 convert_reduce_fusion
  520.7 3.2 multiply_reduce_fusion.1
  525.8 3.1 convolution_convert_fusion.2
  529.7 22.8 %shard_map.294 = (bf16[16,80,128]{2,1,0:T(8,128)(2,1)}, f32[16,24,128]{2,1,0:T(8,128)}) custom-call(bf16[16,80,128]{2,1,0:T(8,128)(2,1)} %pad.41.refs_0_, f32[16,24,128]{2,1,0:T(8,128)} %pad.43.refs_1_), custom_call_target="tpu_custom_call" | custom-call | bytes 1048576 | tf_op jit(solution)/shard_map/pallas_call | solution.py:786
  557.9 1.9 reshape.285
  559.7 2.0 slice.108
  566.3 2.3 add.74
  (140 shorter events, 46.4 us)
Async XLA Ops:
  0.6 3.4 copy-start.14
  4.1 1.5 copy-start.15
  4.1 2.3 copy-start.18
  4.1 2.3 copy-start.20
  4.1 2.3 copy-start.21
  4.1 2.3 copy-start.22
  6.4 66.8 %copy-start.10 = (bf16[128,1408]{1,0:T(8,128)(2,1)S(1)}, bf16[128,1408]{1,0:T(8,128)(2,1)}, u32[]{:S(2)}) copy-start(bf16[128,1408]{1,0:T(8,128)(2,1)} %param.26) | copy-start | bytes 1081348
  7.1 66.4 %copy-start.11 = (bf16[128,1408]{1,0:T(8,128)(2,1)S(1)}, bf16[128,1408]{1,0:T(8,128)(2,1)}, u32[]{:S(2)}) copy-start(bf16[128,1408]{1,0:T(8,128)(2,1)} %param.27) | copy-start | bytes 1081348
  7.1 66.6 %copy-start.12 = (bf16[1408,128]{1,0:T(8,128)(2,1)S(1)}, bf16[1408,128]{1,0:T(8,128)(2,1)}, u32[]{:S(2)}) copy-start(bf16[1408,128]{1,0:T(8,128)(2,1)} %param.28) | copy-start | bytes 1081348
  73.5 1.3 copy-start.6
  75.6 91.0 %copy-start = (f32[128,2048]{1,0:T(8,128)S(1)}, f32[128,2048]{1,0:T(8,128)}, u32[]{:S(2)}) copy-start(f32[128,2048]{1,0:T(8,128)} %refs_3_.1) | copy-start | bytes 3145732
  166.7 1.6 copy-start.16
  168.4 2.8 copy-start.1
  268.2 9.0 %copy-start.23 = (bf16[16,64,2048]{2,1,0:T(8,128)(2,1)S(1)}, bf16[16,64,2048]{2,1,0:T(8,128)(2,1)}, u32[]{:S(2)}) copy-start(bf16[16,64,2048]{2,1,0:T(8,128)(2,1)} %get-tuple-element.85) | copy-start | bytes 12582916
  268.2 9.0 %copy-start.25 = (bf16[16,64,704]{2,1,0:T(8,128)(2,1)S(1)}, bf16[16,64,704]{2,1,0:T(8,128)(2,1)}, u32[]{:S(2)}) copy-start(bf16[16,64,704]{2,1,0:T(8,128)(2,1)} %get-tuple-element.87) | copy-start | bytes 4325380
  277.2 5.1 copy-start.24
  282.3 5.1 copy-start.9
  282.3 5.2 copy-start.13
  288.4 49.4 %copy-start.17 = (bf16[16,32,128]{2,1,0:T(8,128)(2,1)S(1)}, bf16[16,32,128]{2,1,0:T(8,128)(2,1)}, u32[]{:S(2)}) copy-start(bf16[16,32,128]{2,1,0:T(8,128)(2,1)} %get-tuple-element.56) | copy-start | bytes 393220
  336.6 3.0 copy-start.7
  339.6 1.5 copy-start.8
  460.6 1.3 copy-start.27
  529.0 28.0 %slice-start = ((f32[8,384,128]{2,1,0:T(8,128)}), f32[8,64,128]{2,1,0:T(8,128)S(1)}, s32[]{:S(2)}) async-start(f32[8,384,128]{2,1,0:T(8,128)} %copy-done.3), calls=%async_computation | async-start | bytes 524288 | tf_op jit(solution)/shard_map/slice | solution.py:1636
  559.7 2.0 copy-start.5
  (5 other events, 5.7 us)

commit v4 on v3

--- a/solution.py
+++ b/solution.py
@@ -102,6 +102,11 @@
         self.below = {EXPERT: self.chip - 4}
         self.mate = {TENSOR: 1 - self.core}
 
+    def spot(self, q):
+        x = lax.rem(self.here + 1 - lax.rem(q, 2), 2)
+        y = lax.rem(self.here // 2 + 1 - q // 2, 2)
+        return 2 * y + x
+
     def partner(self, j):
         return lax.rem(self.chip + j, self.groups)
 
@@ -111,7 +116,7 @@
         return lax.rem(level + t, planes)
     flip = level // 2
     near = lax.rem(level + flip, 2)
-    order = t + near * (1 - 2 * t) if t < 2 else t
+    order = t + near * (1 - 2 * t) * (1 - t // 2)
     return order * (1 - 2 * flip) + 3 * flip
 
 
@@ -148,23 +153,54 @@
         chip = self.place.chip
         return pltpu.make_async_copy(self.source.at[chip], self.result.at[chip], self.own_sem)
 
-    def send(self, first):
-        for j in range(first, min(first + self.pace, self.groups)):
-            self.copy(j, self.place.partner(j), self.place.chip).start()
+    def send(self, i):
+        for q in range(min(self.pace, self.groups - 1)):
+            j = 1 + i * self.pace + q
+
+            @pl.when(j < self.groups)
+            def _(j=j):
+                self.copy(j, self.place.partner(j), self.place.chip).start()
 
     def begin(self):
         self.own().start()
-        self.send(1)
-
-    def middle(self):
-        firsts = range(1 + self.pace, self.groups, self.pace)
-        return [functools.partial(self.send, first) for first in firsts]
+        self.send(0)
+
+    def rest(self, offset):
+        count = -(-(self.groups - 1) // self.pace) - 1
+        return [(offset, count, lambda i: self.send(i + 1))]
+
+    def segments(self):
+        return self.rest(0)
 
     def end(self):
         self.own().wait()
-        for j in range(1, self.groups):
+
+        @pl.loop(1, self.groups)
+        def _(j):
             self.copy(j, self.place.chip, self.place.partner(self.groups - j)).wait_recv()
             self.copy(j, self.place.partner(j), self.place.chip).wait_send()
+
+
+class MadeSwap(Swap):
+    def __init__(self, operands, shape, make, delay, pace, scratch=()):
+        self.pace, self.make, self.delay = pace, make, delay
+        self.ins = [(a, pltpu.VMEM) for a in operands]
+        self.outs = [(jax.ShapeDtypeStruct(shape, jnp.bfloat16), pl.ANY)]
+        groups = shape[0]
+        self.scratch = [DMA, DMA((groups,)), DMA((groups,)), pltpu.VMEM(shape, jnp.bfloat16)]
+        self.scratch += list(scratch)
+
+    def bind(self, place, ins, outs, scratch):
+        super().bind(place, [scratch[3]], outs, scratch[:3])
+        self.refs, self.extra = ins, scratch[4:]
+
+    def begin(self):
+        pass
+
+    def segments(self):
+        calls = self.make(self) + [lambda i: super(MadeSwap, self).begin()]
+        parts = [(self.delay + k, 1, call) for k, call in enumerate(calls)]
+        return parts + self.rest(self.delay + len(calls))
 
 
 class Gather:
@@ -235,23 +271,23 @@
     def begin(self):
         for a in range(self.count):
             self.own(a).start()
-        self.first(0)
-
-    def relays(self, a, t, act):
+        self.first(0, True)
+
+    def relays(self, a, t, own, act):
         lev = level_at(self.level, self.planes, t)
         up, down = self.has_up, self.has_down
-        if t > 0:
+        if not own:
             up, down = up & (lev < self.level), down & (lev > self.level)
-        pl.when(up)(lambda: act(self.along_z(a, lev, t == 0, True)))
-        pl.when(down)(lambda: act(self.along_z(a, lev, t == 0, False)))
-
-    def first(self, t):
+        pl.when(up)(lambda: act(self.along_z(a, lev, own, True)))
+        pl.when(down)(lambda: act(self.along_z(a, lev, own, False)))
+
+    def first(self, t, own=False):
         lev = level_at(self.level, self.planes, t)
         for a in range(self.count):
-            own, slot = t == 0, lev * 4 + self.place.here
+            slot = lev * 4 + self.place.here
             if not own:
                 self.along_z(a, lev, own, True).wait_recv()
-            self.relays(a, t, lambda copy: copy.start())
+            self.relays(a, t, own, lambda copy: copy.start())
             self.along_x(a, lev, slot, own).start()
             self.along_y(a, lev, slot, own).start()
             if not own:
@@ -278,34 +314,32 @@
             self.share(a, slot).start()
 
     def advance(self, i):
-        if i < self.planes:
-            self.first(i)
-        if 0 <= i - 1 < self.planes:
-            self.second(i - 1)
-        if 0 <= i - 2 < self.planes:
-            self.third(i - 2)
-
-    def middle(self):
-        return [functools.partial(self.advance, i) for i in range(1, self.planes + 2)]
+        pl.when(i < self.planes)(lambda: self.first(i))
+        pl.when(i < self.planes + 1)(lambda: self.second(i - 1))
+        pl.when(i > 1)(lambda: self.third(i - 2))
+
+    def segments(self):
+        return [(0, self.planes + 1, lambda i: self.advance(i + 1))]
+
+    def sent(self, t, own):
+        place, lev = self.place, level_at(self.level, self.planes, t)
+        for a in range(self.count):
+            slot = lev * 4 + place.here
+            self.relays(a, t, own, lambda copy: copy.wait_send())
+            self.along_x(a, lev, slot, own).wait_send()
+            self.along_y(a, lev, slot, own).wait_send()
+            self.corner_x(a, lev, lev * 4 + place.there_y).wait_send()
+            self.corner_y(a, lev, lev * 4 + place.there_x).wait_send()
+            for other in [place.there_y, place.there_x, place.across]:
+                self.share(a, lev * 4 + other).wait_send()
+            if not own:
+                self.share(a, slot).wait_send()
 
     def end(self):
-        place = self.place
         if not self.landed:
-            for t in range(self.planes):
-                self.receive(t)
-        for t in range(self.planes):
-            lev = level_at(self.level, self.planes, t)
-            for a in range(self.count):
-                own, slot = t == 0, lev * 4 + place.here
-                self.relays(a, t, lambda copy: copy.wait_send())
-                self.along_x(a, lev, slot, own).wait_send()
-                self.along_y(a, lev, slot, own).wait_send()
-                self.corner_x(a, lev, lev * 4 + place.there_y).wait_send()
-                self.corner_y(a, lev, lev * 4 + place.there_x).wait_send()
-                for other in [place.there_y, place.there_x, place.across]:
-                    self.share(a, lev * 4 + other).wait_send()
-                if not own:
-                    self.share(a, slot).wait_send()
+            self.receive_all()
+        self.sent(0, True)
+        pl.loop(1, self.planes)(lambda t: self.sent(t, False))
 
     def ready(self, slot, other):
         for a in range(self.count):
@@ -316,9 +350,14 @@
 
     def receive(self, t):
         place, lev = self.place, level_at(self.level, self.planes, t)
-        self.ready(lev * 4 + place.here, t > 0)
+        pl.when(t == 0)(lambda: self.ready(lev * 4 + place.here, False))
+        pl.when(t > 0)(lambda: self.ready(lev * 4 + place.here, True))
         for spot in (place.there_y, place.there_x, place.across):
             self.ready(lev * 4 + spot, True)
+
+    def receive_all(self):
+        self.landed = True
+        pl.loop(0, self.planes)(self.receive)
 
 
 class NormGather(Gather):
@@ -447,8 +486,9 @@
         return level_at(self.level, self.planes, self.planes - 1 - i)
 
     def make(self, i):
-        for spot in (self.place.across, self.place.there_y, self.place.there_x, self.place.here):
-            slot = self.plane(i) * 4 + spot
+        @pl.loop(0, 4)
+        def _(q):
+            slot = self.plane(i) * 4 + self.place.spot(q)
             if self.produce is not None:
                 self.produce(self.part, slot, self.refs)
             self.swap(slot).start()
@@ -485,24 +525,31 @@
         self.send_y(lev).wait_recv()
         self.send_x(lev).wait_recv()
         terms = [(mine, 0), (self.from_y.at[lev], 0), (self.from_x.at[lev], 0)]
-        own = i == self.planes - 1
-        total = out.at[part_rows(self.place.core * rows, rows)] if own else mine
-        self.add_into(total, terms, 0, rows)
-
-        def more(cond, send, arrived):
+
+        def more(total, cond, send, arrived):
             @pl.when(cond)
             def _():
                 send(lev).wait_recv()
                 self.add_into(total, [(total, 0), (arrived.at[lev], 0)], 0, rows)
 
-        if own:
-            more(self.has_up, self.send_down, self.from_up)
-            more(self.has_down, self.send_up, self.from_down)
-        else:
-            more(self.has_up & (lev < self.level), self.send_down, self.from_up)
-            more(self.has_down & (lev > self.level), self.send_up, self.from_down)
-            pl.when(lev < self.level)(lambda: self.send_down(lev).start())
-            pl.when(lev > self.level)(lambda: self.send_up(lev).start())
+        @pl.when(lev == self.level)
+        def _():
+            total = out.at[part_rows(self.place.core * rows, rows)]
+            self.add_into(total, terms, 0, rows)
+            more(total, self.has_up, self.send_down, self.from_up)
+            more(total, self.has_down, self.send_up, self.from_down)
+
+        @pl.when(lev < self.level)
+        def _():
+            self.add_into(mine, terms, 0, rows)
+            more(mine, self.has_up, self.send_down, self.from_up)
+            self.send_down(lev).start()
+
+        @pl.when(lev > self.level)
+        def _():
+            self.add_into(mine, terms, 0, rows)
+            more(mine, self.has_down, self.send_up, self.from_down)
+            self.send_up(lev).start()
 
     def begin(self):
         if self.prepare is not None:
@@ -511,21 +558,18 @@
             self.make(0)
 
     def advance(self, i):
-        if i + 1 < self.planes:
-            self.make(i + 1)
-        if i < self.planes:
-            self.first(i)
-        if 0 <= i - 1 < self.planes:
-            self.second(i - 1)
-        if 0 <= i - 2 < self.planes:
-            self.third(i - 2)
-
-    def middle(self):
-        calls = []
+        pl.when(i + 1 < self.planes)(lambda: self.make(i + 1))
+        pl.when(i < self.planes)(lambda: self.first(i))
+        pl.when((i > 0) & (i < self.planes + 1))(lambda: self.second(i - 1))
+        pl.when(i > 1)(lambda: self.third(i - 2))
+
+    def segments(self):
+        parts, start = [], 0
         if self.prelude is not None:
-            calls += [lambda: None] * self.delay + self.prelude(self.refs)
-            calls.append(functools.partial(self.make, 0))
-        return calls + [functools.partial(self.advance, i) for i in range(self.planes + 2)]
+            count, call = self.prelude(self.refs)
+            parts = [(self.delay, count, call), (self.delay + count, 1, self.make)]
+            start = self.delay + count + 1
+        return parts + [(start, self.planes + 2, self.advance)]
 
     def hand(self, whose):
         spot = part_rows(whose * self.rows, self.rows)
@@ -534,23 +578,24 @@
     def end(self):
         self.hand(self.place.core).start()
 
-        for i in range(self.planes):
-            lev = self.plane(i)
+
+        @pl.loop(0, self.planes)
+        def _(lev):
             for spot in range(4):
                 self.swap(lev * 4 + spot).wait_send()
             for send in (self.send_a, self.send_b, self.send_y, self.send_x):
                 send(lev).wait_send()
-            if i < self.planes - 1:
-                pl.when(lev < self.level)(lambda lev=lev: self.send_down(lev).wait_send())
-                pl.when(lev > self.level)(lambda lev=lev: self.send_up(lev).wait_send())
+            pl.when(lev < self.level)(lambda: self.send_down(lev).wait_send())
+            pl.when(lev > self.level)(lambda: self.send_up(lev).wait_send())
+
         self.hand(self.place.core).wait_send()
         self.hand(1 - self.place.core).wait_recv()
 
 
 class Experts:
-    def __init__(self, gather, out_all, weights, shared_w, capacity):
-        slots, seq, width = out_all.shape
-        hidden, room, bf16 = weights[0].shape[1], shared_w.shape[1], jnp.bfloat16
+    def __init__(self, gather, weights, shared_w, capacity):
+        slots, seq, width = gather.outs[0][0].shape
+        hidden, room, bf16 = weights[0].shape[0], shared_w.shape[1], jnp.bfloat16
         self.gather, self.capacity, self.room, self.reach = gather, capacity, room, gather.reach
         self.slots, self.seq, self.width, self.hidden = slots, seq, width, hidden
         rows = (slots, capacity)
@@ -559,7 +604,7 @@
         def shape(dims, kind=bf16):
             return jax.ShapeDtypeStruct(dims, kind)
 
-        self.ins = [(a, pl.ANY) for a in [out_all] + weights] + [(shared_w, pltpu.VMEM)]
+        self.ins = [(a, pl.ANY) for a in weights] + [(shared_w, pltpu.VMEM)]
         self.outs = [
             (shape((slots, seq, width + LANES)), pltpu.VMEM),
             (shape(rows + (width,)), pltpu.VMEM),
@@ -570,31 +615,31 @@
             (shape(rows + (width,)), pl.ANY),
         ] + [(shape(rows + (hidden,)), pltpu.VMEM)] * 3
         self.scratch = (
-            [pltpu.VMEM(out_all.shape, bf16)]
-            + [pltpu.VMEM(w.shape, bf16) for w in weights]
-            + [pltpu.VMEM((4 * capacity, width), bf16)] * 4
+            [pltpu.VMEM(w.shape, bf16) for w in weights]
+            + [pltpu.VMEM((4 * capacity, width), bf16)] * 3
             + [
                 pltpu.VMEM((4 * capacity, LANES), jnp.float32),
-                pltpu.VMEM((capacity + 2 * room, width), bf16),
-                pltpu.VMEM((4, capacity + 2 * room, seq), bf16),
+                pltpu.VMEM((4 * capacity + 2 * room, width), bf16),
+                pltpu.VMEM((4 * capacity + 2 * room, 4 * seq), bf16),
                 pltpu.VMEM((3, room, width), jnp.float32),
-                DMA((4,)),
+                DMA((3,)),
                 DMA((2,)),
             ]
         )
 
     def bind(self, place, ins, outs, scratch):
         self.place = place
-        self.out_hbm, self.hbm_weights, self.shared_w = ins[0], ins[1:4], ins[4]
+        self.hbm_weights, self.shared_w = ins[:3], ins[3]
+        self.tokens, self.out_rows, self.marked = self.gather.results
         self.part, self.out_block, self.picks, self.act_turn, self.shared_grads = outs[:5]
         self.rows_hbm, self.cot_hbm, self.act, self.gate_delta, self.up_delta = outs[5:]
-        self.out_rows, self.gate, self.up, self.down = scratch[:4]
-        self.rows, self.cot, self.grads, self.back = scratch[4:8]
-        self.weight, self.held, self.left, self.total, self.load_sem, self.save_sem = scratch[8:]
+        self.gate, self.up, self.down = scratch[:3]
+        self.rows, self.cot, self.grads = scratch[3:6]
+        self.weight, self.held, self.left, self.total, self.load_sem, self.save_sem = scratch[6:]
         self.level = lax.rem(place.chip // 4, self.gather.planes)
 
     def loads(self):
-        pairs = zip([self.out_hbm, *self.hbm_weights], [self.out_rows, self.gate, self.up, self.down])
+        pairs = zip(self.hbm_weights, [self.gate, self.up, self.down])
         return [
             pltpu.make_async_copy(src, dst, self.load_sem.at[k]) for k, (src, dst) in enumerate(pairs)
         ]
@@ -613,19 +658,23 @@
         for load in self.loads():
             load.start()
         self.total[...] = jnp.zeros_like(self.total)
-        self.held[self.capacity :] = self.shared_w[:2].reshape(2 * self.room, self.width)
+        self.held[4 * self.capacity :] = self.shared_w[:2].reshape(2 * self.room, self.width)
+        self.left[: 4 * self.capacity] = jnp.zeros((4 * self.capacity, 4 * self.seq), jnp.bfloat16)
 
     def choose(self, lev, t):
-        marked, seq, cap = self.gather.results[1], self.seq, self.capacity
+        seq, cap = self.seq, self.capacity
         below = lax.broadcasted_iota(jnp.int32, (seq, seq), 0)
         upto = (below <= lax.broadcasted_iota(jnp.int32, (seq, seq), 1)).astype(jnp.bfloat16)
         place_in = lax.broadcasted_iota(jnp.int32, (cap, seq), 0).astype(jnp.float32)
-        if t > 0:
+
+        @pl.when(t > 0)
+        def _():
             for save in self.saves(lev):
                 save.wait()
+
         for j in range(4):
             slot, at = lev * 4 + j, slice(j * cap, (j + 1) * cap)
-            turned = marked[slot].T
+            turned = self.marked[slot].T
             here = jnp.sum(jnp.where(below == self.place.chip, turned, 0.0), axis=0, keepdims=True)
             routed = jnp.where(here >= 0.0, 1.0, 0.0)
             order = fdot(jnp.broadcast_to(routed, (8, seq)).astype(jnp.bfloat16), upto)[:1] - 1.0
@@ -633,15 +682,19 @@
             weight = jnp.sum(hit * here, axis=-1, keepdims=True)
             pick = hit.astype(jnp.bfloat16)
             self.picks[slot] = pick
-            self.left[j, :cap] = pick
+            self.left[at, j * seq : (j + 1) * seq] = pick
             self.weight[at] = jnp.broadcast_to(weight, (cap, LANES))
-            for col in range(0, self.width, 512):
-                cols = slice(col, col + 512)
-                own = fdot(pick, self.gather.results[0][slot, :, cols])
-                self.rows[at, cols] = own.astype(jnp.bfloat16)
-                grad = fdot(pick, self.out_rows[slot, :, cols])
-                self.grads[at, cols] = grad.astype(jnp.bfloat16)
-                self.cot[at, cols] = (weight * grad).astype(jnp.bfloat16)
+        chosen, weight = self.left[: 4 * cap], self.weight[:, :1]
+
+        @pl.loop(0, self.width // 512, unroll=True)
+        def _(k):
+            cols, four = part_rows(k * 512, 512), pl.ds(lev * 4, 4)
+            own = fdot(chosen, self.tokens[four, :, cols].reshape(4 * seq, 512))
+            self.rows[:, cols] = own.astype(jnp.bfloat16)
+            grad = fdot(chosen, self.out_rows[four, :, cols].reshape(4 * seq, 512))
+            self.grads[:, cols] = grad.astype(jnp.bfloat16)
+            self.cot[:, cols] = (weight * grad).astype(jnp.bfloat16)
+
         for save in self.saves(lev):
             save.start()
 
@@ -650,8 +703,8 @@
         for start in range(0, self.hidden, chunk):
             cols = slice(start, min(start + chunk, self.hidden))
             shape = (4, self.capacity, cols.stop - cols.start)
-            gate = fdot(self.rows[...], self.gate[:, cols])
-            up = fdot(self.rows[...], self.up[:, cols])
+            gate = dot_nt(self.rows[...], self.gate[cols])
+            up = dot_nt(self.rows[...], self.up[cols])
             grad = dot_nt(self.cot[...], self.down[cols])
             sig = jax.nn.sigmoid(gate)
             gated = gate * sig
@@ -662,7 +715,7 @@
 
     def shared_units(self, lev):
         seq4, room = 4 * self.seq, self.room
-        tokens = self.gather.results[0][pl.ds(lev * 4, 4)].reshape(seq4, self.width)
+        tokens = self.tokens[pl.ds(lev * 4, 4)].reshape(seq4, self.width)
         grads = self.out_rows[pl.ds(lev * 4, 4)].reshape(seq4, self.width)
         both = dot_nt(self.shared_w[:2].reshape(2 * room, self.width), tokens)
         gate, up = both[:room], both[room:]
@@ -672,15 +725,17 @@
         gate_delta = (grad * up * (sig * (1.0 + gate * (1.0 - sig)))).astype(jnp.bfloat16)
         up_delta = (grad * gate * sig).astype(jnp.bfloat16)
         self.act_turn[:, part_rows(lev * seq4, seq4)] = act
-        for j in range(4):
-            at = slice(j * self.seq, (j + 1) * self.seq)
-            self.left[j, self.capacity : self.capacity + room] = gate_delta[:, at]
-            self.left[j, self.capacity + room :] = up_delta[:, at]
-        for col in range(0, self.width, 512):
-            cols = slice(col, col + 512)
-            self.total[0, :, cols] += fdot(gate_delta, tokens[:, cols])
-            self.total[1, :, cols] += fdot(up_delta, tokens[:, cols])
-            self.total[2, :, cols] += fdot(act, grads[:, cols])
+        self.left[4 * self.capacity : 4 * self.capacity + room] = gate_delta
+        self.left[4 * self.capacity + room :] = up_delta
+
+        @pl.loop(0, self.width // 512, unroll=True)
+        def _(k):
+            cols, four = part_rows(k * 512, 512), pl.ds(lev * 4, 4)
+            some = self.tokens[four, :, cols].reshape(seq4, 512)
+            self.total[0, :, cols] += fdot(gate_delta, some)
+            self.total[1, :, cols] += fdot(up_delta, some)
+            some = self.out_rows[four, :, cols].reshape(seq4, 512)
+            self.total[2, :, cols] += fdot(act, some)
 
     def outward(self, lev):
         slots, cap, count = pl.ds(lev * 4, 4), self.capacity, 4 * self.capacity
@@ -688,43 +743,54 @@
         gate_delta = self.gate_delta[slots].reshape(count, self.hidden)
         up_delta = self.up_delta[slots].reshape(count, self.hidden)
         weight = self.weight[:, :1]
-        route = jnp.zeros((count, 1), jnp.float32)
-        for col in range(0, self.width, 512):
-            cols = slice(col, col + 512)
+
+        def some(k, route):
+            cols = part_rows(k * 512, 512)
             out = fdot(act, self.down[:, cols]).astype(jnp.bfloat16).astype(jnp.float32)
             route += jnp.sum(out * self.grads[:, cols].astype(jnp.float32), axis=-1, keepdims=True)
             out = (weight * out).astype(jnp.bfloat16)
             self.out_block[slots, :, cols] = out.reshape(4, cap, 512)
-            back = dot_nt(gate_delta, self.gate[cols]) + dot_nt(up_delta, self.up[cols])
-            self.back[:, cols] = back.astype(jnp.bfloat16)
+            back = fdot(gate_delta, self.gate[:, cols]) + fdot(up_delta, self.up[:, cols])
+            self.held[:count, cols] = back.astype(jnp.bfloat16)
+            return route
+
+        route = lax.fori_loop(
+            0, self.width // 512, some, jnp.zeros((count, 1), jnp.float32), unroll=True
+        )
         lane = lax.broadcasted_iota(jnp.int32, (count, LANES), 1)
         routes = jnp.where(lane == self.place.chip, route, 0.0).astype(jnp.bfloat16)
-        for j in range(4):
-            slot, at = lev * 4 + j, slice(j * cap, (j + 1) * cap)
-            self.held[:cap] = self.back[at]
-            left = self.left[j]
-            for col in range(0, self.width, 512):
-                cols = slice(col, col + 512)
-                self.part[slot, :, cols] = dot_tn(left, self.held[:, cols]).astype(jnp.bfloat16)
-            self.part[slot, :, self.width :] = dot_tn(left[:cap], routes[at]).astype(jnp.bfloat16)
+        shape = (4, self.seq, LANES)
+        turned = dot_tn(self.left[:count], routes).astype(jnp.bfloat16)
+        self.part[slots, :, self.width :] = turned.reshape(shape)
+        left = self.left[...]
+
+        @pl.loop(0, self.width // 512, unroll=True)
+        def _(k):
+            cols = part_rows(k * 512, 512)
+            sums = dot_tn(left, self.held[:, cols]).astype(jnp.bfloat16)
+            self.part[slots, :, cols] = sums.reshape(4, self.seq, 512)
+
+    def compute(self, t):
+        lev = level_at(self.level, self.gather.planes, t)
+
+        @pl.when(t == 0)
+        def _():
+            for load in self.loads():
+                load.wait()
+
+        self.gather.receive(t)
+        self.choose(lev, t)
+        self.hidden_units(lev)
+        self.shared_units(lev)
 
     def advance(self, i):
-        if 0 <= i - 2 < self.gather.planes:
-            self.outward(level_at(self.level, self.gather.planes, i - 2))
-        if 0 <= i - 1 < self.gather.planes:
-            t = i - 1
-            lev = level_at(self.level, self.gather.planes, t)
-            if t == 0:
-                self.gather.landed = True
-                for load in self.loads():
-                    load.wait()
-            self.gather.receive(t)
-            self.choose(lev, t)
-            self.hidden_units(lev)
-            self.shared_units(lev)
-
-    def middle(self):
-        return [functools.partial(self.advance, i) for i in range(self.gather.planes + 2)]
+        planes = self.gather.planes
+        pl.when(i > 1)(lambda: self.outward(level_at(self.level, planes, i - 2)))
+        pl.when((i > 0) & (i < planes + 1))(lambda: self.compute(i - 1))
+
+    def segments(self):
+        self.gather.landed = True
+        return [(0, self.gather.planes + 2, self.advance)]
 
     def end(self):
         for save in self.saves(level_at(self.level, self.gather.planes, self.gather.planes - 1)):
@@ -768,11 +834,15 @@
     greet(place, ops)
     for op in ops:
         op.begin()
-    queues = [op.middle() for op in ops]
-    for i in range(max(len(q) for q in queues)):
-        for queue in queues:
-            if i < len(queue):
-                queue[i]()
+    parts = [part for op in ops for part in op.segments() if part[1] > 0]
+    if parts:
+
+        @pl.loop(0, max(start + count for start, count, _ in parts))
+        def _(r):
+            for start, count, call in parts:
+                inside = (r >= start) & (r < start + count)
+                pl.when(inside)(functools.partial(call, r - start))
+
     ended = [op.gains for op in ops if isinstance(op, NormGather)]
     for op in ops:
         if op not in ended:
@@ -1194,12 +1264,6 @@
     return whole and block % 64 == 0 and width == groups * LANES
 
 
-def masked_scores(query_rows, key_rows):
-    scores = fsum("sqd,skd->sqk", query_rows, key_rows) * DQK ** (-0.5)
-    places = jnp.arange(query_rows.shape[1], dtype=jnp.int32)
-    return jnp.where(places[None, None, :] <= places[None, :, None], scores, -1e30)
-
-
 def to_blocks(grad_rows, groups):
     rows, width = grad_rows.shape
     kept = lax.optimization_barrier(grad_rows.astype(jnp.bfloat16))
@@ -1328,7 +1392,7 @@
                     kv_w[down, across] = parts[j, start : start + lat_rows]
 
         def some(first):
-            rows = rows_in[first : first + fold].reshape(fold * seq_len, width)
+            rows = rows_in[pl.ds(first, fold)].reshape(fold * seq_len, width)
             query = dot_nt(rows, query_w[...])
             query_plain, query_turn = query[:, :DN].astype(bf16), rotated(query[:, DN:], cos_ref, sin_ref, 1.0)
             full = fdot(rows, lat_w[...])
@@ -1336,8 +1400,8 @@
             latent = (plain * rms_scale(plain) * kv_gain_ref[...]).astype(bf16)
             key_turn = rotated(full[:, lat_width:], cos_ref, sin_ref, 1.0)
             key_value = fdot(latent, kv_w[...]).astype(bf16)
-            latent_out[first : first + fold] = latent.reshape(fold, seq_len, lat_width)
-            lat_out[first : first + fold] = plain.reshape(fold, seq_len, lat_width)
+            latent_out[pl.ds(first, fold)] = latent.reshape(fold, seq_len, lat_width)
+            lat_out[pl.ds(first, fold)] = plain.reshape(fold, seq_len, lat_width)
             ahead = lax.broadcasted_iota(jnp.int32, (seq_len, seq_len), 1) > lax.broadcasted_iota(
                 jnp.int32, (seq_len, seq_len), 0
             )
@@ -1356,23 +1420,25 @@
                 key_out[seq, :, :DN], key_out[seq, :, DN:] = key_value[at, :DN], key_turn[at]
                 value_out[seq] = values
 
-        steps = [functools.partial(some, first) for first in range(0, heads, fold)]
-        return [assemble] + steps
+        def two(r):
+            pl.when(r == 0)(assemble)
+            pl.loop(0, 2)(lambda q: some((2 * r + q) * fold))
+
+        return heads // (2 * fold), two
 
     out_rows = out_grad.astype(bf16)
 
     def attn_part(part, slot, refs):
-        for col in range(0, width, 512):
-            product = fdot(refs[12][slot], refs[13][:, col : col + 512])
-            part[slot, :, col : col + 512] = product.astype(bf16)
+        @pl.loop(0, width // 512)
+        def _(k):
+            cols = part_rows(k * 512, 512)
+            part[slot, :, cols] = fdot(refs[12][slot], refs[13][:, cols]).astype(bf16)
 
     def shaped(last, kind):
         return jax.ShapeDtypeStruct((heads, seq_len, last), kind)
 
-    (out_all,), (shared_got,), attended = exchange(
+    attended, (shared_got,) = exchange(
         [
-            Gather([out_rows], all_planes),
-            Swap(shared_parts),
             Reduce(
                 [normed1_all, got, latent_w, gain_kv[None, :], turn_cos, turn_sin],
                 attn_part,
@@ -1393,14 +1459,12 @@
                 ],
                 prelude=attend_forward,
             ),
+            Swap(shared_parts, pace=3),
         ],
         2,
     )
     attn_sum, query_rows, key_rows, value_rows, att_probs, lat_plain, latent, mixed = attended[:8]
     output_w, query_wt, kvup_w = attended[8:]
-    mixed_flat = mixed.reshape(heads * seq_len, DV)
-    normed1_all = normed1_all.reshape(heads * seq_len, width)
-    latent = latent.reshape(heads * seq_len, lat_width)
 
     gate_sht = from_blocks(shared_got[:, :hidden])
     up_sht = from_blocks(shared_got[:, hidden : 2 * hidden])
@@ -1419,11 +1483,10 @@
     def stacked(blocks):
         return jnp.pad(blocks, [(0, room - hidden), (0, 0)])
 
-    token_gather = Gather([normed2, marked], all_planes, True)
+    token_gather = Gather([normed2, out_rows, marked], all_planes, True)
     experts_op = Experts(
         token_gather,
-        out_all,
-        [expert_gate[0], expert_up[0], expert_down[0]],
+        [expert_gate[0].T, expert_up[0].T, expert_down[0]],
         jnp.stack([stacked(gate_sht), stacked(up_sht), stacked(down_sh)]),
         capacity,
     )
@@ -1447,14 +1510,11 @@
     def expert_part(part, slot, refs):
         left, own, held = refs[0], refs[1], refs[-1]
         held[:capacity] = own[slot]
-        for col in range(0, width, 512):
-            product = lax.dot_general(
-                left[slot],
-                held[:, col : col + 512],
-                (((0,), (0,)), ((), ())),
-                preferred_element_type=jnp.float32,
-            )
-            part[slot, :, col : col + 512] = product.astype(bf16)
+
+        @pl.loop(0, width // 512)
+        def _(k):
+            cols = part_rows(k * 512, 512)
+            part[slot, :, cols] = dot_tn(left[slot], held[:, cols]).astype(bf16)
 
     def hold_shared(refs):
         refs[-1][capacity:] = refs[2][...]
@@ -1483,10 +1543,14 @@
         query_to, kv_to, turn_to = refs[9:]
         place, hidden_in = hidden_gather.place, hidden_gather.results[0]
 
-        def some(level, first, second, own):
-            slots = [level * 4 + first, level * 4 + second]
-            hidden_gather.ready(slots[0], not own)
-            hidden_gather.ready(slots[1], True)
+        def some(r):
+            level = lax.rem(hidden_gather.level + r // 2, planes)
+            first = level * 4 + place.spot(3 - 2 * lax.rem(r, 2))
+            second = level * 4 + place.spot(2 - 2 * lax.rem(r, 2))
+            slots = [first, second]
+            pl.when(r == 0)(lambda: hidden_gather.ready(first, False))
+            pl.when(r > 0)(lambda: hidden_gather.ready(first, True))
+            hidden_gather.ready(second, True)
             rows = jnp.concatenate([hidden_in[slot] for slot in slots], axis=0)
             mixed_grads = dot_nt(rows, out_w[...]).astype(bf16)
             for k in range(2):
@@ -1506,34 +1570,22 @@
                 turn_to[slot, :, :DR] = key_grad[:, DN:].astype(bf16)
                 turn_to[slot, :, DR:] = jnp.zeros((seq_len, LANES - DR), bf16)
 
-        level, calls = hidden_gather.level, []
         hidden_gather.landed = True
-        for far in range(planes):
-            where = lax.rem(level + far, planes)
-            calls.append(functools.partial(some, where, place.here, place.there_x, far == 0))
-            calls.append(functools.partial(some, where, place.there_y, place.across, False))
-        return calls
+        return 2 * planes, some
 
     def back_part(part, slot, refs):
-        for col in range(0, width, 512):
-            product = fdot(refs[9][slot], refs[7][:, col : col + 512])
-            part[slot, :, col : col + 512] = product.astype(bf16)
+        @pl.loop(0, width // 512)
+        def _(k):
+            cols = part_rows(k * 512, 512)
+            part[slot, :, cols] = fdot(refs[9][slot], refs[7][:, cols]).astype(bf16)
+
         product = dot_nt(refs[10][slot], refs[8][...])
         part[slot, :, width : width + lat_width] = product.astype(bf16)
         part[slot, :, width + lat_width :] = refs[11][slot]
 
-    ((hidden_all,), (out_sum,), (back, query_delta, kv_delta), (owned_early,)) = exchange(
+    (hidden_all,), (back, query_delta, kv_delta), (owned_early,) = exchange(
         [
             hidden_gather,
-            Reduce(
-                [out_left, out_block, stacked(down_sh)],
-                expert_part,
-                groups,
-                seq_len,
-                width,
-                [pltpu.VMEM((capacity + room, width), bf16)],
-                hold_shared,
-            ),
             Reduce(
                 [
                     query_rows,
@@ -1559,9 +1611,6 @@
         ],
         5,
     )
-    layer_out = hidden_state + out_sum
-    hidden_all = hidden_all.reshape(heads * seq_len, width)
-    o_grad = fdot(lax.optimization_barrier(mixed_flat.T), hidden_all)
     normed1_query = back[:, :width]
     latent_grad = back[:, width : width + lat_width]
     rot_sum = back[:, width + lat_width : width + lat_width + DR]
@@ -1577,27 +1626,6 @@
     latent_delta = jnp.concatenate(
         [latent_back, rotate_back(rot_sum, cosine, sine_part)], axis=-1
     ).astype(bf16)
-    query_delta_t = lax.optimization_barrier(query_delta.reshape(heads * seq_len, DQK).T)
-    kv_flat = kv_delta.reshape(heads * seq_len, DN + DV)
-    latent_t = lax.optimization_barrier(latent.T)
-    kvb_blocks = (
-        lax.optimization_barrier(fdot(latent_t, kv_flat).astype(bf16))
-        .reshape(groups, lat_rows, kv_halves, own_cols)
-        .transpose(0, 2, 1, 3)
-        .reshape(groups, kv_block, own_cols)
-    )
-    head_grads = jnp.concatenate(
-        [
-            to_blocks(fdot(query_delta_t, normed1_all), groups),
-            kvb_blocks,
-            to_blocks(o_grad, groups),
-        ],
-        axis=1,
-    )
-    (latent_delta_all,), (owned_heads,) = exchange(
-        [Gather([latent_delta], planes), Swap(head_grads, pace=4)], 7
-    )
-    latent_delta_all = latent_delta_all.reshape(heads * seq_len, -1)
     normed1_grad = normed1_query + fsum("tl,dl->td", latent_delta, latent_w)
     norm1_gain_grad = jnp.sum(normed1_grad * unit_one, axis=0)
     scaled_one = normed1_grad * gain_one
@@ -1605,9 +1633,7 @@
         scaled_one - unit_one * jnp.mean(scaled_one * unit_one, axis=-1, keepdims=True)
     )
 
-    share = latent_delta_all.shape[1] // heads
-    latent_share = lax.dynamic_slice_in_dim(latent_delta_all, head * share, share, 1)
-    kva_blocks = to_blocks(fdot(lax.optimization_barrier(latent_share.T), normed1_all), groups)
+    share = (lat_width + DR) // heads
 
     def by_owner(row):
         return widen(row.reshape(groups, 1, -1), own_cols)
@@ -1622,8 +1648,94 @@
         axis=1,
     )
     small_grads = jnp.pad(small_grads, [(0, 0), (0, -small_grads.shape[1] % 8), (0, 0)])
-    kva_blocks = jnp.pad(kva_blocks, [(0, 0), (0, -share % 16), (0, 0)])
-    (owned_share,), (owned_small,) = exchange([Swap(kva_blocks), Swap(small_grads)], 8)
+
+    def make_head_grads(op):
+        query_ref, rows_ref, mixed_ref, hidden_ref, latent_ref, kv_ref = op.refs
+        tokens = heads * seq_len
+
+        def projections(_):
+            queries = query_ref[...].reshape(tokens, DQK)
+            mixed_rows = mixed_ref[...].reshape(tokens, DV)
+
+            @pl.loop(0, width // 512)
+            def _(part):
+                cols, first = part_rows(part * 512, 512), part * (512 // own_cols)
+                rows = rows_ref[:, :, cols].reshape(tokens, 512)
+                hidden_part = hidden_ref[:, :, cols].reshape(tokens, 512)
+                of_query = dot_tn(queries, rows).astype(bf16)
+                of_out = dot_tn(mixed_rows, hidden_part).astype(bf16)
+                for k in range(512 // own_cols):
+                    at = slice(k * own_cols, (k + 1) * own_cols)
+                    op.source[first + k, :at_kv] = of_query[:, at]
+                    op.source[first + k, at_o:at_gate] = of_out[:, at]
+
+        def latents(_):
+            lat = latent_ref[...].reshape(tokens, lat_width)
+            of_kv = dot_tn(lat, kv_ref[...].reshape(tokens, DN + DV)).astype(bf16)
+            for j in range(groups):
+                for half in range(kv_halves):
+                    start = at_kv + half * lat_rows
+                    block = of_kv[
+                        j * lat_rows : (j + 1) * lat_rows, half * own_cols : (half + 1) * own_cols
+                    ]
+                    op.source[j, start : start + lat_rows] = block
+
+        return [projections, latents]
+
+    latent_gather = Gather([latent_delta], planes, True)
+    head_swap = MadeSwap(
+        [query_delta, normed1_all, mixed, hidden_all, latent, kv_delta],
+        (groups, at_gate, own_cols),
+        make_head_grads,
+        0,
+        4,
+    )
+
+    def make_latent_grads(op):
+        def product(_):
+            pl.loop(0, planes)(latent_gather.receive)
+            deltas = latent_gather.results[0][...].reshape(heads * seq_len, lat_width + DR)
+
+            @pl.loop(0, width // 512)
+            def _(part):
+                cols = part_rows(part * 512, 512)
+                rows = head_swap.refs[1][:, :, cols].reshape(heads * seq_len, 512)
+                op.extra[0][:, cols] = dot_tn(deltas, rows)
+
+            first = lax.rem(op.place.chip, heads) * share
+            mine = op.extra[0][pl.ds(pl.multiple_of(first, 8), share), :].astype(bf16)
+            for j in range(groups):
+                op.source[j] = mine[:, j * own_cols : (j + 1) * own_cols]
+
+        latent_gather.landed = True
+        return [product]
+
+    (latent_delta_all,), (out_sum,), (owned_heads,), (owned_small,), (owned_share,) = exchange(
+        [
+            latent_gather,
+            Reduce(
+                [out_left, out_block, stacked(down_sh)],
+                expert_part,
+                groups,
+                seq_len,
+                width,
+                [pltpu.VMEM((capacity + room, width), bf16)],
+                hold_shared,
+            ),
+            head_swap,
+            Swap(small_grads, pace=5),
+            MadeSwap(
+                [],
+                (groups, share, own_cols),
+                make_latent_grads,
+                planes + 1,
+                groups,
+                [pltpu.VMEM((lat_width + DR, width), jnp.float32)],
+            ),
+        ],
+        6,
+    )
+    layer_out = hidden_state + out_sum
     small_sums = jnp.sum(owned_small, axis=0)
 
     def over_copies(blocks):

time: 580 us -> 536 us (0.924); the launches traced: 569 us -> 535 us
  local copies, waits for them, and re-layouts: 40.5 us -> 27 us
  matrix products: 35.4 us -> 26 us
  Pallas kernels: 465 us -> 457 us
    dot_general x5 -> x1, matrix products: 11.8 us -> 2.46 us  [fdot(): return jnp.dot(left, right, preferred_element_type=jnp.float32)]
    unnamed x65, local copies, waits for them, and re-layouts: 16.7 us -> 8.51 us
    pallas_call x7 -> x6, Pallas kernels: 465 us -> 457 us  [exchange(): pl.pallas_call(functools.partial(chip_kernel, ops), out_shape=[shape for...]
where the time goes in v4:
time: 536 us; the launch traced here: 535 us
  Pallas kernels  457 us (85%)
  local copies, waits for them, and re-layouts  27 us (5%)
  matrix products  26 us (5%)
  other arithmetic  23.3 us (4%)
    pallas_call x6, Pallas kernels, exchange(): pl.pallas_call(functools.partial(chip_kernel, ops), out_shape=[shape for...  457 us
    dot_general x6, matrix products, fsum(): return jnp.einsum(spec, left, right, preferred_element_type=jnp.float32)  23.5 us

profile of v4, /device:TPU:0, one launch (start us, length us, event | category | flops | bytes accessed | tf_op | source)
XLA Modules:
  0.0 534.7 jit_solution(9263298122617291488)
XLA Ops:
  1.8 1.2 copy.100
  4.1 1.4 tile.4
  7.1 64.7 %shard_map.288 = (bf16[16,32,128]{2,1,0:T(8,128)(2,1)}, bf16[16,128,576]{2,1,0:T(8,128)(2,1)}, bf16[16,384,128]{2,1,0:T(8,128)(2,1)}, bf16[8,128,2048]{2,1,0:T(8,128)(2,1)}) custom-call(bf16[16,32,128]{2,1,0:T(8,128)(2,1)} %broadcast_in_dim.21.refs_0_, bf16[128,576]{1,0:T(8,128)(2,1)} %copy.102.refs_1_, bf16[16,384,128]{2,1,0:T(8,128)(2,1)} %bitcast.152, ...), custom_call_target="tpu_custom_call" | custom-call | bytes 11157504 | tf_op jit(solution)/shard_map/pallas_call | solution.py:856
  74.8 60.9 %shard_map.289 = (f32[128,2048]{1,0:T(8,128)}, bf16[8,128,192]{2,1,0:T(8,128)(2,1)}, bf16[8,128,192]{2,1,0:T(8,128)(2,1)}, bf16[8,128,128]{2,1,0:T(8,128)(2,1)},...) custom-call(bf16[8,128,2048]{2,1,0:T(8,128)(2,1)} %get-tuple-element, ...), custom_call_target="tpu_custom_call" | custom-call | bytes 17958912 | tf_op jit(solution)/shard_map/pallas_call | solution.py:856
  135.8 1.5 multiply_reduce_fusion.5
  139.0 1.3 slice_bitcast_fusion.2
  143.7 111.6 %shard_map.290 = (bf16[16,128,2048]{2,1,0:T(8,128)(2,1)}, bf16[16,128,2048]{2,1,0:T(8,128)(2,1)}, f32[16,128,128]{2,1,0:T(8,128)}, bf16[16,128,2176]{2,1,0:T(8,1...) custom-call(bf16[128,2048]{1,0:T(8,128)(2,1)} %copy-done.1, ...), custom_call_target="tpu_custom_call" | custom-call | bytes 56426496 | tf_op jit(solution)/shard_map/pallas_call | solution.py:856
  255.4 8.5 %convolution_bitcast_fusion.2 = f32[1,704,2048]{2,1,0:T(8,128)} fusion(bf16[16,64,704]{2,1,0:T(8,128)(2,1)} %get-tuple-element.84, bf16[16,64,2048]{2,1,0:T(8,128)(2,1)} %get-tuple-element.85), kind=kOutput, calls=%fused_computation.2 | convolution fusion | flops 2952790016 | bytes 11403264 | tf_op jit(solution)/shard_map/mf,md->fd/dot_general | solution.py:71
  263.9 5.1 convolution_bitcast_fusion
  269.0 5.1 convolution_bitcast_fusion.1
  274.1 51.4 %shard_map.291 = f32[128,2176]{1,0:T(8,128)} custom-call(bf16[16,128,2176]{2,1,0:T(8,128)(2,1)} %get-tuple-element.58.refs_0_), custom_call_target="tpu_custom_call" | custom-call | bytes 10027008 | tf_op jit(solution)/shard_map/pallas_call | solution.py:856
  327.7 2.5 multiply_reduce_fusion.1
  330.2 1.5 fusion.13
  332.0 1.3 copy.144
  333.3 75.0 %shard_map.292 = (bf16[8,128,2048]{2,1,0:T(8,128)(2,1)}, f32[128,2688]{1,0:T(8,128)}, bf16[8,128,192]{2,1,0:T(8,128)(2,1)}, bf16[8,128,256]{2,1,0:T(8,128)(2,1)}, bf16[16,264,128]{2,1,0:T(8,128)(2,1)}) custom-call(bf16[128,2048]{1,0:T(8,128)(2,1)} %get-tuple-element.156.refs_0_, bf16[8,128,192]{2,1,0:T(8,128)(2,1)} %get-tuple-element.59.refs_1_, ...), custom_call_target="tpu_custom_call" | custom-call | bytes 12386304 | tf_op jit(solution)/shard_map/pallas_call | solution.py:856
  410.3 1.3 multiply_reduce_fusion.6
  412.8 1.2 subtract_convert_fusion
  414.2 3.4 multiply_reduce_fusion
  419.5 1.8 pad_maximum_fusion.3.refs_1_
  421.3 93.5 %shard_map.293 = (bf16[8,128,576]{2,1,0:T(8,128)(2,1)}, f32[128,2048]{1,0:T(8,128)}, bf16[16,384,128]{2,1,0:T(8,128)(2,1)}, f32[16,24,128]{2,1,0:T(8,128)}, bf16[16,72,128]{2,1,0:T(8,128)(2,1)}) custom-call(bf16[128,576]{1,0:T(8,128)(2,1)} %copy-done.8, bf16[16,160,128]{2,1,0:T(8,128)(2,1)} %pad_maximum_fusion.3.refs_1_, ...), custom_call_target="tpu_custom_call" | custom-call | bytes 20496384 | tf_op jit(solution)/shard_map/pallas_call | solution.py:856
  514.8 1.9 convert_reduce_fusion
  518.8 2.3 copy.118
  522.0 1.9 reshape.237
  523.9 2.6 multiply_add_fusion
  (125 shorter events, 30.5 us)
Async XLA Ops:
  0.6 3.4 copy-start.15
  4.1 2.3 copy-start.20
  4.1 2.3 copy-start.23
  4.1 2.3 copy-start.24
  4.1 2.3 copy-start.25
  6.4 66.9 %copy-start.11 = (bf16[128,1408]{1,0:T(8,128)(2,1)S(1)}, bf16[128,1408]{1,0:T(8,128)(2,1)}, u32[]{:S(2)}) copy-start(bf16[128,1408]{1,0:T(8,128)(2,1)} %param.26) | copy-start | bytes 1081348
  7.1 66.4 %copy-start.12 = (bf16[128,1408]{1,0:T(8,128)(2,1)S(1)}, bf16[128,1408]{1,0:T(8,128)(2,1)}, u32[]{:S(2)}) copy-start(bf16[128,1408]{1,0:T(8,128)(2,1)} %param.27) | copy-start | bytes 1081348
  7.1 66.6 %copy-start.13 = (bf16[1408,128]{1,0:T(8,128)(2,1)S(1)}, bf16[1408,128]{1,0:T(8,128)(2,1)}, u32[]{:S(2)}) copy-start(bf16[1408,128]{1,0:T(8,128)(2,1)} %param.28) | copy-start | bytes 1081348
  74.8 60.9 %copy-start = (f32[128,2048]{1,0:T(8,128)S(1)}, f32[128,2048]{1,0:T(8,128)}, u32[]{:S(2)}) copy-start(f32[128,2048]{1,0:T(8,128)} %refs_3_.1) | copy-start | bytes 3145732
  135.7 1.6 copy-start.18
  137.5 2.8 copy-start.1
  141.3 1.5 copy-start.6
  255.4 8.6 %copy-start.26 = (bf16[16,64,2048]{2,1,0:T(8,128)(2,1)S(1)}, bf16[16,64,2048]{2,1,0:T(8,128)(2,1)}, u32[]{:S(2)}) copy-start(bf16[16,64,2048]{2,1,0:T(8,128)(2,1)} %get-tuple-element.81) | copy-start | bytes 12582916
  255.4 8.6 %copy-start.28 = (bf16[16,64,704]{2,1,0:T(8,128)(2,1)S(1)}, bf16[16,64,704]{2,1,0:T(8,128)(2,1)}, u32[]{:S(2)}) copy-start(bf16[16,64,704]{2,1,0:T(8,128)(2,1)} %get-tuple-element.83) | copy-start | bytes 4325380
  263.9 5.1 copy-start.27
  274.1 52.5 %copy-start.2 = (bf16[128,2048]{1,0:T(8,128)(2,1)S(1)}, bf16[128,2048]{1,0:T(8,128)(2,1)}, u32[]{:S(2)}) copy-start(bf16[128,2048]{1,0:T(8,128)(2,1)} %copy-done.1) | copy-start | bytes 1572868
  410.3 3.9 copy-start.7
  414.1 3.5 copy-start.8
  414.2 3.5 copy-start.19
  518.8 2.3 slice-start
  518.8 5.1 copy-start.22
  523.9 2.6 copy-start.4
  527.9 1.8 copy-start.16
  527.9 3.5 copy-start.5
  (6 other events, 7.4 us)

commit v5 on v4

--- a/solution.py
+++ b/solution.py
@@ -121,7 +121,7 @@
 
 
 class Swap:
-    reach = 0
+    reach, lazy = 0, False
 
     def __init__(self, blocks, vmem_result=False, pace=2):
         groups = blocks.shape[0]
@@ -195,15 +195,22 @@
         self.refs, self.extra = ins, scratch[4:]
 
     def begin(self):
-        pass
+        if self.delay is None:
+            for call in self.make(self):
+                call(0)
+            super().begin()
 
     def segments(self):
+        if self.delay is None:
+            return self.rest(0)
         calls = self.make(self) + [lambda i: super(MadeSwap, self).begin()]
         parts = [(self.delay + k, 1, call) for k, call in enumerate(calls)]
         return parts + self.rest(self.delay + len(calls))
 
 
 class Gather:
+    lazy = False
+
     def __init__(self, arrays, planes, vmem_result=False):
         count, slots = len(arrays), planes * 4
         self.planes, self.count, self.reach = planes, count, planes
@@ -393,7 +400,7 @@
         self.outs = [(jax.ShapeDtypeStruct((block, width), jnp.float32), pltpu.VMEM)]
         self.outs += [(shape, pltpu.VMEM) for shape in extra]
         self.own_scratch, self.produce, self.prepare = len(scratch), produce, prepare
-        self.prelude, self.delay = prelude, delay
+        self.prelude, self.delay, self.lazy = prelude, delay, prelude is not None
         by_level = DMA((planes,))
         self.scratch = (
             list(scratch)
@@ -593,6 +600,8 @@
 
 
 class Experts:
+    lazy = False
+
     def __init__(self, gather, weights, shared_w, capacity):
         slots, seq, width = gather.outs[0][0].shape
         hidden, room, bf16 = weights[0].shape[0], shared_w.shape[1], jnp.bfloat16
@@ -606,15 +615,18 @@
 
         self.ins = [(a, pl.ANY) for a in weights] + [(shared_w, pltpu.VMEM)]
         self.outs = [
-            (shape((slots, seq, width + LANES)), pltpu.VMEM),
-            (shape(rows + (width,)), pltpu.VMEM),
+            (shape((slots, seq, width + LANES)), pl.ANY),
+            (shape(rows + (width,)), pl.ANY),
             (shape(rows + (seq,)), pltpu.VMEM),
             (shape(turn), pltpu.VMEM),
             (shape((3, room, width)), pltpu.VMEM),
             (shape(rows + (width,)), pl.ANY),
             (shape(rows + (width,)), pl.ANY),
-        ] + [(shape(rows + (hidden,)), pltpu.VMEM)] * 3
-        self.scratch = (
+        ] + [(shape(rows + (hidden,)), pl.ANY)] * 3
+        staged = [self.outs[k][0] for k in (0, 1, 7, 8, 9)]
+        self.scratch = [pltpu.VMEM(x.shape, bf16) for x in staged]
+        self.scratch += [DMA((len(staged), gather.planes))]
+        self.scratch += (
             [pltpu.VMEM(w.shape, bf16) for w in weights]
             + [pltpu.VMEM((4 * capacity, width), bf16)] * 3
             + [
@@ -631,8 +643,10 @@
         self.place = place
         self.hbm_weights, self.shared_w = ins[:3], ins[3]
         self.tokens, self.out_rows, self.marked = self.gather.results
-        self.part, self.out_block, self.picks, self.act_turn, self.shared_grads = outs[:5]
-        self.rows_hbm, self.cot_hbm, self.act, self.gate_delta, self.up_delta = outs[5:]
+        self.picks, self.act_turn, self.shared_grads, self.rows_hbm, self.cot_hbm = outs[2:7]
+        self.staged, self.leave_sem, scratch = scratch[:5], scratch[5], scratch[6:]
+        self.part, self.out_block, self.act, self.gate_delta, self.up_delta = self.staged
+        self.final = list(outs[:2]) + list(outs[7:])
         self.gate, self.up, self.down = scratch[:3]
         self.rows, self.cot, self.grads = scratch[3:6]
         self.weight, self.held, self.left, self.total, self.load_sem, self.save_sem = scratch[6:]
@@ -770,6 +784,16 @@
             sums = dot_tn(left, self.held[:, cols]).astype(jnp.bfloat16)
             self.part[slots, :, cols] = sums.reshape(4, self.seq, 512)
 
+        for copy in self.leaving(lev):
+            copy.start()
+
+    def leaving(self, lev):
+        four = pl.ds(lev * 4, 4)
+        return [
+            pltpu.make_async_copy(src.at[four], dst.at[four], self.leave_sem.at[k, lev])
+            for k, (src, dst) in enumerate(zip(self.staged, self.final))
+        ]
+
     def compute(self, t):
         lev = level_at(self.level, self.gather.planes, t)
 
@@ -796,6 +820,11 @@
         for save in self.saves(level_at(self.level, self.gather.planes, self.gather.planes - 1)):
             save.wait()
         self.shared_grads[...] = self.total[...].astype(jnp.bfloat16)
+
+        @pl.loop(0, self.gather.planes)
+        def _(lev):
+            for copy in self.leaving(lev):
+                copy.wait()
 
 
 def greet(place, ops):
@@ -822,19 +851,46 @@
     pl.semaphore_wait(barrier, expected)
 
 
+def is_large(pair):
+    array, space = pair
+    return space == pltpu.VMEM and array.size * array.dtype.itemsize >= 1 << 17
+
+
 def chip_kernel(ops, *refs):
     place = Place()
-    n_in = sum(len(op.ins) for op in ops)
+    pairs = [pair for op in ops for pair in op.ins]
+    n_in, large = len(pairs), [k for k, pair in enumerate(pairs) if is_large(pair)]
     n_out = sum(len(op.outs) for op in ops)
-    ins, outs, scratch = refs[:n_in], refs[n_in : n_in + n_out], refs[n_in + n_out :]
+    ins, outs, scratch = list(refs[:n_in]), refs[n_in : n_in + n_out], refs[n_in + n_out :]
+    loads = {}
+    for n, k in enumerate(large):
+        loads[k] = pltpu.make_async_copy(ins[k], scratch[n], scratch[len(large)].at[n])
+        loads[k].start()
+        ins[k] = scratch[n]
+    scratch = scratch[len(large) + 1 :]
+    first = 0
     for op in ops:
+        op.fetches = [loads[k] for k in range(first, first + len(op.ins)) if k in loads]
+        first += len(op.ins)
         op.bind(place, ins[: len(op.ins)], outs[: len(op.outs)], scratch[: len(op.scratch)])
         ins, outs = ins[len(op.ins) :], outs[len(op.outs) :]
         scratch = scratch[len(op.scratch) :]
     greet(place, ops)
+
+
+    def load(op):
+        for copy in op.fetches:
+            copy.wait()
+
+    parts = []
     for op in ops:
+        segments = [part for part in op.segments() if part[1] > 0]
+        if op.lazy:
+            parts.append((min(start for start, _, _ in segments), 1, lambda _, op=op: load(op)))
+        else:
+            load(op)
         op.begin()
-    parts = [part for op in ops for part in op.segments() if part[1] > 0]
+        parts += segments
     if parts:
 
         @pl.loop(0, max(start + count for start, count, _ in parts))
@@ -853,12 +909,15 @@
     ins = [pair for op in ops for pair in op.ins]
     outs = [pair for op in ops for pair in op.outs]
     moved = sum(a.size * a.dtype.itemsize for a, _ in ins + outs)
+    large = [pair[0] for pair in ins if is_large(pair)]
+    spaces = [pl.ANY if is_large(pair) else pair[1] for pair in ins]
+    held = [pltpu.VMEM(a.shape, a.dtype) for a in large] + [DMA((max(1, len(large)),))]
     results = pl.pallas_call(
         functools.partial(chip_kernel, ops),
         out_shape=[shape for shape, _ in outs],
-        in_specs=[pl.BlockSpec(memory_space=space) for _, space in ins],
+        in_specs=[pl.BlockSpec(memory_space=space) for space in spaces],
         out_specs=[pl.BlockSpec(memory_space=space) for _, space in outs],
-        scratch_shapes=[entry for op in ops for entry in op.scratch],
+        scratch_shapes=held + [entry for op in ops for entry in op.scratch],
         compiler_params=pltpu.CompilerParams(
             collective_id=ident, has_side_effects=True, vmem_limit_bytes=60 << 20
         ),
@@ -869,6 +928,94 @@
         split.append(results[: len(op.outs)])
         results = results[len(op.outs) :]
     return split
+
+
+def grads_kernel(act, gate_delta, up_delta, rows, cot, gate_out, up_out, down_out):
+    gate_out[...] = dot_tn(gate_delta[...], rows[...])
+    up_out[...] = dot_tn(up_delta[...], rows[...])
+    down_out[...] = dot_tn(act[...], cot[...])
+
+
+def expert_weight_grads(act, gate_delta, up_delta, rows, cot):
+    count, hidden = act.shape
+    width, tile = rows.shape[1], 256
+    left = pl.BlockSpec((count, hidden), lambda i: (0, 0), pipeline_mode=pl.Buffered(1))
+    right = pl.BlockSpec((count, tile), lambda i: (0, i))
+    return pl.pallas_call(
+        grads_kernel,
+        grid=(width // tile,),
+        out_shape=[jax.ShapeDtypeStruct((hidden, width), jnp.float32)] * 3,
+        in_specs=[left] * 3 + [right] * 2,
+        out_specs=[pl.BlockSpec((hidden, tile), lambda i: (0, i))] * 3,
+        compiler_params=pltpu.CompilerParams(vmem_limit_bytes=48 << 20),
+        cost_estimate=pl.CostEstimate(
+            flops=6 * count * hidden * width,
+            bytes_accessed=12 * hidden * width + 4 * count * width,
+            transcendentals=0,
+        ),
+    )(act, gate_delta, up_delta, rows, cot)
+
+
+def finish_kernel(sizes, heads_in, shared_in, share_in, small_in, state, added, *refs):
+    heads, at_kv, at_o, lat_rows, hidden, share = sizes
+    layer_out, q_out, kvb_out, o_out, gate_out, up_out, down_out, kva_out, small_out = refs[:9]
+    q_turn, gate_turn, up_turn = refs[9:]
+    groups, own_cols = heads_in.shape[0], heads_in.shape[2]
+    copies = range(0, groups, heads)
+
+    def over_copies(ref, k):
+        return sum(ref[first + k].astype(jnp.float32) for first in copies)
+
+    layer_out[...] = state[...] + added[...]
+    small_out[...] = sum(small_in[j] for j in range(groups))
+    for k in range(heads):
+        block = over_copies(heads_in, k)
+        q_turn[k * at_kv : (k + 1) * at_kv] = block[:at_kv]
+        halves = (at_o - at_kv) // lat_rows
+        for half in range(halves):
+            start, col = at_kv + half * lat_rows, (k * halves + half) * own_cols
+            kvb_out[:, col : col + own_cols] = block[start : start + lat_rows]
+        wide = block.shape[0] - at_o
+        o_out[k * wide : (k + 1) * wide] = block[at_o:]
+        kva_out[k * share : (k + 1) * share] = over_copies(share_in, k)
+    for j in range(groups):
+        block, at = shared_in[j].astype(jnp.float32), slice(j * hidden, (j + 1) * hidden)
+        gate_turn[at] = block[:hidden]
+        up_turn[at] = block[hidden : 2 * hidden]
+        down_out[at] = block[2 * hidden :]
+    q_out[...] = q_turn[...].T
+    gate_out[...] = gate_turn[...].T
+    up_out[...] = up_turn[...].T
+
+
+def finish(sizes, heads_in, shared_in, share_in, small_in, state, added):
+    heads, at_kv, at_o, lat_rows, hidden, share = sizes
+    groups, rows, own_cols = heads_in.shape
+    many = groups * hidden
+
+    def shape(*dims):
+        return jax.ShapeDtypeStruct(dims, jnp.float32)
+
+    outs = [
+        shape(*state.shape),
+        shape(own_cols, heads * at_kv),
+        shape(lat_rows, heads * (at_o - at_kv) // lat_rows * own_cols),
+        shape(heads * (rows - at_o), own_cols),
+        shape(own_cols, many),
+        shape(own_cols, many),
+        shape(many, own_cols),
+        shape(heads * share, own_cols),
+        shape(*small_in.shape[1:]),
+    ]
+    turned = [(heads * at_kv, own_cols), (many, own_cols), (many, own_cols)]
+    return pl.pallas_call(
+        functools.partial(finish_kernel, sizes),
+        out_shape=outs,
+        in_specs=[pl.BlockSpec(memory_space=pltpu.VMEM)] * 6,
+        out_specs=[pl.BlockSpec(memory_space=pltpu.VMEM)] * len(outs),
+        scratch_shapes=[pltpu.VMEM(dims, jnp.float32) for dims in turned],
+        compiler_params=pltpu.CompilerParams(vmem_limit_bytes=32 << 20),
+    )(heads_in, shared_in, share_in, small_in, state, added)
 
 
 def general_scores(query_blk, key_rows, first_row):
@@ -1495,9 +1642,11 @@
     rows_in, cot_in, expert_act, gate_delta, up_delta = (
         x.reshape(groups * capacity, -1) for x in expert_results[5:]
     )
-    expert_down_grad = fsum("mf,md->fd", expert_act, cot_in)[None]
-    expert_gate_grad = fsum("md,mf->df", rows_in, gate_delta)[None]
-    expert_up_grad = fsum("md,mf->df", rows_in, up_delta)[None]
+    gate_grad_turn, up_grad_turn, down_grad = expert_weight_grads(
+        expert_act, gate_delta, up_delta, rows_in, cot_in
+    )
+    expert_gate_grad, expert_up_grad = gate_grad_turn.T[None], up_grad_turn.T[None]
+    expert_down_grad = down_grad[None]
     shared_grads = (
         shared_sums[:, :hidden]
         .reshape(3 * hidden, groups, own_cols)
@@ -1687,8 +1836,8 @@
         [query_delta, normed1_all, mixed, hidden_all, latent, kv_delta],
         (groups, at_gate, own_cols),
         make_head_grads,
-        0,
-        4,
+        None,
+        5,
     )
 
     def make_latent_grads(op):
@@ -1735,32 +1884,26 @@
         ],
         6,
     )
-    layer_out = hidden_state + out_sum
-    small_sums = jnp.sum(owned_small, axis=0)
-
-    def over_copies(blocks):
-        blocks = blocks.astype(jnp.float32).reshape((copies, heads) + blocks.shape[1:])
-        return jnp.sum(blocks, axis=0)
-
-    of_heads = over_copies(owned_heads)
-    q_grad = of_heads[:, :at_kv].transpose(2, 0, 1).reshape(own_cols, heads * DQK)
-    kvb_grad = (
-        of_heads[:, at_kv:at_o]
-        .reshape(heads, kv_halves, lat_rows, own_cols)
-        .transpose(2, 0, 1, 3)
-        .reshape(lat_rows, heads * (DN + DV))
-    )
-    own_o_grad = of_heads[:, at_o:].reshape(heads * DV, own_cols)
-    kva_grad = over_copies(owned_share)[:, :share].reshape(heads * share, own_cols).T
-    of_shared = owned_early[:, : 3 * hidden].astype(jnp.float32)
-
-    def columns(blocks):
-        return blocks.reshape(groups * hidden, own_cols)
-
-    shared_gate_grad = columns(of_shared[:, :hidden]).T
-    shared_up_grad = columns(of_shared[:, hidden : 2 * hidden]).T
-    shared_down_grad = columns(of_shared[:, 2 * hidden :])
-    router_grad = small_sums[:groups].T
+    (
+        layer_out,
+        q_grad,
+        kvb_grad,
+        own_o_grad,
+        shared_gate_grad,
+        shared_up_grad,
+        shared_down_grad,
+        kva_turn,
+        small_sums,
+    ) = finish(
+        (heads, at_kv, at_o, lat_rows, hidden, share),
+        owned_heads,
+        owned_early,
+        owned_share,
+        owned_small,
+        hidden_state,
+        out_sum,
+    )
+    kva_grad, router_grad = kva_turn.T, small_sums[:groups].T
     return (
         layer_out,
         x_grad,

time: 536 us -> 499 us (0.931)
  matrix products: 26 us -> 6.21 us
  other arithmetic: 23.3 us -> 16.4 us
  Pallas kernels: 457 us -> 451 us
    pallas_call x6, Pallas kernels: 457 us -> 433 us  [exchange(): pl.pallas_call(functools.partial(chip_kernel, ops), out_shape=[shape for...]
    dot_general x6 -> x3, matrix products: 23.5 us -> 4.38 us  [fsum(): return jnp.einsum(spec, left, right, preferred_element_type=jnp.float32)]
    pallas_call x0 -> x2, Pallas kernels: none -> 17.9 us  [the longest x1 15.3 us: expert_weight_grads(): pl.pallas_call(grads_kernel, grid=(width // tile,), out_shape=[jax.ShapeD...]
    unnamed x65 -> x64, local copies, waits for them, and re-layouts: 8.51 us -> 13.3 us
where the time goes in v5:
time: 499 us; the launch traced here: 498 us
  Pallas kernels  451 us (90%)
  local copies, waits for them, and re-layouts  23 us (5%)
  other arithmetic  16.4 us (3%)
  matrix products  6.21 us (1%)
    pallas_call x6, Pallas kernels, exchange(): pl.pallas_call(functools.partial(chip_kernel, ops), out_shape=[shape for...  433 us
    pallas_call x1, Pallas kernels, expert_weight_grads(): pl.pallas_call(grads_kernel, grid=(width // tile,), out_shape=[jax.ShapeD...  15.3 us
    unnamed x64, local copies, waits for them, and re-layouts  13.3 us

profile of v5, /device:TPU:0, one launch (start us, length us, event | category | flops | bytes accessed | tf_op | source)
XLA Modules:
  0.0 497.7 jit_solution(3652186128992450063)
XLA Ops:
  1.8 1.2 copy.84
  4.1 1.4 tile.4
  7.1 62.8 %shard_map.288 = (bf16[16,32,128]{2,1,0:T(8,128)(2,1)}, bf16[16,128,576]{2,1,0:T(8,128)(2,1)}, bf16[16,384,128]{2,1,0:T(8,128)(2,1)}, bf16[8,128,2048]{2,1,0:T(8,128)(2,1)}) custom-call(bf16[16,32,128]{2,1,0:T(8,128)(2,1)} %broadcast_in_dim.21.refs_0_, bf16[128,576]{1,0:T(8,128)(2,1)} %copy.86.refs_1_, bf16[16,384,128]{2,1,0:T(8,128)(2,1)} %bitcast.133, ...), custom_call_target="tpu_custom_call" | custom-call | bytes 11157504 | tf_op jit(solution)/shard_map/pallas_call | solution.py:915
  73.0 58.3 %shard_map.289 = (f32[128,2048]{1,0:T(8,128)}, bf16[8,128,192]{2,1,0:T(8,128)(2,1)}, bf16[8,128,192]{2,1,0:T(8,128)(2,1)}, bf16[8,128,128]{2,1,0:T(8,128)(2,1)},...) custom-call(bf16[8,128,2048]{2,1,0:T(8,128)(2,1)} %get-tuple-element, ...), custom_call_target="tpu_custom_call" | custom-call | bytes 17958912 | tf_op jit(solution)/shard_map/pallas_call | solution.py:915
  131.3 1.5 multiply_reduce_fusion.5
  134.6 1.3 slice_bitcast_fusion.2
  139.3 108.3 %shard_map.290 = (bf16[16,128,2048]{2,1,0:T(8,128)(2,1)}, bf16[16,128,2048]{2,1,0:T(8,128)(2,1)}, f32[16,128,128]{2,1,0:T(8,128)}, bf16[16,128,2176]{2,1,0:T(8,1...) custom-call(bf16[128,2048]{1,0:T(8,128)(2,1)} %copy-done.9, ...), custom_call_target="tpu_custom_call" | custom-call | bytes 56426496 | tf_op jit(solution)/shard_map/pallas_call | solution.py:915
  247.6 1.4 copy-done.5
  249.0 1.4 copy-done.6
  250.4 1.4 copy-done.7
  251.8 15.3 %shard_map.295 = (f32[704,2048]{1,0:T(8,128)}, f32[704,2048]{1,0:T(8,128)}, f32[704,2048]{1,0:T(8,128)}) custom-call(bf16[1024,704]{1,0:T(8,128)(2,1)S(1)} %bitcast.128, bf16[1024,704]{1,0:T(8,128)(2,1)S(1)} %bitcast.129, bf16[1024,704]{1,0:T(8,128)(2,1)S(1)} %bitcast.130, bf16[1024,2048]{1,0:T(8,128)(2,1)} %bitcast.163, bf16[1024,2048]{1,0:T(8,128)(2,1)} %bitcast.164), custom_call_target="tpu_custom_call" | custom-call | flops 8858370048 | bytes 25690112 | tf_op jit(solution)/shard_map/pallas_call | solution.py:944
  267.2 47.1 %shard_map.291 = f32[128,2176]{1,0:T(8,128)} custom-call(bf16[16,128,2176]{2,1,0:T(8,128)(2,1)} %get-tuple-element.70.refs_0_), custom_call_target="tpu_custom_call" | custom-call | bytes 10027008 | tf_op jit(solution)/shard_map/pallas_call | solution.py:915
  315.4 1.8 multiply_reduce_fusion.1
  318.8 1.3 copy.124
  320.2 74.5 %shard_map.292 = (bf16[8,128,2048]{2,1,0:T(8,128)(2,1)}, f32[128,2688]{1,0:T(8,128)}, bf16[8,128,192]{2,1,0:T(8,128)(2,1)}, bf16[8,128,256]{2,1,0:T(8,128)(2,1)}, bf16[16,264,128]{2,1,0:T(8,128)(2,1)}) custom-call(bf16[128,2048]{1,0:T(8,128)(2,1)} %get-tuple-element.116.refs_0_, bf16[8,128,192]{2,1,0:T(8,128)(2,1)} %get-tuple-element.71.refs_1_, ...), custom_call_target="tpu_custom_call" | custom-call | bytes 12386304 | tf_op jit(solution)/shard_map/pallas_call | solution.py:915
  395.9 1.3 multiply_reduce_fusion.6
  398.4 1.2 subtract_convert_fusion
  399.8 2.9 multiply_reduce_fusion
  402.7 1.3 multiply_add_fusion
  404.0 1.2 convolution_bitcast_fusion
  407.0 81.9 %shard_map.293 = (bf16[8,128,576]{2,1,0:T(8,128)(2,1)}, f32[128,2048]{1,0:T(8,128)}, bf16[16,384,128]{2,1,0:T(8,128)(2,1)}, f32[16,24,128]{2,1,0:T(8,128)}, bf16[16,72,128]{2,1,0:T(8,128)(2,1)}) custom-call(bf16[128,576]{1,0:T(8,128)(2,1)} %copy-done.14, bf16[16,160,128]{2,1,0:T(8,128)(2,1)} %pad_maximum_fusion.3.refs_1_, ...), custom_call_target="tpu_custom_call" | custom-call | bytes 20496384 | tf_op jit(solution)/shard_map/pallas_call | solution.py:915
  489.0 1.4 copy-done
  490.4 1.2 copy-done.2
  493.5 2.6 shard_map.294
  (110 shorter events, 22.2 us)
Async XLA Ops:
  0.6 3.4 copy-start.21
  4.1 1.5 copy-start.22
  4.1 2.3 copy-start.24
  4.1 2.3 copy-start.26
  4.1 2.3 copy-start.27
  4.1 2.3 copy-start.28
  6.4 65.0 %copy-start.17 = (bf16[128,1408]{1,0:T(8,128)(2,1)S(1)}, bf16[128,1408]{1,0:T(8,128)(2,1)}, u32[]{:S(2)}) copy-start(bf16[128,1408]{1,0:T(8,128)(2,1)} %param.26) | copy-start | bytes 1081348
  7.1 64.5 %copy-start.18 = (bf16[128,1408]{1,0:T(8,128)(2,1)S(1)}, bf16[128,1408]{1,0:T(8,128)(2,1)}, u32[]{:S(2)}) copy-start(bf16[128,1408]{1,0:T(8,128)(2,1)} %param.27) | copy-start | bytes 1081348
  7.1 64.8 %copy-start.19 = (bf16[1408,128]{1,0:T(8,128)(2,1)S(1)}, bf16[1408,128]{1,0:T(8,128)(2,1)}, u32[]{:S(2)}) copy-start(bf16[1408,128]{1,0:T(8,128)(2,1)} %param.28) | copy-start | bytes 1081348
  73.0 58.4 %copy-start.8 = (f32[128,2048]{1,0:T(8,128)S(1)}, f32[128,2048]{1,0:T(8,128)}, u32[]{:S(2)}) copy-start(f32[128,2048]{1,0:T(8,128)} %refs_3_.1) | copy-start | bytes 3145732
  131.3 1.6 copy-start.23
  133.1 2.8 copy-start.9
  136.9 1.5 copy-start.11
  247.6 1.4 copy-start.5
  249.0 1.4 copy-start.6
  250.4 1.4 copy-start.7
  314.2 3.0 copy-start.12
  395.9 3.9 copy-start.13
  399.7 2.9 copy-start.14
  402.7 1.3 copy-start.10
  404.0 2.1 copy-start.16
  404.0 2.1 copy-start.20
  407.0 81.9 %copy-start.1 = (bf16[16,264,128]{2,1,0:T(8,128)(2,1)S(1)}, bf16[16,264,128]{2,1,0:T(8,128)(2,1)}, u32[]{:S(2)}) copy-start(bf16[16,264,128]{2,1,0:T(8,128)(2,1)} %get-tuple-element.89.shared_in) | copy-start | bytes 3244036
  488.9 1.4 copy-start
  (5 other events, 5.2 us)

commit v6 on v5

--- a/solution.py
+++ b/solution.py
@@ -392,7 +392,7 @@
 
 class Reduce:
     def __init__(
-        self, operands, produce, slots, block, width, scratch=(), prepare=None, extra=(), prelude=None, delay=0
+        self, operands, produce, slots, block, width, scratch=(), prepare=None, extra=(), prelude=None, delay=0, maker=None
     ):
         planes, rows, kind = slots // 4, block // 2, jnp.bfloat16
         self.planes, self.reach = planes, planes
@@ -400,7 +400,8 @@
         self.outs = [(jax.ShapeDtypeStruct((block, width), jnp.float32), pltpu.VMEM)]
         self.outs += [(shape, pltpu.VMEM) for shape in extra]
         self.own_scratch, self.produce, self.prepare = len(scratch), produce, prepare
-        self.prelude, self.delay, self.lazy = prelude, delay, prelude is not None
+        self.prelude, self.delay, self.maker = prelude, delay, maker
+        self.lazy = prelude is not None
         by_level = DMA((planes,))
         self.scratch = (
             list(scratch)
@@ -419,7 +420,7 @@
         self.place, self.out = place, outs[0]
         self.refs = list(ins) + list(outs[1:]) + list(scratch[: self.own_scratch])
         scratch = scratch[self.own_scratch :]
-        self.part = scratch[0] if self.produce else ins[0]
+        self.part = scratch[0] if self.produce else self.maker.part
         self.mine = scratch[1]
         self.from_a, self.from_b, self.from_x, self.from_y = scratch[2:6]
         self.from_up, self.from_down = scratch[6:8]
@@ -561,7 +562,7 @@
     def begin(self):
         if self.prepare is not None:
             self.prepare(self.refs)
-        if self.prelude is None:
+        if self.prelude is None and self.maker is None:
             self.make(0)
 
     def advance(self, i):
@@ -576,6 +577,8 @@
             count, call = self.prelude(self.refs)
             parts = [(self.delay, count, call), (self.delay + count, 1, self.make)]
             start = self.delay + count + 1
+        if self.maker is not None:
+            parts, start = [(self.delay, 1, self.make)], self.delay + 1
         return parts + [(start, self.planes + 2, self.advance)]
 
     def hand(self, whose):
@@ -615,7 +618,6 @@
 
         self.ins = [(a, pl.ANY) for a in weights] + [(shared_w, pltpu.VMEM)]
         self.outs = [
-            (shape((slots, seq, width + LANES)), pl.ANY),
             (shape(rows + (width,)), pl.ANY),
             (shape(rows + (seq,)), pltpu.VMEM),
             (shape(turn), pltpu.VMEM),
@@ -623,11 +625,14 @@
             (shape(rows + (width,)), pl.ANY),
             (shape(rows + (width,)), pl.ANY),
         ] + [(shape(rows + (hidden,)), pl.ANY)] * 3
-        staged = [self.outs[k][0] for k in (0, 1, 7, 8, 9)]
-        self.scratch = [pltpu.VMEM(x.shape, bf16) for x in staged]
+        staged = [self.outs[k][0] for k in (0, 6, 7, 8)]
+        self.scratch = [pltpu.VMEM((slots, seq, width + LANES), bf16)]
+        self.scratch += [pltpu.VMEM(x.shape, bf16) for x in staged]
         self.scratch += [DMA((len(staged), gather.planes))]
         self.scratch += (
-            [pltpu.VMEM(w.shape, bf16) for w in weights]
+            [pltpu.VMEM((4, seq, width), bf16)] * 2
+            + [pltpu.VMEM((4, seq, LANES), jnp.float32), DMA((3,))]
+            + [pltpu.VMEM(w.shape, bf16) for w in weights]
             + [pltpu.VMEM((4 * capacity, width), bf16)] * 3
             + [
                 pltpu.VMEM((4 * capacity, LANES), jnp.float32),
@@ -642,11 +647,13 @@
     def bind(self, place, ins, outs, scratch):
         self.place = place
         self.hbm_weights, self.shared_w = ins[:3], ins[3]
-        self.tokens, self.out_rows, self.marked = self.gather.results
-        self.picks, self.act_turn, self.shared_grads, self.rows_hbm, self.cot_hbm = outs[2:7]
-        self.staged, self.leave_sem, scratch = scratch[:5], scratch[5], scratch[6:]
-        self.part, self.out_block, self.act, self.gate_delta, self.up_delta = self.staged
-        self.final = list(outs[:2]) + list(outs[7:])
+        self.picks, self.act_turn, self.shared_grads, self.rows_hbm, self.cot_hbm = outs[1:6]
+        self.part, self.staged, self.leave_sem = scratch[0], scratch[1:5], scratch[5]
+        scratch = scratch[6:]
+        self.out_block, self.act, self.gate_delta, self.up_delta = self.staged
+        self.final = [outs[0]] + list(outs[6:])
+        self.tokens, self.out_rows, self.marked, self.plane_sem = scratch[:4]
+        scratch = scratch[4:]
         self.gate, self.up, self.down = scratch[:3]
         self.rows, self.cot, self.grads = scratch[3:6]
         self.weight, self.held, self.left, self.total, self.load_sem, self.save_sem = scratch[6:]
@@ -688,7 +695,7 @@
 
         for j in range(4):
             slot, at = lev * 4 + j, slice(j * cap, (j + 1) * cap)
-            turned = self.marked[slot].T
+            turned = self.marked[j].T
             here = jnp.sum(jnp.where(below == self.place.chip, turned, 0.0), axis=0, keepdims=True)
             routed = jnp.where(here >= 0.0, 1.0, 0.0)
             order = fdot(jnp.broadcast_to(routed, (8, seq)).astype(jnp.bfloat16), upto)[:1] - 1.0
@@ -702,10 +709,10 @@
 
         @pl.loop(0, self.width // 512, unroll=True)
         def _(k):
-            cols, four = part_rows(k * 512, 512), pl.ds(lev * 4, 4)
-            own = fdot(chosen, self.tokens[four, :, cols].reshape(4 * seq, 512))
+            cols = part_rows(k * 512, 512)
+            own = fdot(chosen, self.tokens[:, :, cols].reshape(4 * seq, 512))
             self.rows[:, cols] = own.astype(jnp.bfloat16)
-            grad = fdot(chosen, self.out_rows[four, :, cols].reshape(4 * seq, 512))
+            grad = fdot(chosen, self.out_rows[:, :, cols].reshape(4 * seq, 512))
             self.grads[:, cols] = grad.astype(jnp.bfloat16)
             self.cot[:, cols] = (weight * grad).astype(jnp.bfloat16)
 
@@ -729,8 +736,8 @@
 
     def shared_units(self, lev):
         seq4, room = 4 * self.seq, self.room
-        tokens = self.tokens[pl.ds(lev * 4, 4)].reshape(seq4, self.width)
-        grads = self.out_rows[pl.ds(lev * 4, 4)].reshape(seq4, self.width)
+        tokens = self.tokens[...].reshape(seq4, self.width)
+        grads = self.out_rows[...].reshape(seq4, self.width)
         both = dot_nt(self.shared_w[:2].reshape(2 * room, self.width), tokens)
         gate, up = both[:room], both[room:]
         grad = dot_nt(self.shared_w[2], grads)
@@ -744,11 +751,11 @@
 
         @pl.loop(0, self.width // 512, unroll=True)
         def _(k):
-            cols, four = part_rows(k * 512, 512), pl.ds(lev * 4, 4)
-            some = self.tokens[four, :, cols].reshape(seq4, 512)
+            cols = part_rows(k * 512, 512)
+            some = self.tokens[:, :, cols].reshape(seq4, 512)
             self.total[0, :, cols] += fdot(gate_delta, some)
             self.total[1, :, cols] += fdot(up_delta, some)
-            some = self.out_rows[four, :, cols].reshape(seq4, 512)
+            some = self.out_rows[:, :, cols].reshape(seq4, 512)
             self.total[2, :, cols] += fdot(act, some)
 
     def outward(self, lev):
@@ -803,6 +810,15 @@
                 load.wait()
 
         self.gather.receive(t)
+        held = [self.tokens, self.out_rows, self.marked]
+        copies = [
+            pltpu.make_async_copy(src.at[pl.ds(lev * 4, 4)], dst, self.plane_sem.at[k])
+            for k, (src, dst) in enumerate(zip(self.gather.results, held))
+        ]
+        for copy in copies:
+            copy.start()
+        for copy in copies:
+            copy.wait()
         self.choose(lev, t)
         self.hidden_units(lev)
         self.shared_units(lev)
@@ -1496,7 +1512,7 @@
         [
             small_swap,
             Gather([kva_weight], all_planes),
-            Swap(jnp.tile(head_parts, (copies, 1, 1))),
+            Swap(jnp.tile(head_parts, (copies, 1, 1)), pace=4),
             NormGather(layer_in, small_swap, groups, planes),
         ],
         1,
@@ -1606,7 +1622,7 @@
                 ],
                 prelude=attend_forward,
             ),
-            Swap(shared_parts, pace=3),
+            Swap(shared_parts, pace=groups),
         ],
         2,
     )
@@ -1630,17 +1646,26 @@
     def stacked(blocks):
         return jnp.pad(blocks, [(0, room - hidden), (0, 0)])
 
-    token_gather = Gather([normed2, out_rows, marked], all_planes, True)
+    token_gather = Gather([normed2, out_rows, marked], all_planes)
     experts_op = Experts(
         token_gather,
         [expert_gate[0].T, expert_up[0].T, expert_down[0]],
         jnp.stack([stacked(gate_sht), stacked(up_sht), stacked(down_sh)]),
         capacity,
     )
-    _, expert_results = exchange([token_gather, experts_op], 3)
-    grad_parts, out_block, picks, shared_act, shared_sums = expert_results[:5]
+    grad_reduce = Reduce(
+        [],
+        None,
+        groups,
+        seq_len,
+        width + marked.shape[1],
+        delay=all_planes + 2,
+        maker=experts_op,
+    )
+    _, expert_results, (summed,) = exchange([token_gather, experts_op, grad_reduce], 3)
+    out_block, picks, shared_act, shared_sums = expert_results[:4]
     rows_in, cot_in, expert_act, gate_delta, up_delta = (
-        x.reshape(groups * capacity, -1) for x in expert_results[5:]
+        x.reshape(groups * capacity, -1) for x in expert_results[4:]
     )
     gate_grad_turn, up_grad_turn, down_grad = expert_weight_grads(
         expert_act, gate_delta, up_delta, rows_in, cot_in
@@ -1668,9 +1693,6 @@
     def hold_shared(refs):
         refs[-1][capacity:] = refs[2][...]
 
-    ((summed,),) = exchange(
-        [Reduce([grad_parts], None, groups, seq_len, width + marked.shape[1])], 4
-    )
     normed2_sum = summed[:, :width]
     prob_grad = summed[:, width : width + groups]
     logit_delta = (
@@ -1756,7 +1778,7 @@
                 prelude=attend_backward,
                 delay=2,
             ),
-            Swap(shared_grads),
+            Swap(shared_grads, pace=4),
         ],
         5,
     )
@@ -1837,7 +1859,7 @@
         (groups, at_gate, own_cols),
         make_head_grads,
         None,
-        5,
+        groups,
     )
 
     def make_latent_grads(op):
@@ -1872,7 +1894,7 @@
                 hold_shared,
             ),
             head_swap,
-            Swap(small_grads, pace=5),
+            Swap(small_grads, pace=groups),
             MadeSwap(
                 [],
                 (groups, share, own_cols),

time: 499 us -> 487 us (0.976)
  Pallas kernels: 451 us -> 439 us
    pallas_call x6 -> x5, Pallas kernels: 433 us -> 421 us  [exchange(): pl.pallas_call(functools.partial(chip_kernel, ops), out_shape=[shape for...]
where the time goes in v6:
time: 487 us; the launch traced here: 486 us
  Pallas kernels  439 us (90%)
  local copies, waits for them, and re-layouts  22.9 us (5%)
  other arithmetic  16.4 us (3%)
  matrix products  6.21 us (1%)
    pallas_call x5, Pallas kernels, exchange(): pl.pallas_call(functools.partial(chip_kernel, ops), out_shape=[shape for...  421 us
    pallas_call x1, Pallas kernels, expert_weight_grads(): pl.pallas_call(grads_kernel, grid=(width // tile,), out_shape=[jax.ShapeD...  15.4 us
    unnamed x64, local copies, waits for them, and re-layouts  13.2 us

profile of v6, /device:TPU:0, one launch (start us, length us, event | category | flops | bytes accessed | tf_op | source)
XLA Modules:
  0.0 485.7 jit_solution(12666338652933518469)
XLA Ops:
  1.8 1.2 copy.84
  4.1 1.4 tile.4
  7.1 61.9 %shard_map.288 = (bf16[16,32,128]{2,1,0:T(8,128)(2,1)}, bf16[16,128,576]{2,1,0:T(8,128)(2,1)}, bf16[16,384,128]{2,1,0:T(8,128)(2,1)}, bf16[8,128,2048]{2,1,0:T(8,128)(2,1)}) custom-call(bf16[16,32,128]{2,1,0:T(8,128)(2,1)} %broadcast_in_dim.21.refs_0_, bf16[128,576]{1,0:T(8,128)(2,1)} %copy.86.refs_1_, bf16[16,384,128]{2,1,0:T(8,128)(2,1)} %bitcast.133, ...), custom_call_target="tpu_custom_call" | custom-call | bytes 11157504 | tf_op jit(solution)/shard_map/pallas_call | solution.py:931
  72.1 49.1 %shard_map.289 = (f32[128,2048]{1,0:T(8,128)}, bf16[8,128,192]{2,1,0:T(8,128)(2,1)}, bf16[8,128,192]{2,1,0:T(8,128)(2,1)}, bf16[8,128,128]{2,1,0:T(8,128)(2,1)},...) custom-call(bf16[8,128,2048]{2,1,0:T(8,128)(2,1)} %get-tuple-element, ...), custom_call_target="tpu_custom_call" | custom-call | bytes 17958912 | tf_op jit(solution)/shard_map/pallas_call | solution.py:931
  121.2 1.5 multiply_reduce_fusion.5
  124.5 1.3 slice_bitcast_fusion.2
  129.3 152.1 %shard_map.290 = (bf16[16,128,2048]{2,1,0:T(8,128)(2,1)}, bf16[16,128,2048]{2,1,0:T(8,128)(2,1)}, f32[16,128,128]{2,1,0:T(8,128)}, bf16[16,64,2048]{2,1,0:T(8,12...) custom-call(bf16[128,2048]{1,0:T(8,128)(2,1)} %copy-done.9, ...), custom_call_target="tpu_custom_call" | custom-call | bytes 48627712 | tf_op jit(solution)/shard_map/pallas_call | solution.py:931
  281.4 1.4 copy-done.5
  282.8 1.4 copy-done.6
  284.2 1.4 copy-done.7
  285.6 15.4 %shard_map.294 = (f32[704,2048]{1,0:T(8,128)}, f32[704,2048]{1,0:T(8,128)}, f32[704,2048]{1,0:T(8,128)}) custom-call(bf16[1024,704]{1,0:T(8,128)(2,1)S(1)} %bitcast.128, bf16[1024,704]{1,0:T(8,128)(2,1)S(1)} %bitcast.129, bf16[1024,704]{1,0:T(8,128)(2,1)S(1)} %bitcast.130, bf16[1024,2048]{1,0:T(8,128)(2,1)} %bitcast.163, bf16[1024,2048]{1,0:T(8,128)(2,1)} %bitcast.164), custom_call_target="tpu_custom_call" | custom-call | flops 8858370048 | bytes 25690112 | tf_op jit(solution)/shard_map/pallas_call | solution.py:960
  301.4 1.3 copy.124
  303.8 1.8 multiply_reduce_fusion.1
  306.8 75.5 %shard_map.291 = (bf16[8,128,2048]{2,1,0:T(8,128)(2,1)}, f32[128,2688]{1,0:T(8,128)}, bf16[8,128,192]{2,1,0:T(8,128)(2,1)}, bf16[8,128,256]{2,1,0:T(8,128)(2,1)}, bf16[16,264,128]{2,1,0:T(8,128)(2,1)}) custom-call(bf16[128,2048]{1,0:T(8,128)(2,1)} %get-tuple-element.116.refs_0_, bf16[8,128,192]{2,1,0:T(8,128)(2,1)} %get-tuple-element.71.refs_1_, ...), custom_call_target="tpu_custom_call" | custom-call | bytes 12386304 | tf_op jit(solution)/shard_map/pallas_call | solution.py:931
  383.4 1.3 multiply_reduce_fusion.6
  384.8 1.2 multiply_convert_fusion.1
  385.9 1.2 subtract_convert_fusion
  387.3 2.9 multiply_reduce_fusion
  390.3 1.3 multiply_add_fusion
  391.5 1.2 convolution_bitcast_fusion
  394.6 82.4 %shard_map.292 = (bf16[8,128,576]{2,1,0:T(8,128)(2,1)}, f32[128,2048]{1,0:T(8,128)}, bf16[16,384,128]{2,1,0:T(8,128)(2,1)}, f32[16,24,128]{2,1,0:T(8,128)}, bf16[16,72,128]{2,1,0:T(8,128)(2,1)}) custom-call(bf16[128,576]{1,0:T(8,128)(2,1)} %copy-done.14, bf16[16,160,128]{2,1,0:T(8,128)(2,1)} %pad_maximum_fusion.3.refs_1_, ...), custom_call_target="tpu_custom_call" | custom-call | bytes 20496384 | tf_op jit(solution)/shard_map/pallas_call | solution.py:931
  477.0 1.4 copy-done
  478.4 1.2 copy-done.2
  481.6 2.6 shard_map.293
  (109 shorter events, 20.9 us)
Async XLA Ops:
  0.6 3.4 copy-start.21
  4.1 1.5 copy-start.22
  4.1 2.3 copy-start.24
  4.1 2.3 copy-start.26
  4.1 2.3 copy-start.27
  4.1 2.3 copy-start.28
  6.4 64.1 %copy-start.17 = (bf16[128,1408]{1,0:T(8,128)(2,1)S(1)}, bf16[128,1408]{1,0:T(8,128)(2,1)}, u32[]{:S(2)}) copy-start(bf16[128,1408]{1,0:T(8,128)(2,1)} %param.26) | copy-start | bytes 1081348
  7.1 63.6 %copy-start.18 = (bf16[128,1408]{1,0:T(8,128)(2,1)S(1)}, bf16[128,1408]{1,0:T(8,128)(2,1)}, u32[]{:S(2)}) copy-start(bf16[128,1408]{1,0:T(8,128)(2,1)} %param.27) | copy-start | bytes 1081348
  7.1 63.9 %copy-start.19 = (bf16[1408,128]{1,0:T(8,128)(2,1)S(1)}, bf16[1408,128]{1,0:T(8,128)(2,1)}, u32[]{:S(2)}) copy-start(bf16[1408,128]{1,0:T(8,128)(2,1)} %param.28) | copy-start | bytes 1081348
  72.1 49.2 %copy-start.8 = (f32[128,2048]{1,0:T(8,128)S(1)}, f32[128,2048]{1,0:T(8,128)}, u32[]{:S(2)}) copy-start(f32[128,2048]{1,0:T(8,128)} %refs_3_.1) | copy-start | bytes 3145732
  121.2 1.6 copy-start.23
  123.0 2.8 copy-start.9
  126.9 1.5 copy-start.11
  281.3 1.4 copy-start.5
  282.8 1.4 copy-start.6
  284.2 1.4 copy-start.7
  285.6 15.4 %copy-start.15 = (bf16[3,96,2048]{2,1,0:T(8,128)(2,1)S(1)}, bf16[3,96,2048]{2,1,0:T(8,128)(2,1)}, u32[]{:S(2)}) copy-start(bf16[3,96,2048]{2,1,0:T(8,128)(2,1)} %get-tuple-element.78) | copy-start | bytes 3538948
  302.7 3.0 copy-start.12
  383.4 3.9 copy-start.13
  387.3 3.0 copy-start.14
  391.5 2.1 copy-start.16
  391.5 2.1 copy-start.20
  394.6 82.4 %copy-start.1 = (bf16[16,264,128]{2,1,0:T(8,128)(2,1)S(1)}, bf16[16,264,128]{2,1,0:T(8,128)(2,1)}, u32[]{:S(2)}) copy-start(bf16[16,264,128]{2,1,0:T(8,128)(2,1)} %get-tuple-element.89.shared_in) | copy-start | bytes 3244036
  477.0 1.4 copy-start
  (5 other events, 5.2 us)

commit v7 on v6

--- a/solution.py
+++ b/solution.py
@@ -1776,7 +1776,7 @@
                 [pltpu.VMEM((heads, seq_len, LANES), bf16)],
                 extra=[shaped(DQK, bf16), shaped(DN + DV, bf16)],
                 prelude=attend_backward,
-                delay=2,
+                delay=1,
             ),
             Swap(shared_grads, pace=4),
         ],

time: 487 us -> 486 us (level)
  no operation moved by 1% of the time
where the time goes in v7:
time: 486 us; the launch traced here: 485 us
  Pallas kernels  439 us (90%)
  local copies, waits for them, and re-layouts  22.9 us (5%)
  other arithmetic  16.4 us (3%)
  matrix products  6.21 us (1%)
    pallas_call x5, Pallas kernels, exchange(): pl.pallas_call(functools.partial(chip_kernel, ops), out_shape=[shape for...  421 us
    pallas_call x1, Pallas kernels, expert_weight_grads(): pl.pallas_call(grads_kernel, grid=(width // tile,), out_shape=[jax.ShapeD...  15.4 us
    unnamed x64, local copies, waits for them, and re-layouts  13.2 us

profile of v7, /device:TPU:0, one launch (start us, length us, event | category | flops | bytes accessed | tf_op | source)
XLA Modules:
  0.0 485.2 jit_solution(14235469296132037733)
XLA Ops:
  1.8 1.2 copy.84
  4.1 1.4 tile.4
  7.1 61.9 %shard_map.288 = (bf16[16,32,128]{2,1,0:T(8,128)(2,1)}, bf16[16,128,576]{2,1,0:T(8,128)(2,1)}, bf16[16,384,128]{2,1,0:T(8,128)(2,1)}, bf16[8,128,2048]{2,1,0:T(8,128)(2,1)}) custom-call(bf16[16,32,128]{2,1,0:T(8,128)(2,1)} %broadcast_in_dim.21.refs_0_, bf16[128,576]{1,0:T(8,128)(2,1)} %copy.86.refs_1_, bf16[16,384,128]{2,1,0:T(8,128)(2,1)} %bitcast.133, ...), custom_call_target="tpu_custom_call" | custom-call | bytes 11157504 | tf_op jit(solution)/shard_map/pallas_call | solution.py:931
  72.1 49.1 %shard_map.289 = (f32[128,2048]{1,0:T(8,128)}, bf16[8,128,192]{2,1,0:T(8,128)(2,1)}, bf16[8,128,192]{2,1,0:T(8,128)(2,1)}, bf16[8,128,128]{2,1,0:T(8,128)(2,1)},...) custom-call(bf16[8,128,2048]{2,1,0:T(8,128)(2,1)} %get-tuple-element, ...), custom_call_target="tpu_custom_call" | custom-call | bytes 17958912 | tf_op jit(solution)/shard_map/pallas_call | solution.py:931
  121.2 1.5 multiply_reduce_fusion.5
  124.5 1.3 slice_bitcast_fusion.2
  129.3 152.1 %shard_map.290 = (bf16[16,128,2048]{2,1,0:T(8,128)(2,1)}, bf16[16,128,2048]{2,1,0:T(8,128)(2,1)}, f32[16,128,128]{2,1,0:T(8,128)}, bf16[16,64,2048]{2,1,0:T(8,12...) custom-call(bf16[128,2048]{1,0:T(8,128)(2,1)} %copy-done.9, ...), custom_call_target="tpu_custom_call" | custom-call | bytes 48627712 | tf_op jit(solution)/shard_map/pallas_call | solution.py:931
  281.4 1.4 copy-done.5
  282.8 1.4 copy-done.6
  284.2 1.4 copy-done.7
  285.6 15.4 %shard_map.294 = (f32[704,2048]{1,0:T(8,128)}, f32[704,2048]{1,0:T(8,128)}, f32[704,2048]{1,0:T(8,128)}) custom-call(bf16[1024,704]{1,0:T(8,128)(2,1)S(1)} %bitcast.128, bf16[1024,704]{1,0:T(8,128)(2,1)S(1)} %bitcast.129, bf16[1024,704]{1,0:T(8,128)(2,1)S(1)} %bitcast.130, bf16[1024,2048]{1,0:T(8,128)(2,1)} %bitcast.163, bf16[1024,2048]{1,0:T(8,128)(2,1)} %bitcast.164), custom_call_target="tpu_custom_call" | custom-call | flops 8858370048 | bytes 25690112 | tf_op jit(solution)/shard_map/pallas_call | solution.py:960
  301.4 1.3 copy.124
  303.8 1.8 multiply_reduce_fusion.1
  306.8 74.2 %shard_map.291 = (bf16[8,128,2048]{2,1,0:T(8,128)(2,1)}, f32[128,2688]{1,0:T(8,128)}, bf16[8,128,192]{2,1,0:T(8,128)(2,1)}, bf16[8,128,256]{2,1,0:T(8,128)(2,1)}, bf16[16,264,128]{2,1,0:T(8,128)(2,1)}) custom-call(bf16[128,2048]{1,0:T(8,128)(2,1)} %get-tuple-element.116.refs_0_, bf16[8,128,192]{2,1,0:T(8,128)(2,1)} %get-tuple-element.71.refs_1_, ...), custom_call_target="tpu_custom_call" | custom-call | bytes 12386304 | tf_op jit(solution)/shard_map/pallas_call | solution.py:931
  382.2 1.3 multiply_reduce_fusion.6
  383.5 1.2 multiply_convert_fusion.1
  384.7 1.2 subtract_convert_fusion
  386.1 2.9 multiply_reduce_fusion
  389.0 1.3 multiply_add_fusion
  390.3 1.2 convolution_bitcast_fusion
  393.3 83.2 %shard_map.292 = (bf16[8,128,576]{2,1,0:T(8,128)(2,1)}, f32[128,2048]{1,0:T(8,128)}, bf16[16,384,128]{2,1,0:T(8,128)(2,1)}, f32[16,24,128]{2,1,0:T(8,128)}, bf16[16,72,128]{2,1,0:T(8,128)(2,1)}) custom-call(bf16[128,576]{1,0:T(8,128)(2,1)} %copy-done.14, bf16[16,160,128]{2,1,0:T(8,128)(2,1)} %pad_maximum_fusion.3.refs_1_, ...), custom_call_target="tpu_custom_call" | custom-call | bytes 20496384 | tf_op jit(solution)/shard_map/pallas_call | solution.py:931
  476.5 1.4 copy-done
  477.9 1.2 copy-done.2
  481.0 2.6 shard_map.293
  (109 shorter events, 20.9 us)
Async XLA Ops:
  0.6 3.4 copy-start.21
  4.1 1.5 copy-start.22
  4.1 2.3 copy-start.24
  4.1 2.3 copy-start.26
  4.1 2.3 copy-start.27
  4.1 2.3 copy-start.28
  6.4 64.1 %copy-start.17 = (bf16[128,1408]{1,0:T(8,128)(2,1)S(1)}, bf16[128,1408]{1,0:T(8,128)(2,1)}, u32[]{:S(2)}) copy-start(bf16[128,1408]{1,0:T(8,128)(2,1)} %param.26) | copy-start | bytes 1081348
  7.1 63.6 %copy-start.18 = (bf16[128,1408]{1,0:T(8,128)(2,1)S(1)}, bf16[128,1408]{1,0:T(8,128)(2,1)}, u32[]{:S(2)}) copy-start(bf16[128,1408]{1,0:T(8,128)(2,1)} %param.27) | copy-start | bytes 1081348
  7.1 63.9 %copy-start.19 = (bf16[1408,128]{1,0:T(8,128)(2,1)S(1)}, bf16[1408,128]{1,0:T(8,128)(2,1)}, u32[]{:S(2)}) copy-start(bf16[1408,128]{1,0:T(8,128)(2,1)} %param.28) | copy-start | bytes 1081348
  72.1 49.2 %copy-start.8 = (f32[128,2048]{1,0:T(8,128)S(1)}, f32[128,2048]{1,0:T(8,128)}, u32[]{:S(2)}) copy-start(f32[128,2048]{1,0:T(8,128)} %refs_3_.1) | copy-start | bytes 3145732
  121.2 1.6 copy-start.23
  123.0 2.8 copy-start.9
  126.9 1.5 copy-start.11
  281.3 1.4 copy-start.5
  282.8 1.4 copy-start.6
  284.2 1.4 copy-start.7
  285.6 15.4 %copy-start.15 = (bf16[3,96,2048]{2,1,0:T(8,128)(2,1)S(1)}, bf16[3,96,2048]{2,1,0:T(8,128)(2,1)}, u32[]{:S(2)}) copy-start(bf16[3,96,2048]{2,1,0:T(8,128)(2,1)} %get-tuple-element.78) | copy-start | bytes 3538948
  302.7 3.0 copy-start.12
  382.2 3.9 copy-start.13
  386.0 3.0 copy-start.14
  390.3 2.1 copy-start.16
  390.3 2.1 copy-start.20
  393.3 83.2 %copy-start.1 = (bf16[16,264,128]{2,1,0:T(8,128)(2,1)S(1)}, bf16[16,264,128]{2,1,0:T(8,128)(2,1)}, u32[]{:S(2)}) copy-start(bf16[16,264,128]{2,1,0:T(8,128)(2,1)} %get-tuple-element.89.shared_in) | copy-start | bytes 3244036
  476.5 1.4 copy-start
  (5 other events, 5.2 us)
